TPU v7x, 32 devices: a whole 2x2x4 slice. The times are simulated.
32 devices in a mesh: dp: 8 (over y, x, core), tensor: 4 (over z).
Axes of the slice: x: 2, y: 2, z: 4, core: 2. Of those that a mesh axis runs over, the one named last changes fastest.
Arguments:
- tokens: bfloat16 [2048, 2048], P('dp'), may hold values from -6 to 6
- w_query: bfloat16 [2048, 2048], P('dp', 'tensor'), may hold values from -0.125 to 0.125
- w_key: bfloat16 [2048, 2048], P('dp', 'tensor'), may hold values from -0.125 to 0.125
- w_value: bfloat16 [2048, 2048], P('dp', 'tensor'), may hold values from -0.125 to 0.125
- w_out: bfloat16 [2048, 2048], P('tensor', 'dp'), may hold values from -0.5 to 0.5
- gain_attn: bfloat16 [2048], P('dp'), may hold values from 0.5 to 1.5
- gain_ffn: bfloat16 [2048], P('dp'), may hold values from 0.5 to 1.5
- w_router: bfloat16 [2048, 16], P('dp'), may hold values from -0.25 to 0.25
- shared_gate: bfloat16 [2048, 5632], P('dp', 'tensor'), may hold values from -0.125 to 0.125
- shared_up: bfloat16 [2048, 5632], P('dp', 'tensor'), may hold values from -0.125 to 0.125
- shared_down: bfloat16 [5632, 2048], P('tensor', 'dp'), may hold values from -0.15625 to 0.15625
- shared_switch: bfloat16 [2048], P('dp'), may hold values from -0.125 to 0.125
- expert_gate: bfloat16 [16, 2048, 1408], P('dp', None, 'tensor'), may hold values from -0.125 to 0.125
- expert_up_weight: bfloat16 [16, 2048, 1408], P('dp', None, 'tensor'), may hold values from -0.125 to 0.125
- expert_down: bfloat16 [16, 1408, 2048], P('dp', 'tensor'), may hold values from -1.25 to 1.25
- routes: int32 [2048, 4], P('dp'), may hold values from 0 to 15, all different within a row; in each aligned block of 256 rows (0 to 255, 256 to 511, ...) at most 96 rows name the same one
- segments: int32 [8, 256], P('dp'), may hold values from 0 to 3, never falling along the last dimension, each value on 1 to 128 neighbouring positions
- cotangent: bfloat16 [2048, 2048], P('dp'), may hold values from -6 to 6
Outputs:
- output: bfloat16 [2048, 2048], P('dp')
- grad_input: float32 [2048, 2048], P('dp')
- grad_query: float32 [2048, 2048], P('dp', 'tensor')
- grad_key: float32 [2048, 2048], P('dp', 'tensor')
- grad_value: float32 [2048, 2048], P('dp', 'tensor')
- grad_out_proj: float32 [2048, 2048], P('tensor', 'dp')
- grad_gain_attn: float32 [2048], P('dp')
- grad_gain_ffn: float32 [2048], P('dp')
- grad_router: float32 [2048, 16], P('dp')
- grad_shared_gate: float32 [2048, 5632], P('dp', 'tensor')
- grad_shared_up: float32 [2048, 5632], P('dp', 'tensor')
- grad_shared_down: float32 [5632, 2048], P('tensor', 'dp')
- grad_shared_switch: float32 [2048], P('dp')
- grad_expert_gate: float32 [16, 2048, 1408], P('dp', None, 'tensor')
- grad_expert_up: float32 [16, 2048, 1408], P('dp', None, 'tensor')
- grad_expert_down: float32 [16, 1408, 2048], P('dp', 'tensor')
Inputs may be any that keep to these rules, and one draw needn't show every extreme that they name: `routes`: A token names 4 different experts. Within the tokens of one device (aligned blocks of 256 tokens) no expert is named by more than 96 tokens, and in every draw some expert is named by exactly 96. `segments`: within a packed row segment numbers never fall; each segment holds 1 to 128 positions, and one holds exactly 128.
All inputs are finite; a program needn't handle non-finite values.
Results may differ from a plain program's by a relative error of at most 0.025.
Values may be sent and summed in bfloat16 or wider, within the bound.
A program may use at most 256 MiB of HBM per device.

v0:
```python
import jax
import jax.numpy as jnp
from jax import lax
from jax.sharding import PartitionSpec as P

HEAD_DIM = 128
TOP = 4
SEQ = 256


EPSILON = 1e-06


def dot_rows(left, right):
    return lax.dot_general(
        left, right, (((0,), (0,)), ((), ())), preferred_element_type=jnp.float32
    )


def dot_last(left, right):
    return lax.dot_general(
        left, right, (((1,), (1,)), ((), ())), preferred_element_type=jnp.float32
    )


def forward_rms_norm(values, gain):
    inverse = lax.rsqrt(jnp.mean(values * values, axis=-1, keepdims=True) + EPSILON)
    normed = values * inverse
    return (normed * gain, normed, inverse)


def norm_backward(grad, normed, inverse, gain):
    scaled = grad * gain
    back = inverse * (scaled - normed * jnp.mean(scaled * normed, axis=-1, keepdims=True))
    return (back, jnp.sum(grad * normed, axis=0))


def softmax_last(scores):
    exponent = jnp.exp(scores)
    return exponent / jnp.sum(exponent, axis=-1, keepdims=True)


def rope_tables():
    half_dim = HEAD_DIM // 2
    exponent = jnp.arange(half_dim, dtype=jnp.float32) * (2.0 / HEAD_DIM)
    inverse_freq = jnp.exp(-exponent * jnp.log(jnp.float32(1000000.0)))
    angles = jnp.arange(SEQ, dtype=jnp.float32)[:, None] * inverse_freq[None, :]
    return (jnp.cos(angles), jnp.sin(angles))


def rotate(values, cosine, sine, sign):
    half_dim = values.shape[-1] // 2
    first = values[..., :half_dim]
    second = values[..., half_dim:]
    cos_table = cosine[:, None, :]
    sin_table = sine[:, None, :] * sign
    return jnp.concatenate(
        [first * cos_table - second * sin_table, second * cos_table + first * sin_table], axis=-1
    )


def masked_scores(queries, key_rows, segment_row):
    raw = jnp.einsum(
        "qhd,khd->hqk", queries, key_rows, preferred_element_type=jnp.float32
    ) * HEAD_DIM ** (-0.5)
    spots = jnp.arange(segment_row.shape[0], dtype=jnp.int32)
    allowed = (spots[None, :] <= spots[:, None]) & (segment_row[None, :] == segment_row[:, None])
    return jnp.where(allowed[None], raw, -1e30)


def attend_forward(inputs):
    queries, key_rows, value_rows, segment_row = inputs
    scores = masked_scores(queries, key_rows, segment_row)
    exponent = jnp.exp(scores)
    totals = jnp.sum(exponent, axis=-1, keepdims=True)
    probs = (exponent / totals).astype(jnp.bfloat16)
    context = jnp.einsum(
        "hqk,khd->qhd", probs, value_rows, preferred_element_type=jnp.float32
    ).astype(jnp.bfloat16)
    return (context, jnp.log(totals[..., 0]))


def attend_backward(inputs):
    queries, key_rows, value_rows, segment_row, log_total, grad_context = inputs
    scores = masked_scores(queries, key_rows, segment_row)
    probs = jnp.exp(scores - log_total[..., None])
    probs_low = probs.astype(jnp.bfloat16)
    grad_probs = jnp.einsum(
        "qhd,khd->hqk", grad_context, value_rows, preferred_element_type=jnp.float32
    )
    inner = jnp.sum(probs * grad_probs, axis=-1, keepdims=True)
    grad_scores = (probs * (grad_probs - inner)).astype(jnp.bfloat16)
    grad_queries = jnp.einsum(
        "hqk,khd->qhd", grad_scores, key_rows, preferred_element_type=jnp.float32
    ) * HEAD_DIM ** (-0.5)
    grad_keys = jnp.einsum(
        "hqk,qhd->khd", grad_scores, queries, preferred_element_type=jnp.float32
    ) * HEAD_DIM ** (-0.5)
    grad_values = jnp.einsum(
        "hqk,qhd->khd", probs_low, grad_context, preferred_element_type=jnp.float32
    )
    return (grad_queries, grad_keys, grad_values)


def dispatch(rows_out, places, local_experts, span):
    buffer = (
        jnp.zeros((local_experts * span, rows_out.shape[1]), rows_out.dtype)
        .at[places]
        .set(rows_out)
    )
    buffer = buffer.reshape(local_experts, span, rows_out.shape[1])
    return lax.all_to_all(buffer, "dp", split_axis=1, concat_axis=1, tiled=True)


def shards(
    tokens,
    w_query,
    w_key,
    w_value,
    w_out,
    gain_attn,
    gain_ffn,
    w_router,
    shared_gate,
    shared_up,
    shared_down,
    shared_switch,
    expert_gate,
    expert_up_weight,
    expert_down,
    routes,
    segments,
    cotangent,
):
    data_ranks = lax.axis_size("dp")
    token_count = tokens.shape[0]
    width = tokens.shape[1]
    local_experts = expert_gate.shape[0]
    expert_count = local_experts * data_ranks
    capacity = 3 * token_count * TOP // (2 * expert_count)
    span = data_ranks * capacity
    row_count = token_count // SEQ
    (
        query_full,
        key_full,
        value_full,
        out_full,
        gate_full,
        up_full,
        down_full,
        attn_gain,
        ffn_gain,
        router_full,
        switch_full,
    ) = (
        lax.all_gather(w_query, "dp", axis=0, tiled=True),
        lax.all_gather(w_key, "dp", axis=0, tiled=True),
        lax.all_gather(w_value, "dp", axis=0, tiled=True),
        lax.all_gather(w_out, "dp", axis=1, tiled=True),
        lax.all_gather(shared_gate, "dp", axis=0, tiled=True),
        lax.all_gather(shared_up, "dp", axis=0, tiled=True),
        lax.all_gather(shared_down, "dp", axis=1, tiled=True),
        lax.all_gather(gain_attn, "dp", axis=0, tiled=True),
        lax.all_gather(gain_ffn, "dp", axis=0, tiled=True),
        lax.all_gather(w_router, "dp", axis=0, tiled=True),
        lax.all_gather(shared_switch, "dp", axis=0, tiled=True),
    )
    attn_gain = attn_gain.astype(jnp.float32)
    ffn_gain = ffn_gain.astype(jnp.float32)
    head_count = query_full.shape[1] // HEAD_DIM
    shape_four = (row_count, SEQ, head_count, HEAD_DIM)
    cosine, sine = rope_tables()
    inputs = tokens.astype(jnp.float32)
    attn_pre, attn_normed, attn_inverse = forward_rms_norm(inputs, attn_gain)
    attn_in = attn_pre.astype(jnp.bfloat16)
    queries = rotate(
        jnp.dot(attn_in, query_full, preferred_element_type=jnp.float32).reshape(shape_four),
        cosine,
        sine,
        1.0,
    ).astype(jnp.bfloat16)
    key_rows = rotate(
        jnp.dot(attn_in, key_full, preferred_element_type=jnp.float32).reshape(shape_four),
        cosine,
        sine,
        1.0,
    ).astype(jnp.bfloat16)
    value_rows = (
        jnp.dot(attn_in, value_full, preferred_element_type=jnp.float32)
        .astype(jnp.bfloat16)
        .reshape(shape_four)
    )
    contexts, log_totals = lax.map(attend_forward, (queries, key_rows, value_rows, segments))
    context_flat = contexts.reshape(token_count, head_count * HEAD_DIM)
    attn_out = lax.psum(
        jnp.dot(context_flat, out_full, preferred_element_type=jnp.float32), "tensor"
    )
    middle = inputs + attn_out
    ffn_pre, ffn_normed, ffn_inverse = forward_rms_norm(middle, ffn_gain)
    ffn_in = ffn_pre.astype(jnp.bfloat16)
    router_probs = softmax_last(jnp.dot(ffn_in, router_full, preferred_element_type=jnp.float32))
    hits = routes[:, :, None] == jnp.arange(expert_count, dtype=jnp.int32)[None, None, :]
    route_weight = jnp.sum(jnp.where(hits, router_probs[:, None, :], 0.0), axis=-1)
    flat_routes = routes.reshape(-1)
    onehot = hits.reshape(token_count * TOP, expert_count).astype(jnp.int32)
    ranking = jnp.sum((jnp.cumsum(onehot, axis=0) - 1) * onehot, axis=-1)
    places = flat_routes % local_experts * span + flat_routes // local_experts * capacity + ranking
    owners = jnp.arange(token_count * TOP, dtype=jnp.int32) // TOP
    arrived_rows = dispatch(ffn_in[owners], places, local_experts, span)
    expert_pre_gate = jnp.einsum(
        "jrd,jdf->jrf", arrived_rows, expert_gate, preferred_element_type=jnp.float32
    )
    expert_pre_up = jnp.einsum(
        "jrd,jdf->jrf", arrived_rows, expert_up_weight, preferred_element_type=jnp.float32
    )
    expert_sig = lax.logistic(expert_pre_gate)
    expert_activation = expert_pre_gate * expert_sig
    expert_hidden_state = (expert_activation * expert_pre_up).astype(jnp.bfloat16)
    expert_part = jnp.einsum(
        "jrf,jfd->jrd", expert_hidden_state, expert_down, preferred_element_type=jnp.float32
    ).astype(jnp.bfloat16)
    shared_pre_gate = jnp.dot(ffn_in, gate_full, preferred_element_type=jnp.float32)
    shared_pre_up = jnp.dot(ffn_in, up_full, preferred_element_type=jnp.float32)
    shared_sig = lax.logistic(shared_pre_gate)
    shared_act = shared_pre_gate * shared_sig
    shared_hidden = (shared_act * shared_pre_up).astype(jnp.bfloat16)
    shared_part = jnp.dot(shared_hidden, down_full, preferred_element_type=jnp.float32)
    switch = lax.logistic(jnp.dot(ffn_in, switch_full, preferred_element_type=jnp.float32))[:, None]
    grad_moe = cotangent.astype(jnp.float32)
    returned = lax.all_to_all(expert_part, "dp", split_axis=1, concat_axis=1, tiled=True).reshape(
        local_experts * span, width
    )
    route_rows = returned[places].reshape(token_count, TOP, width)
    routed = route_rows[:, 0, :].astype(jnp.float32) * route_weight[:, 0:1]
    for which in range(1, TOP):
        routed = (
            routed
            + route_rows[:, which, :].astype(jnp.float32) * route_weight[:, which : which + 1]
        )
    moe = lax.psum((routed + switch * shared_part).astype(jnp.bfloat16), "tensor").astype(
        jnp.float32
    )
    output = (middle + moe).astype(jnp.bfloat16)
    route_part = jnp.sum(route_rows.astype(jnp.float32) * grad_moe[:, None, :], axis=-1)
    switch_part = jnp.sum(grad_moe * shared_part, axis=-1)
    grad_rows = (
        (route_weight[:, :, None] * grad_moe[:, None, :])
        .astype(jnp.bfloat16)
        .reshape(token_count * TOP, width)
    )
    grad_received = dispatch(grad_rows, places, local_experts, span)
    hidden_gradient = jnp.einsum(
        "jrd,jfd->jrf", grad_received, expert_down, preferred_element_type=jnp.float32
    )
    grad_expert_down = jnp.einsum(
        "jrf,jrd->jfd", expert_hidden_state, grad_received, preferred_element_type=jnp.float32
    )
    expert_up_gradient = (hidden_gradient * expert_activation).astype(jnp.bfloat16)
    grad_egate = (
        hidden_gradient * expert_pre_up * expert_sig * (1.0 + expert_pre_gate * (1.0 - expert_sig))
    ).astype(jnp.bfloat16)
    grad_expert_gate = jnp.einsum(
        "bzt,bzl->btl", arrived_rows, grad_egate, preferred_element_type=jnp.float32
    )
    grad_expert_up = jnp.einsum(
        "bzt,bzl->btl", arrived_rows, expert_up_gradient, preferred_element_type=jnp.float32
    )
    expert_back = jnp.einsum(
        "mzg,mvg->mzv", grad_egate, expert_gate, preferred_element_type=jnp.float32
    )
    expert_back = expert_back + jnp.einsum(
        "mzg,mvg->mzv", expert_up_gradient, expert_up_weight, preferred_element_type=jnp.float32
    )
    grad_shared_out = (switch * grad_moe).astype(jnp.bfloat16)
    shared_hidden_gradient = dot_last(grad_shared_out, down_full)
    grad_shared_down = dot_rows(shared_hidden, grad_shared_out)
    grad_sup = (shared_hidden_gradient * shared_act).astype(jnp.bfloat16)
    grad_sgate = (
        shared_hidden_gradient
        * shared_pre_up
        * shared_sig
        * (1.0 + shared_pre_gate * (1.0 - shared_sig))
    ).astype(jnp.bfloat16)
    grad_shared_gate = dot_rows(ffn_in, grad_sgate)
    grad_shared_up = dot_rows(ffn_in, grad_sup)
    shared_back = dot_last(grad_sgate, gate_full) + dot_last(grad_sup, up_full)
    back_flat = lax.all_to_all(expert_back, "dp", split_axis=1, concat_axis=1, tiled=True).reshape(
        local_experts * span, width
    )
    routed_back = jnp.sum(back_flat[places].reshape(token_count, TOP, width), axis=1)
    grad_ffn_part, grad_route_weight, grad_switch_total = lax.psum(
        (routed_back + shared_back, route_part, switch_part), "tensor"
    )
    grad_probs = jnp.sum(jnp.where(hits, grad_route_weight[:, :, None], 0.0), axis=1)
    grad_logits = (
        router_probs * (grad_probs - jnp.sum(router_probs * grad_probs, axis=-1, keepdims=True))
    ).astype(jnp.bfloat16)
    grad_router = dot_rows(ffn_in, grad_logits)
    grad_switch_logit = grad_switch_total[:, None] * switch * (1.0 - switch)
    grad_shared_switch = jnp.sum(grad_switch_logit * ffn_in.astype(jnp.float32), axis=0)
    grad_ffn_in = (
        grad_ffn_part
        + dot_last(grad_logits, router_full)
        + grad_switch_logit * switch_full.astype(jnp.float32)[None, :]
    )
    middle_back, grad_gain_ffn = norm_backward(grad_ffn_in, ffn_normed, ffn_inverse, ffn_gain)
    grad_middle = grad_moe + middle_back
    grad_attn_out = grad_middle.astype(jnp.bfloat16)
    grad_out_proj = dot_rows(context_flat, grad_attn_out)
    grad_context = dot_last(grad_attn_out, out_full).astype(jnp.bfloat16).reshape(shape_four)
    grad_queries, grad_keys, grad_values = lax.map(
        attend_backward, (queries, key_rows, value_rows, segments, log_totals, grad_context)
    )
    flat_shape = (token_count, head_count * HEAD_DIM)
    grad_queries = rotate(grad_queries, cosine, sine, -1.0).reshape(flat_shape).astype(jnp.bfloat16)
    grad_keys = rotate(grad_keys, cosine, sine, -1.0).reshape(flat_shape).astype(jnp.bfloat16)
    grad_values = grad_values.reshape(flat_shape).astype(jnp.bfloat16)
    grad_query = dot_rows(attn_in, grad_queries)
    grad_key = dot_rows(attn_in, grad_keys)
    grad_value = dot_rows(attn_in, grad_values)
    attn_back_part = (
        dot_last(grad_queries, query_full)
        + dot_last(grad_keys, key_full)
        + dot_last(grad_values, value_full)
    )
    grad_attn_in = lax.psum(attn_back_part.astype(jnp.bfloat16), "tensor").astype(jnp.float32)
    input_back, grad_gain_attn = norm_backward(grad_attn_in, attn_normed, attn_inverse, attn_gain)
    grad_input = grad_middle + input_back
    (
        grad_query,
        grad_key,
        grad_value,
        grad_out_proj,
        grad_shared_gate,
        grad_shared_up,
        grad_shared_down,
        grad_gain_attn,
        grad_gain_ffn,
        grad_router,
        grad_shared_switch,
    ) = (
        lax.psum_scatter(
            grad_query.astype(jnp.bfloat16), "dp", scatter_dimension=0, tiled=True
        ).astype(jnp.float32),
        lax.psum_scatter(
            grad_key.astype(jnp.bfloat16), "dp", scatter_dimension=0, tiled=True
        ).astype(jnp.float32),
        lax.psum_scatter(
            grad_value.astype(jnp.bfloat16), "dp", scatter_dimension=0, tiled=True
        ).astype(jnp.float32),
        lax.psum_scatter(
            grad_out_proj.astype(jnp.bfloat16), "dp", scatter_dimension=1, tiled=True
        ).astype(jnp.float32),
        lax.psum_scatter(
            grad_shared_gate.astype(jnp.bfloat16), "dp", scatter_dimension=0, tiled=True
        ).astype(jnp.float32),
        lax.psum_scatter(
            grad_shared_up.astype(jnp.bfloat16), "dp", scatter_dimension=0, tiled=True
        ).astype(jnp.float32),
        lax.psum_scatter(
            grad_shared_down.astype(jnp.bfloat16), "dp", scatter_dimension=1, tiled=True
        ).astype(jnp.float32),
        lax.psum_scatter(
            grad_gain_attn.astype(jnp.bfloat16), "dp", scatter_dimension=0, tiled=True
        ).astype(jnp.float32),
        lax.psum_scatter(
            grad_gain_ffn.astype(jnp.bfloat16), "dp", scatter_dimension=0, tiled=True
        ).astype(jnp.float32),
        lax.psum_scatter(
            grad_router.astype(jnp.bfloat16), "dp", scatter_dimension=0, tiled=True
        ).astype(jnp.float32),
        lax.psum_scatter(
            grad_shared_switch.astype(jnp.bfloat16), "dp", scatter_dimension=0, tiled=True
        ).astype(jnp.float32),
    )
    return (
        output,
        grad_input,
        grad_query,
        grad_key,
        grad_value,
        grad_out_proj,
        grad_gain_attn,
        grad_gain_ffn,
        grad_router,
        grad_shared_gate,
        grad_shared_up,
        grad_shared_down,
        grad_shared_switch,
        grad_expert_gate,
        grad_expert_up,
        grad_expert_down,
    )


def solution(mesh):
    in_specs = (
        P("dp", None),
        P("dp", "tensor"),
        P("dp", "tensor"),
        P("dp", "tensor"),
        P("tensor", "dp"),
        P("dp"),
        P("dp"),
        P("dp", None),
        P("dp", "tensor"),
        P("dp", "tensor"),
        P("tensor", "dp"),
        P("dp"),
        P("dp", None, "tensor"),
        P("dp", None, "tensor"),
        P("dp", "tensor", None),
        P("dp", None),
        P("dp", None),
        P("dp", None),
    )
    out_specs = (
        P("dp", None),
        P("dp", None),
        P("dp", "tensor"),
        P("dp", "tensor"),
        P("dp", "tensor"),
        P("tensor", "dp"),
        P("dp"),
        P("dp"),
        P("dp", None),
        P("dp", "tensor"),
        P("dp", "tensor"),
        P("tensor", "dp"),
        P("dp"),
        P("dp", None, "tensor"),
        P("dp", None, "tensor"),
        P("dp", "tensor", None),
    )
    return jax.shard_map(shards, mesh=mesh, in_specs=in_specs, out_specs=out_specs, check_vma=False)
```

profile of v0, /device:TPU:0, one launch (start us, length us, event | category | flops | bytes accessed | tf_op | source)
XLA Modules:
  0.0 1489.3 jit_solution(17194333472703945350)
XLA Ops:
  10.7 10.4 all-gather
  24.6 15.8 %all-gather.13.cloned.1.call-done = bf16[2048,512]{1,0:T(8,128)(2,1)} async-done(((bf16[256,512]{1,0:T(8,128)(2,1)}), bf16[2048,512]{1,0:T(8,128)(2,1)}) %all-gather.13.cloned.1.call-update) | async-done | bytes 2097168 | tf_op jit(solution)/shard_map/all_gather | solution.py:156
  45.1 25.0 %all-gather.15.cloned.1.call-done = bf16[2048,512]{1,0:T(8,128)(2,1)} async-done(((bf16[256,512]{1,0:T(8,128)(2,1)}), bf16[2048,512]{1,0:T(8,128)(2,1)}) %all-gather.15.cloned.1.call-update) | async-done | bytes 2097168 | tf_op jit(solution)/shard_map/all_gather | solution.py:157
  80.2 19.6 %all-gather.11.cloned.1.call-done = bf16[2048,512]{1,0:T(8,128)(2,1)} async-done(((bf16[256,512]{1,0:T(8,128)(2,1)}), bf16[2048,512]{1,0:T(8,128)(2,1)}) %all-gather.11.cloned.1.call-update) | async-done | bytes 2097168 | tf_op jit(solution)/shard_map/all_gather | solution.py:158
  103.3 26.4 %all-gather.17.cloned.1.call-done = bf16[512,2048]{1,0:T(8,128)(2,1)} async-done(((bf16[512,256]{1,0:T(8,128)(2,1)}), bf16[512,2048]{1,0:T(8,128)(2,1)}) %all-gather.17.cloned.1.call-update) | async-done | bytes 2097168 | tf_op jit(solution)/shard_map/all_gather | solution.py:159
  129.7 3.6 fusion.83
  135.2 9.1 all-gather.1
  144.4 4.5 reduce-window.6
  149.4 70.2 %all-reduce.10.cloned.1.call-done = f32[256,2048]{1,0:T(8,128)} async-done(((f32[256,2048]{1,0:T(8,128)}), f32[256,2048]{1,0:T(8,128)}) %all-reduce.10.cloned.1.call-update) | async-done | bytes 2097168 | tf_op jit(solution)/shard_map/psum | solution.py:195
  224.4 23.2 %scatter_custom_fusion = bf16[1536,2048]{1,0:T(8,128)(2,1)} fusion(s32[1024]{0:T(1024)S(1)} %bitcast.175, bf16[256,2048]{1,0:T(8,128)(2,1)} %multiply_convert_fusion.6, s32[1024]{0:T(1024)S(1)} %broadcast_clamp_fusion.1, bf16[]{:T(256)} %constant.112.clone.1), kind=kCustom, calls=%fused_computation.17 | custom fusion | bytes 6291968 | tf_op jit(solution)/shard_map/scatter | solution.py:109
  247.6 12.6 copy.214
  260.3 4.9 all-to-all-start
  265.9 94.0 %all-to-all-done = bf16[2,768,2048]{2,0,1:T(2,128)(2,1)} async-done(((bf16[2,768,2048]{2,0,1:T(2,128)(2,1)}), bf16[2,768,2048]{2,0,1:T(2,128)(2,1)}, u32[]{:S(2)}, u32[]{:S(2)}) %all-to-all-start) | async-done | bytes 6291488 | tf_op jit(solution)/shard_map/all_to_all | solution.py:112
  359.9 8.5 fusion.14
  368.4 10.1 multiply_convert_fusion.4
  378.5 3.9 convolution_convert_fusion.3
  382.4 18.8 %copy.217 = bf16[2,768,2048]{2,0,1:T(2,128)(2,1)} copy(bf16[2,768,2048]{2,1,0:T(8,128)(2,1)S(1)} %convolution_convert_fusion.3) | data formatting | bytes 12582912 | tf_op jit(solution)/shard_map/convert_element_type | solution.py:221
  401.2 4.8 all-to-all-start.1
  408.8 6.8 mul.698
  415.7 10.1 mul.699
  425.7 55.0 %all_gather.39 = bf16[2048,16]{0,1:T(8,128)(2,1)S(1)} all-gather(bf16[256,16]{0,1:T(8,128)(2,1)S(1)} %copy-done.55), channel_id=1, replica_groups=mesh['dp'=8,'tensor'=4] {'dp'}, dimensions={0}, use_global_device_ids=true | all-gather | bytes 73728 | tf_op jit(solution)/shard_map/all_gather | solution.py:165
  483.0 5.9 fusion.85
  488.9 6.5 multiply_convert_fusion.9
  495.4 6.3 multiply_reduce_fusion.4
  501.6 8.4 copy.218
  510.0 12.6 gather_fusion
  522.6 7.2 reshape.474
  529.8 5.1 multiply_reduce_fusion
  534.9 20.0 %all-reduce.3 = (f32[256,4]{1,0:T(8,128)S(1)}, f32[256]{0:T(256)S(1)}) all-reduce(f32[256,4]{1,0:T(8,128)S(1)} %multiply_reduce_fusion, f32[256]{0:T(256)S(1)} %get-tuple-element.121), channel_id=1, replica_groups=mesh['dp'=8,'tensor'=4] {'tensor'}, use_global_device_ids=true, to_apply=%region_15.16 | all-reduce | flops 1280 | bytes 10240 | tf_op jit(solution)/shard_map/psum | solution.py:291
  555.3 12.2 scatter_custom_fusion.1
  567.4 11.1 copy.224
  578.5 74.6 %all_to_all.20 = bf16[2,768,2048]{2,0,1:T(2,128)(2,1)S(1)} all-to-all(bf16[2,768,2048]{2,0,1:T(2,128)(2,1)S(1)} %copy.224), channel_id=1, replica_groups=mesh['dp'=8,'tensor'=4] {'dp'}, dimensions={1} | all-to-all | bytes 12582912 | tf_op jit(solution)/shard_map/all_to_all | solution.py:112
  653.1 8.3 multiply_convert_fusion.2
  661.4 3.6 fusion.86
  665.0 6.7 convolution_add_fusion
  671.7 22.0 %copy.226 = f32[2,768,2048]{2,0,1:T(2,128)} copy(f32[2,768,2048]{2,1,0:T(8,128)} %convolution_add_fusion) | data formatting | bytes 25165824 | tf_op jit(solution)/shard_map/add | solution.py:271
  693.8 5.5 all-to-all-start.3
  699.4 141.9 %all-gather.2 = bf16[8,1,256]{2,1,0:T(2,128)(2,1)S(1)} all-gather(bf16[1,1,256]{2,1,0:T(2,128)(2,1)S(1)} %reshape.526), channel_id=1, replica_groups=mesh['dp'=8,'tensor'=4] {'dp'}, dimensions={0}, use_global_device_ids=true | all-gather | bytes 4608 | tf_op jit(solution)/shard_map/all_gather | solution.py:166
  841.7 5.6 multiply_convert_fusion.7
  848.1 5.8 fusion.87
  853.9 16.4 %copy.227 = f32[2,768,2048]{2,1,0:T(8,128)} copy(f32[2,768,2048]{2,0,1:T(2,128)} %all-to-all-done.3) | data formatting | bytes 25165824 | tf_op jit(solution)/shard_map/all_to_all | solution.py:287
  870.3 14.0 gather_fusion.1
  884.3 9.8 reshape.477
  894.0 10.0 reduce_sum.164
  904.0 7.0 fusion.23
  912.1 5.4 convolution_convert_fusion
  918.6 4.3 convolution_convert_fusion.2
  923.0 4.3 convolution_convert_fusion.1
  928.0 14.2 fusion.78
  942.2 6.3 fusion.35
  948.5 45.4 %all-reduce.12.cloned.1.call-done = f32[256,2048]{1,0:T(8,128)} async-done(((f32[256,2048]{1,0:T(8,128)}), f32[256,2048]{1,0:T(8,128)}) %all-reduce.12.cloned.1.call-update) | async-done | bytes 2097168 | tf_op jit(solution)/shard_map/psum | solution.py:291
  1013.7 3.6 convolution_convert_fusion.4
  1029.1 10.4 fusion
  1041.8 11.2 fusion.10
  1053.0 11.1 fusion.8
  1064.1 26.1 %reduce-scatter.23.cloned.1.call-done = bf16[1408,256]{1,0:T(8,128)(2,1)} async-done(((bf16[1408,2048]{1,0:T(8,128)(2,1)}), bf16[1408,256]{1,0:T(8,128)(2,1)}) %reduce-scatter.23.cloned.1.call-update) | async-done | bytes 720912 | tf_op jit(solution)/shard_map/reduce_scatter | solution.py:360
  1092.5 60.0 %reduce-scatter.19.cloned.1.call-done = bf16[256,1408]{1,0:T(8,128)(2,1)} async-done(((bf16[2048,1408]{1,0:T(8,128)(2,1)}), bf16[256,1408]{1,0:T(8,128)(2,1)}) %reduce-scatter.19.cloned.1.call-update) | async-done | bytes 720912 | tf_op jit(solution)/shard_map/reduce_scatter | solution.py:354
  1154.8 60.2 %reduce-scatter.21.cloned.1.call-done = bf16[256,1408]{1,0:T(8,128)(2,1)} async-done(((bf16[2048,1408]{1,0:T(8,128)(2,1)}), bf16[256,1408]{1,0:T(8,128)(2,1)}) %reduce-scatter.21.cloned.1.call-update) | async-done | bytes 720912 | tf_op jit(solution)/shard_map/reduce_scatter | solution.py:357
  1217.3 86.7 %all-reduce.14.cloned.1.call-done = (bf16[256,2048]{1,0:T(8,128)(2,1)}, bf16[256,2048]{1,0:T(8,128)(2,1)}) async-done(((bf16[256,2048]{1,0:T(8,128)(2,1)}, bf16[256,2048]{1,0:T(8,128)(2,1)}), (bf16[256,2048]{1,0:T(8,128)(2,1)}, bf16[256,2048]{1,0:T(8,128)(2,1)})) %all-reduce.14.cloned.1.call-update) | async-done | bytes 2097168 | tf_op jit(solution)/shard_map/psum | solution.py:240
  1306.4 23.8 %all-reduce.4 = (bf16[2048]{0:T(1024)(128)(2,1)S(1)}, bf16[2048]{0:T(1024)(128)(2,1)S(1)}, bf16[2048]{0:T(1024)(128)(2,1)S(1)}) all-reduce(bf16[2048]{0:T(1024)(128)(2,1)S(1)} %get-tuple-element.69, bf16[2048]{0:T(1024)(128)(2,1)S(1)} %get-tuple-element.57, ...), channel_id=6, replica_groups=mesh['dp'=8,'tensor'=4] {'dp'}, use_global_device_ids=true, to_apply=%region_29.30.clone | all-reduce | flops 6144 | bytes 24576
  1336.7 10.7 reduce-scatter.15.cloned.1.call-done
  1349.1 42.5 %reduce-scatter.13.cloned.1.call-done = bf16[256,512]{1,0:T(8,128)(2,1)} async-done(((bf16[2048,512]{1,0:T(8,128)(2,1)}), bf16[256,512]{1,0:T(8,128)(2,1)}) %reduce-scatter.13.cloned.1.call-update) | async-done | bytes 262160 | tf_op jit(solution)/shard_map/reduce_scatter | solution.py:348
  1393.4 42.5 %reduce-scatter.11.cloned.1.call-done = bf16[256,512]{1,0:T(8,128)(2,1)} async-done(((bf16[2048,512]{1,0:T(8,128)(2,1)}), bf16[256,512]{1,0:T(8,128)(2,1)}) %reduce-scatter.11.cloned.1.call-update) | async-done | bytes 262160 | tf_op jit(solution)/shard_map/reduce_scatter | solution.py:345
  1437.7 42.5 %reduce-scatter.9.cloned.1.call-done = bf16[256,512]{1,0:T(8,128)(2,1)} async-done(((bf16[2048,512]{1,0:T(8,128)(2,1)}), bf16[256,512]{1,0:T(8,128)(2,1)}) %reduce-scatter.9.cloned.1.call-update) | async-done | bytes 262160 | tf_op jit(solution)/shard_map/reduce_scatter | solution.py:342
  (265 shorter events, 98.4 us)
Async XLA Ops:
  7.2 371.3 %copy-start = (bf16[2,352,2048]{2,1,0:T(8,128)(2,1)S(1)}, bf16[2,352,2048]{2,1,0:T(8,128)(2,1)}, u32[]{:S(2)}) copy-start(bf16[2,352,2048]{2,1,0:T(8,128)(2,1)} %param.32) | copy-start | bytes 8650756
  7.2 15.5 %copy-start.56 = (s32[1,256]{1,0:T(1,128)S(1)}, s32[1,256]{1,0:T(1,128)}, u32[]{:S(2)}) copy-start(s32[1,256]{1,0:T(1,128)} %param.34) | copy-start | bytes 3076
  7.2 33.2 %all-gather.13.cloned.1.call-start = ((), (), s32[]{:S(2)}) async-start(), calls=%async_computation.13 | async-start | bytes 2359296 | tf_op jit(solution)/shard_map/all_gather | solution.py:156
  7.9 62.2 %all-gather.15.cloned.1.call-start = ((), (), s32[]{:S(2)}) async-start(), calls=%async_computation.14 | async-start | bytes 2359296 | tf_op jit(solution)/shard_map/all_gather | solution.py:157
  8.7 91.1 %all-gather.11.cloned.1.call-start = ((), (), s32[]{:S(2)}) async-start(), calls=%async_computation.12 | async-start | bytes 2359296 | tf_op jit(solution)/shard_map/all_gather | solution.py:158
  9.4 120.3 %all-gather.17.cloned.1.call-start = ((), (), s32[]{:S(2)}) async-start(), calls=%async_computation.15 | async-start | bytes 2359296 | tf_op jit(solution)/shard_map/all_gather | solution.py:159
  10.0 209.7 %all-reduce.10.cloned.1.call-start = ((), (), s32[]{:S(2)}) async-start(), calls=%async_computation.16 | async-start | bytes 4194304 | tf_op jit(solution)/shard_map/psum | solution.py:195
  21.1 78.7 %copy-start.43 = (f32[8,1,256]{2,1,0:T(1,128)}, f32[8,1,256]{2,1,0:T(1,128)S(1)}, u32[]{:S(2)}) copy-start(f32[8,1,256]{2,1,0:T(1,128)S(1)} %convert_element_type.297) | copy-start | bytes 24580
  22.7 77.2 %copy-start.50 = (f32[256]{0:T(256)}, f32[256]{0:T(256)S(1)}, u32[]{:S(2)}) copy-start(f32[256]{0:T(256)S(1)} %add_rsqrt_fusion.1) | copy-start | bytes 3076
  24.6 52.9 %copy-start.24 = (f32[256,64]{1,0:T(8,128)}, f32[256,64]{1,0:T(8,128)S(1)}, u32[]{:S(2)}) copy-start(f32[256,64]{1,0:T(8,128)S(1)} %get-tuple-element.114) | copy-start | bytes 196612
  75.6 1.9 copy-start.42
  80.2 22.4 %copy-start.57 = (f32[4,256]{1,0:T(4,128)}, f32[4,256]{1,0:T(4,128)S(1)}, u32[]{:S(2)}) copy-start(f32[4,256]{1,0:T(4,128)S(1)} %get-tuple-element.115) | copy-start | bytes 12292
  99.8 2.8 copy-start.11
  103.3 30.0 %copy-start.27 = (bf16[4,128,256]{2,1,0:T(8,128)(2,1)}, bf16[4,128,256]{2,1,0:T(8,128)(2,1)S(1)}, u32[]{:S(2)}) copy-start(bf16[4,128,256]{2,1,0:T(8,128)(2,1)S(1)} %convolution_convert_fusion.11) | copy-start | bytes 786436
  133.3 1.9 copy-start.59
  133.4 349.6 %all-gather.19.cloned.1.call-start = ((), (), s32[]{:S(2)}) async-start(), calls=%async_computation.17 | async-start | bytes 6488064 | tf_op jit(solution)/shard_map/all_gather | solution.py:160
  134.0 354.9 %all-gather.21.cloned.1.call-start = ((), (), s32[]{:S(2)}) async-start(), calls=%async_computation.18 | async-start | bytes 6488064 | tf_op jit(solution)/shard_map/all_gather | solution.py:161
  144.4 77.6 %copy-start.47 = (f32[8,1,256]{2,1,0:T(1,128)}, f32[8,1,256]{2,1,0:T(1,128)S(1)}, u32[]{:S(2)}) copy-start(f32[8,1,256]{2,1,0:T(1,128)S(1)} %convert_element_type.298) | copy-start | bytes 24580
  221.9 2.5 copy-start.52
  260.3 99.6 %all-to-all-start = ((bf16[2,768,2048]{2,0,1:T(2,128)(2,1)}), bf16[2,768,2048]{2,0,1:T(2,128)(2,1)}, u32[]{:S(2)}, u32[]{:S(2)}) async-start(bf16[2,768,2048]{2,0,1:T(2,128)(2,1)} %copy.214), calls=%async_computation | async-start | bytes 12582912 | tf_op jit(solution)/shard_map/all_to_all | solution.py:112
  265.1 230.2 %all-gather.23.cloned.1.call-start = ((), (), s32[]{:S(2)}) async-start(), calls=%async_computation.19 | async-start | bytes 6488064 | tf_op jit(solution)/shard_map/all_gather | solution.py:162
  359.9 8.5 copy-start.19
  368.4 10.1 copy-start.63
  378.5 3.9 copy-start.62
  401.2 100.5 %all-to-all-start.1 = ((bf16[2,768,2048]{2,0,1:T(2,128)(2,1)}), bf16[2,768,2048]{2,0,1:T(2,128)(2,1)}, u32[]{:S(2)}, u32[]{:S(2)}) async-start(bf16[2,768,2048]{2,0,1:T(2,128)(2,1)} %copy.217), calls=%async_computation.1 | async-start | bytes 12582912 | tf_op jit(solution)/shard_map/all_to_all | solution.py:230
  415.7 10.1 copy-start.55
  578.5 74.6 %copy-start.64 = (f32[2,768,352]{1,2,0:T(8,128)S(1)}, f32[2,768,352]{1,2,0:T(8,128)}, u32[]{:S(2)}) copy-start(f32[2,768,352]{1,2,0:T(8,128)} %copy-done.63) | copy-start | bytes 6488068
  653.1 8.3 copy-start.14
  653.1 8.3 copy-start.18
  661.4 3.6 copy-start.16
  661.4 3.6 copy-start.26
  661.4 3.6 copy-start.20
  693.8 5.6 copy-start.60
  693.8 147.5 %copy-start.6 = (bf16[256,2048]{1,0:T(8,128)(2,1)S(1)}, bf16[256,2048]{1,0:T(8,128)(2,1)}, u32[]{:S(2)}) copy-start(bf16[256,2048]{1,0:T(8,128)(2,1)} %multiply_convert_fusion.6) | copy-start | bytes 3145732
  693.8 147.9 %copy-start.9 = (bf16[256,2048]{1,0:T(8,128)(2,1)S(1)}, bf16[256,2048]{1,0:T(8,128)(2,1)}, u32[]{:S(2)}) copy-start(bf16[256,2048]{1,0:T(8,128)(2,1)} %param.35) | copy-start | bytes 3145732
  693.8 160.1 %all-to-all-start.3 = ((f32[2,768,2048]{2,0,1:T(2,128)}), f32[2,768,2048]{2,0,1:T(2,128)}, u32[]{:S(2)}, u32[]{:S(2)}) async-start(f32[2,768,2048]{2,0,1:T(2,128)} %copy.226), calls=%async_computation.3 | async-start | bytes 25165824 | tf_op jit(solution)/shard_map/all_to_all | solution.py:287
  699.3 294.6 %all-reduce.12.cloned.1.call-start = ((), (), s32[]{:S(2)}) async-start(), calls=%async_computation.20 | async-start | bytes 4194304 | tf_op jit(solution)/shard_map/psum | solution.py:291
  911.0 116.8 %reduce-scatter.17.cloned.1.call-start = ((), (), s32[]{:S(2)}) async-start(), calls=%async_computation.25 | async-start | bytes 73728 | tf_op jit(solution)/shard_map/reduce_scatter | solution.py:369
  912.0 178.1 %reduce-scatter.23.cloned.1.call-start = ((), (), s32[]{:S(2)}) async-start(), calls=%async_computation.28 | async-start | bytes 6488064 | tf_op jit(solution)/shard_map/reduce_scatter | solution.py:360
  917.5 235.0 %reduce-scatter.19.cloned.1.call-start = ((), (), s32[]{:S(2)}) async-start(), calls=%async_computation.26 | async-start | bytes 6488064 | tf_op jit(solution)/shard_map/reduce_scatter | solution.py:354
  923.0 292.0 %reduce-scatter.21.cloned.1.call-start = ((), (), s32[]{:S(2)}) async-start(), calls=%async_computation.27 | async-start | bytes 6488064 | tf_op jit(solution)/shard_map/reduce_scatter | solution.py:357
  927.3 376.7 %all-reduce.14.cloned.1.call-start = ((), (), s32[]{:S(2)}) async-start(), calls=%async_computation.29 | async-start | bytes 4194304 | tf_op jit(solution)/shard_map/psum | solution.py:240
  928.0 14.2 copy-start.23
  942.2 51.7 %copy-start.3 = (f32[256,2048]{1,0:T(8,128)S(1)}, f32[256,2048]{1,0:T(8,128)}, u32[]{:S(2)}) copy-start(f32[256,2048]{1,0:T(8,128)} %copy-done.2) | copy-start | bytes 6291460
  942.2 51.7 %copy-start.40 = (bf16[2048,16]{0,1:T(8,128)(2,1)S(1)}, bf16[2048,16]{0,1:T(8,128)(2,1)}, u32[]{:S(2)}) copy-start(bf16[2048,16]{0,1:T(8,128)(2,1)} %copy-done.39) | copy-start | bytes 196612
  942.2 51.7 %copy-start.48 = (f32[8,1,256]{2,1,0:T(1,128)S(1)}, f32[8,1,256]{2,1,0:T(1,128)}, u32[]{:S(2)}) copy-start(f32[8,1,256]{2,1,0:T(1,128)} %copy-done.47) | copy-start | bytes 24580
  942.2 51.7 %copy-start.53 = (f32[256]{0:T(256)S(1)}, f32[256]{0:T(256)}, u32[]{:S(2)}) copy-start(f32[256]{0:T(256)} %copy-done.52) | copy-start | bytes 3076
  993.9 2.6 copy-start.10
  996.6 2.0 copy-start.13
  999.4 1.7 copy-start.12
  999.5 1.9 copy-start.34
  999.5 1.9 copy-start.36
  1006.8 2.5 copy-start.21
  1012.7 334.6 %reduce-scatter.15.cloned.1.call-start = ((), (), s32[]{:S(2)}) async-start(), calls=%async_computation.24 | async-start | bytes 2359296 | tf_op jit(solution)/shard_map/reduce_scatter | solution.py:351
  1017.3 374.3 %reduce-scatter.13.cloned.1.call-start = ((), (), s32[]{:S(2)}) async-start(), calls=%async_computation.23 | async-start | bytes 2359296 | tf_op jit(solution)/shard_map/reduce_scatter | solution.py:348
  1021.5 3.6 copy-start.61
  1021.5 414.4 %reduce-scatter.11.cloned.1.call-start = ((), (), s32[]{:S(2)}) async-start(), calls=%async_computation.22 | async-start | bytes 2359296 | tf_op jit(solution)/shard_map/reduce_scatter | solution.py:345
  1025.0 455.2 %reduce-scatter.9.cloned.1.call-start = ((), (), s32[]{:S(2)}) async-start(), calls=%async_computation.21 | async-start | bytes 2359296 | tf_op jit(solution)/shard_map/reduce_scatter | solution.py:342
  1029.1 10.4 copy-start.4
  1041.8 11.2 copy-start.17
  1332.0 2.6 copy-start.5
  1332.0 2.6 copy-start.8
  1332.1 2.6 copy-start.15
  1334.7 147.3 %copy-start.1 = (bf16[2,352,2048]{2,1,0:T(8,128)(2,1)S(1)}, bf16[2,352,2048]{2,1,0:T(8,128)(2,1)}, u32[]{:S(2)}) copy-start(bf16[2,352,2048]{2,1,0:T(8,128)(2,1)} %param.32) | copy-start | bytes 8650756
  (22 other events, 21.7 us)
Sparse Core Ops, SparseCore 0:
  9.9 30.4 all-gather.12
  42.3 27.7 all-gather.14
  72.0 27.7 all-gather.10
  101.6 28.0 all-gather.16
  133.5 86.1 all-reduce.9
  221.4 42.2 all-gather.18
  265.5 77.6 all-gather.20
  345.2 57.3 all-gather.22
  911.2 82.7 all-reduce.11
  997.3 30.4 reduce-scatter.16
  1031.3 58.8 reduce-scatter.22
  1093.4 59.0 reduce-scatter.18
  1155.9 58.9 reduce-scatter.20
  1217.8 86.1 all-reduce.13
  1307.1 40.1 reduce-scatter.14
  1350.5 41.1 reduce-scatter.12
  1394.7 41.1 reduce-scatter.10
  1439.0 41.1 reduce-scatter.8
where the time goes:
time: 1500 us; the launch traced here: 1490 us
  waiting for transfers between devices  673 us (45%)
  blocking collectives  335 us (22%)
  local copies, waits for them, and re-layouts  204 us (14%)
  matrix products  168 us (11%)
  other arithmetic  76.3 us (5%)
  between operations  16.4 us (1%)
  starting transfers between devices  16.1 us (1%)
    all_gather x1, blocking collectives, shards(): lax.all_gather(shared_switch, 'dp', axis=0, tiled=True)  142 us
    all_to_all x1, waiting for transfers between devices, dispatch(): return lax.all_to_all(buffer, 'dp', split_axis=1, concat_axis=1, tiled=True)  94 us
    psum x1, waiting for transfers between devices, shards(): lax.psum((routed + switch * shared_part).astype(jnp.bfloat16), 'tensor')  86.7 us
    all_to_all x1, blocking collectives, dispatch(): return lax.all_to_all(buffer, 'dp', split_axis=1, concat_axis=1, tiled=True)  74.6 us
    psum x1, waiting for transfers between devices, shards(): lax.psum(jnp.dot(context_flat, out_full, preferred_element_type=jnp.float...  70.2 us
    reduce_scatter x1, waiting for transfers between devices, shards(): lax.psum_scatter(grad_shared_up.astype(jnp.bfloat16), 'dp', scatter_dimen...  60.2 us
    reduce_scatter x1, waiting for transfers between devices, shards(): lax.psum_scatter(grad_shared_gate.astype(jnp.bfloat16), 'dp', scatter_dim...  60 us
    all_gather x1, blocking collectives, shards(): lax.all_gather(w_router, 'dp', axis=0, tiled=True)  55 us
  transfers between devices with their start and end apart: 21, of which 16 were waited for; matrix products, arithmetic and copies ran while one was open for 19% of the time, Pallas kernels for 0%

commit v1 on v0

v1 whole, which is shorter than its diff:
```python
import functools

import jax
import jax.numpy as jnp
from jax import lax
from jax.experimental import pallas as pl
from jax.experimental.pallas import tpu as pltpu
from jax.sharding import PartitionSpec as P

HEAD_DIM = 128
TOP = 4
SEQ = 256


EPSILON = 1e-06
MESH = pl.DeviceIdType.MESH


def ring_chip(position, chips):
    half = chips // 2
    upper = position // half
    return position + upper * (chips - 1 + half - 2 * position)


def ring_spot(chip, chips):
    return ring_chip(chip, chips)


def greet(partners):
    barrier = pltpu.get_barrier_semaphore()
    for partner in partners:
        pl.semaphore_signal(barrier, inc=1, device_id=partner, device_id_type=MESH)
    pl.semaphore_wait(barrier, len(partners))


def remote(source, target, axis, device, sends, recvs, slot):
    return pltpu.make_async_remote_copy(
        src_ref=source,
        dst_ref=target,
        send_sem=sends.at[slot],
        recv_sem=recvs.at[slot],
        device_id={axis: device},
        device_id_type=MESH,
    )


class Ring:
    def __init__(self, ranks):
        self.ranks = ranks
        self.chips = ranks // 2
        self.half = self.chips // 2
        self.me = lax.axis_index("dp")
        self.core = self.me % 2
        self.position = ring_spot(self.me // 2, self.chips)
        self.sibling = self.me + 1 - 2 * self.core
        self.ahead = self.device(1)
        self.behind = self.device(-1)

    def chip(self, offset):
        return ring_chip((self.position + offset + self.chips) % self.chips, self.chips)

    def device(self, offset):
        return self.chip(offset) * 2 + self.core

    def other(self, offset):
        return self.chip(offset) * 2 + 1 - self.core

    def partners(self):
        return [{"dp": self.ahead}, {"dp": self.behind}, {"dp": self.sibling}]


def gather_slots(half):
    return 2 * half


def side_slots(half):
    return 2 * half + 1


class RingGather:
    def __init__(self, ring, place, rows, sends, recvs, side_sends, side_recvs, base, side_base):
        self.ring, self.place, self.rows, self.cut = ring, place, rows, rows // 2
        self.sends, self.recvs = sends, recvs
        self.side_sends, self.side_recvs = side_sends, side_recvs
        self.base, self.side_base = base, side_base
        self.started, self.side_sizes = [], []

    def hop(self, source, target, device, slot):
        copy = remote(source, target, "dp", device, self.sends, self.recvs, self.base + slot)
        copy.start()
        self.started.append(copy)
        return copy

    def share(self, source, target, size):
        slot = self.side_base + len(self.side_sizes)
        copy = remote(source, target, "dp", self.ring.sibling, self.side_sends, self.side_recvs, slot)
        copy.start()
        self.started.append(copy)
        self.side_sizes.append(size)

    def begin(self, source):
        ring = self.ring
        target = self.place(ring.me, 0, self.rows)
        ahead = self.hop(source, target, ring.ahead, 0)
        behind = self.hop(source, target, ring.behind, ring.half)
        self.share(source, target, self.rows)
        self.last = (ahead, behind)

    def step(self, number):
        ring = self.ring
        following = []
        for which, sign in enumerate((-1, 1)):
            owner = ring.device(sign * number)
            onward = (ring.ahead, ring.behind)[which]
            self.last[which].wait_recv()
            if number < ring.half:
                block = self.place(owner, 0, self.rows)
                if number == ring.half - 1:
                    part = self.place(owner, (0, self.cut)[which], self.cut)
                else:
                    part = block
                following.append(self.hop(part, part, onward, which * ring.half + number))
                self.share(block, block, self.rows)
            else:
                part = self.place(owner, (0, self.cut)[which], self.cut)
                self.share(part, part, self.cut)
        self.last = following

    def finish(self):
        ring = self.ring
        for copy in self.started:
            copy.wait_send()
        for index, size in enumerate(self.side_sizes):
            block = self.place(ring.me, 0, size)
            remote(
                block, block, "dp", ring.sibling, self.side_sends, self.side_recvs, self.side_base + index
            ).wait_recv()


def gather_kernel(ranks, counts, *refs):
    amount = len(counts)
    sources, all_ref = refs[:amount], refs[amount]
    stage, local_sem, sends, recvs, side_sends, side_recvs = refs[amount + 1 :]
    rows = stage.shape[0]
    ring = Ring(ranks)
    loads, start = [], 0
    for index, count in enumerate(counts):
        load = pltpu.make_async_copy(
            sources[index], stage.at[:, pl.ds(start, count)], local_sem.at[index]
        )
        load.start()
        loads.append(load)
        start += count

    def place(device, first, size):
        return all_ref.at[pl.ds(device * rows + first, size)]

    greet(ring.partners())
    for load in loads:
        load.wait()
    work = RingGather(ring, place, rows, sends, recvs, side_sends, side_recvs, 0, 0)
    work.begin(stage)
    store = pltpu.make_async_copy(stage, place(ring.me, 0, rows), local_sem.at[amount])
    store.start()
    for number in range(1, ring.half + 1):
        work.step(number)
    store.wait()
    work.finish()


def gather_dp(values, ranks, identity):
    half = ranks // 4
    rows = values[0].shape[0]
    counts = [value.shape[1] for value in values]
    return pl.pallas_call(
        functools.partial(gather_kernel, ranks, counts),
        out_shape=jax.ShapeDtypeStruct((ranks * rows, sum(counts)), values[0].dtype),
        in_specs=[pl.BlockSpec(memory_space=pl.ANY)] * len(values),
        out_specs=pl.BlockSpec(memory_space=pl.ANY),
        scratch_shapes=[
            pltpu.VMEM((rows, sum(counts)), values[0].dtype),
            pltpu.SemaphoreType.DMA((len(counts) + 1,)),
            pltpu.SemaphoreType.DMA((gather_slots(half),)),
            pltpu.SemaphoreType.DMA((gather_slots(half),)),
            pltpu.SemaphoreType.DMA((side_slots(half),)),
            pltpu.SemaphoreType.DMA((side_slots(half),)),
        ],
        compiler_params=pltpu.CompilerParams(collective_id=identity, has_side_effects=True),
        name="gather_dp",
    )(*values)


def near_first(peers):
    order = [0]
    for step in range(1, peers // 2 + 1):
        order.append(step)
        if peers - step != step:
            order.append(peers - step)
    return order


STRIP = 16


def strips(rows, body):
    strip = min(STRIP, rows)

    def step(index, carry):
        body(pl.ds(pl.multiple_of(index * strip, strip), strip), index * strip, strip)
        return carry

    lax.fori_loop(0, rows // strip, step, 0)


def middle_kernel(
    ranks,
    peers,
    part_ref,
    tokens_ref,
    gain_ref,
    all_ref,
    middle_ref,
    own,
    got,
    local_sem,
    z_sends,
    z_recvs,
    x_sends,
    x_recvs,
    sends,
    recvs,
    side_sends,
    side_recvs,
):
    ring = Ring(ranks)
    here = lax.axis_index("tensor")
    block = part_ref.shape[0]
    rows = block // peers
    away = [(here + k) % peers for k in range(peers)]
    greet(ring.partners() + [{"tensor": away[k]} for k in range(1, peers)])
    order = near_first(peers)
    exchanged = []
    for k in reversed(order[1:]):
        copy = remote(
            part_ref.at[pl.ds(away[k] * rows, rows)],
            got.at[peers - k - 1],
            "tensor",
            away[k],
            z_sends,
            z_recvs,
            peers - k - 1,
        )
        copy.start()
        exchanged.append(copy)
    for copy in exchanged:
        copy.wait()
    first = here * rows

    def norm(spot, start, size):
        mine = pl.ds(pl.multiple_of(first + start, size), size)
        total = part_ref[mine, :].astype(jnp.float32)
        for k in range(peers - 1):
            total = total + got[k, spot, :].astype(jnp.float32)
        middle = tokens_ref[mine, :].astype(jnp.float32) + total
        middle_ref[spot, :] = middle
        inverse = lax.rsqrt(jnp.mean(middle * middle, axis=-1, keepdims=True) + EPSILON)
        own[spot, :] = ((middle * inverse) * gain_ref[...]).astype(own.dtype)

    strips(rows, norm)

    def place_of(k):
        def place(device, start, size):
            return all_ref.at[pl.ds(device * block + away[k] * rows + start, size)]

        return place

    mine = place_of(0)(ring.me, 0, rows)
    forwards = []
    for k in order[1:]:
        copy = remote(own, mine, "tensor", away[k], x_sends, x_recvs, peers - k - 1)
        copy.start()
        forwards.append(copy)
    half = ring.half
    works = []
    for k in range(peers):
        works.append(
            RingGather(
                ring,
                place_of(k),
                rows,
                sends,
                recvs,
                side_sends,
                side_recvs,
                k * gather_slots(half),
                k * side_slots(half),
            )
        )
    works[0].begin(own)
    store = pltpu.make_async_copy(own, mine, local_sem)
    store.start()
    for index in range(len(order) + half):
        if 0 < index < len(order):
            k = order[index]
            spot = place_of(k)(ring.me, 0, rows)
            remote(own, spot, "tensor", away[k], x_sends, x_recvs, k - 1).wait_recv()
            works[k].begin(spot)
        for number in range(1, half + 1):
            if 0 <= index - number < len(order):
                works[order[index - number]].step(number)
    store.wait()
    for copy in forwards:
        copy.wait_send()
    for work in works:
        work.finish()


def middle_and_gather(part, tokens, gain, ranks, peers, identity):
    half = ranks // 4
    block, width = part.shape
    rows = block // peers
    vmem = pl.BlockSpec(memory_space=pltpu.VMEM)
    return pl.pallas_call(
        functools.partial(middle_kernel, ranks, peers),
        out_shape=(
            jax.ShapeDtypeStruct((ranks * block, width), part.dtype),
            jax.ShapeDtypeStruct((rows, width), jnp.float32),
        ),
        in_specs=[vmem, vmem, vmem],
        out_specs=(pl.BlockSpec(memory_space=pl.ANY), vmem),
        scratch_shapes=[
            pltpu.VMEM((rows, width), part.dtype),
            pltpu.VMEM((peers - 1, rows, width), part.dtype),
            pltpu.SemaphoreType.DMA,
            pltpu.SemaphoreType.DMA((peers - 1,)),
            pltpu.SemaphoreType.DMA((peers - 1,)),
            pltpu.SemaphoreType.DMA((peers - 1,)),
            pltpu.SemaphoreType.DMA((peers - 1,)),
            pltpu.SemaphoreType.DMA((peers * gather_slots(half),)),
            pltpu.SemaphoreType.DMA((peers * gather_slots(half),)),
            pltpu.SemaphoreType.DMA((peers * side_slots(half),)),
            pltpu.SemaphoreType.DMA((peers * side_slots(half),)),
        ],
        compiler_params=pltpu.CompilerParams(collective_id=identity, has_side_effects=True),
        name="middle_and_gather",
    )(part, tokens, gain)


class RingReduce:
    def __init__(self, ring, part_at, rows, side, stage, got, sends, recvs, side_sends, side_recvs, base, side_base):
        self.ring, self.part_at, self.rows, self.cut = ring, part_at, rows, rows // 2
        self.side, self.stage, self.got = side, stage, got
        self.sends, self.recvs = sends, recvs
        self.side_sends, self.side_recvs = side_sends, side_recvs
        self.base, self.side_base = base, side_base
        self.started = []
        self.arrivals = {}

    def order(self):
        half = self.ring.half
        offsets = [half]
        for distance in range(half - 1, 0, -1):
            offsets += [distance, self.ring.chips - distance]
        return offsets + [0]

    def hand_over(self, offset):
        ring = self.ring
        copy = remote(
            self.part_at(ring.other(offset)),
            self.side.at[offset],
            "dp",
            ring.sibling,
            self.side_sends,
            self.side_recvs,
            self.side_base + offset,
        )
        copy.start()
        self.started.append(copy)
        self.arrivals[offset] = copy

    def hop(self, source, target, device, slot):
        copy = remote(source, target, "dp", device, self.sends, self.recvs, self.base + slot)
        copy.start()
        self.started.append(copy)
        return copy

    def add(self, offset, extra, first, size):
        mine = self.part_at(self.ring.device(offset))

        def whole(spot, start, count):
            total = mine[spot, :].astype(jnp.float32) + self.side[offset, spot, :].astype(jnp.float32)
            self.stage[offset, spot, :] = total.astype(self.stage.dtype)

        def more(spot, start, count):
            here = pl.ds(pl.multiple_of(first + start, count), count)
            total = mine[here, :].astype(jnp.float32) + self.side[offset, here, :].astype(jnp.float32)
            total = total + extra[here, :].astype(jnp.float32)
            self.stage[offset, here, :] = total.astype(self.stage.dtype)

        if extra is None:
            strips(self.rows, whole)
            return
        strips(size, more)
        if size < self.rows:
            rest = self.rows - size
            begin = 0 if first else size

            def plain(spot, start, count):
                here = pl.ds(pl.multiple_of(begin + start, count), count)
                total = mine[here, :].astype(jnp.float32) + self.side[offset, here, :].astype(jnp.float32)
                self.stage[offset, here, :] = total.astype(self.stage.dtype)

            strips(rest, plain)

    def step(self, number):
        ring, half, cut = self.ring, self.ring.half, self.cut
        if number == 0:
            self.arrivals[half].wait_recv()
            self.add(half, None, 0, self.rows)
            self.last = []
            for which, device in enumerate((ring.ahead, ring.behind)):
                part = pl.ds((0, cut)[which], cut)
                self.last.append(
                    self.hop(
                        self.stage.at[half, part], self.got.at[which * half, part], device, which * half
                    )
                )
            return
        following = []
        for which, device in enumerate((ring.ahead, ring.behind)):
            distance = half - number
            offset = distance if which == 0 else ring.chips - distance
            self.arrivals[offset].wait_recv()
            self.last[which].wait_recv()
            extra = self.got.at[which * half + number - 1]
            if number == 1:
                self.add(offset, extra, (0, cut)[which], cut)
            else:
                self.add(offset, extra, 0, self.rows)
            following.append(
                self.hop(
                    self.stage.at[offset],
                    self.got.at[which * half + number],
                    device,
                    which * half + number,
                )
            )
        self.last = following

    def total(self, emit):
        half = self.ring.half
        self.arrivals[0].wait_recv()
        for copy in self.last:
            copy.wait_recv()
        mine = self.part_at(self.ring.me)

        def body(spot, start, size):
            value = mine[spot, :].astype(jnp.float32) + self.side[0, spot, :].astype(jnp.float32)
            value = value + self.got[half - 1, spot, :].astype(jnp.float32)
            value = value + self.got[2 * half - 1, spot, :].astype(jnp.float32)
            emit(spot, start, size, value)

        strips(self.rows, body)

    def finish(self):
        for copy in self.started:
            copy.wait_send()


def back_kernel(
    ranks,
    peers,
    part_ref,
    middle_ref,
    cot_ref,
    gain_ref,
    out_ref,
    grad_ref,
    gain_grad_ref,
    side,
    stage,
    got,
    z_stage,
    z_got,
    low_ref,
    sends,
    recvs,
    side_sends,
    side_recvs,
    z_sends,
    z_recvs,
    x_sends,
    x_recvs,
    local_sem,
):
    ring = Ring(ranks)
    here = lax.axis_index("tensor")
    block = cot_ref.shape[0]
    rows = block // peers
    half, chips = ring.half, ring.chips
    away = [(here + k) % peers for k in range(peers)]
    greet(ring.partners() + [{"tensor": away[k]} for k in range(1, peers)])
    order = list(reversed(near_first(peers)))
    works = {}
    for k in order:

        def part_at(device, k=k):
            return part_ref.at[pl.ds(device * block + away[k] * rows, rows)]

        works[k] = RingReduce(
            ring,
            part_at,
            rows,
            side.at[k],
            stage.at[k],
            got.at[k],
            sends,
            recvs,
            side_sends,
            side_recvs,
            k * 2 * half,
            k * chips,
        )
    for offset in works[order[0]].order():
        for k in order:
            works[k].hand_over(offset)
    reduced = []
    for index in range(len(order) + half):
        for number in range(0, half):
            if 0 <= index - number < len(order):
                works[order[index - number]].step(number)
        if 0 <= index - half < len(order):
            k = order[index - half]

            def emit(spot, start, size, value, k=k):
                z_stage[k, spot, :] = value.astype(z_stage.dtype)

            if k:
                works[k].total(emit)
                copy = remote(
                    z_stage.at[k], z_got.at[peers - k - 1], "tensor", away[k], z_sends, z_recvs, peers - k - 1
                )
                copy.start()
                reduced.append(copy)
    for copy in reduced:
        copy.wait_recv()
    first = here * rows
    gain_grad_ref[...] = jnp.zeros_like(gain_grad_ref)

    def norm(spot, start, size, value):
        for k in range(peers - 1):
            value = value + z_got[k, spot, :].astype(jnp.float32)
        middle = middle_ref[spot, :]
        inverse = lax.rsqrt(jnp.mean(middle * middle, axis=-1, keepdims=True) + EPSILON)
        normed = middle * inverse
        scaled = value * gain_ref[...]
        back = inverse * (scaled - normed * jnp.mean(scaled * normed, axis=-1, keepdims=True))
        mine = pl.ds(pl.multiple_of(first + start, size), size)
        grad = cot_ref[mine, :].astype(jnp.float32) + back
        grad_ref[spot, :] = grad
        low_ref[spot, :] = grad.astype(low_ref.dtype)
        gain_grad_ref[...] += jnp.sum(value * normed, axis=0, keepdims=True)

    works[0].total(norm)
    mine = out_ref.at[pl.ds(here * rows, rows)]
    spread = []
    for k in near_first(peers)[:0:-1]:
        copy = remote(low_ref, mine, "tensor", away[k], x_sends, x_recvs, peers - k - 1)
        copy.start()
        spread.append(copy)
    store = pltpu.make_async_copy(low_ref, mine, local_sem)
    store.start()
    store.wait()
    for copy in reduced:
        copy.wait_send()
    for copy in spread:
        copy.wait()
    for k in order:
        works[k].finish()


def reduce_and_norm(part, middle, cotangent, gain, ranks, peers, identity):
    half = ranks // 4
    chips = ranks // 2
    block, width = cotangent.shape
    rows = block // peers
    vmem = pl.BlockSpec(memory_space=pltpu.VMEM)
    low = part.dtype
    return pl.pallas_call(
        functools.partial(back_kernel, ranks, peers),
        out_shape=(
            jax.ShapeDtypeStruct((block, width), low),
            jax.ShapeDtypeStruct((rows, width), jnp.float32),
            jax.ShapeDtypeStruct((1, width), jnp.float32),
        ),
        in_specs=[vmem] * 4,
        out_specs=(pl.BlockSpec(memory_space=pl.ANY), vmem, vmem),
        scratch_shapes=[
            pltpu.VMEM((peers, chips, rows, width), low),
            pltpu.VMEM((peers, chips, rows, width), low),
            pltpu.VMEM((peers, 2 * half, rows, width), low),
            pltpu.VMEM((peers, rows, width), low),
            pltpu.VMEM((peers - 1, rows, width), low),
            pltpu.VMEM((rows, width), low),
            pltpu.SemaphoreType.DMA((peers * 2 * half,)),
            pltpu.SemaphoreType.DMA((peers * 2 * half,)),
            pltpu.SemaphoreType.DMA((peers * chips,)),
            pltpu.SemaphoreType.DMA((peers * chips,)),
            pltpu.SemaphoreType.DMA((peers - 1,)),
            pltpu.SemaphoreType.DMA((peers - 1,)),
            pltpu.SemaphoreType.DMA((peers - 1,)),
            pltpu.SemaphoreType.DMA((peers - 1,)),
            pltpu.SemaphoreType.DMA,
        ],
        compiler_params=pltpu.CompilerParams(
            collective_id=identity, has_side_effects=True, vmem_limit_bytes=50 << 20
        ),
        name="reduce_and_norm",
    )(part, middle, cotangent, gain)


def final_kernel(
    ranks,
    peers,
    part_ref,
    tokens_ref,
    gain_ref,
    grad_ref,
    gain_grad_ref,
    weights_ref,
    out_ref,
    sum_ref,
    small_ref,
    gains_ref,
    side,
    stage,
    got,
    z_got,
    low_ref,
    small_own,
    small_got,
    gains_own,
    gains_got,
    gains_part,
    gains_z,
    sends,
    recvs,
    side_sends,
    side_recvs,
    z_sends,
    z_recvs,
    x_sends,
    x_recvs,
    s_sends,
    s_recvs,
    g_sends,
    g_recvs,
    h_sends,
    h_recvs,
    local_sem,
):
    ring = Ring(ranks)
    here = lax.axis_index("tensor")
    block, width = part_ref.shape
    rows = block // peers
    half, chips = ring.half, ring.chips
    lot = weights_ref.shape[0] // ranks
    pieces = side.shape[0]
    size = lot // pieces
    wide = sum_ref.shape[1]
    columns = width // ranks
    away = [(here + k) % peers for k in range(peers)]
    others = [(ring.me + k) % ranks for k in range(ranks)]
    greet(
        [{"dp": others[k]} for k in range(1, ranks)] + [{"tensor": away[k]} for k in range(1, peers)]
    )
    far_first = near_first(peers)[:0:-1]
    exchanged = []
    for k in far_first:
        copy = remote(
            part_ref.at[pl.ds(away[k] * rows, rows)],
            z_got.at[peers - k - 1],
            "tensor",
            away[k],
            z_sends,
            z_recvs,
            peers - k - 1,
        )
        copy.start()
        exchanged.append(copy)
    works = []
    for piece in range(pieces):

        def part_at(device, piece=piece):
            return weights_ref.at[pl.ds(device * lot + piece * size, size)]

        works.append(
            RingReduce(
                ring,
                part_at,
                size,
                side.at[piece],
                stage.at[piece],
                got.at[piece],
                sends,
                recvs,
                side_sends,
                side_recvs,
                piece * 2 * half,
                piece * chips,
            )
        )
    for offset in works[0].order():
        for work in works:
            work.hand_over(offset)

    first = here * rows
    gains_own[...] = jnp.zeros_like(gains_own)
    gains_own[1:2, :] = gain_grad_ref[...]

    def norm(spot, start, count):
        mine = pl.ds(pl.multiple_of(first + start, count), count)
        value = part_ref[mine, :].astype(jnp.float32)
        for k in range(peers - 1):
            value = value + z_got[k, spot, :].astype(jnp.float32)
        inputs = tokens_ref[mine, :].astype(jnp.float32)
        inverse = lax.rsqrt(jnp.mean(inputs * inputs, axis=-1, keepdims=True) + EPSILON)
        normed = inputs * inverse
        scaled = value * gain_ref[...]
        back = inverse * (scaled - normed * jnp.mean(scaled * normed, axis=-1, keepdims=True))
        low_ref[spot, :] = (grad_ref[spot, :] + back).astype(low_ref.dtype)
        gains_own[0:1, :] += jnp.sum(value * normed, axis=0, keepdims=True)

    spread, handed = [], []
    mine = out_ref.at[pl.ds(here * rows, rows)]
    store = pltpu.make_async_copy(low_ref, mine, local_sem)

    def after_norm():
        for copy in exchanged:
            copy.wait()
        strips(rows, norm)
        for k in range(1, ranks):
            copy = remote(
                gains_own.at[:, pl.ds(pl.multiple_of(others[k] * columns, columns), columns)],
                gains_got.at[ranks - k - 1],
                "dp",
                others[k],
                g_sends,
                g_recvs,
                ranks - k - 1,
            )
            copy.start()
            handed.append(copy)
        for k in far_first:
            copy = remote(low_ref, mine, "tensor", away[k], x_sends, x_recvs, peers - k - 1)
            copy.start()
            spread.append(copy)
        store.start()

    for index in range(pieces + half):
        if index == half:
            after_norm()
        for number in range(0, half):
            if 0 <= index - number < pieces:
                works[index - number].step(number)
        if 0 <= index - half < pieces:
            piece = index - half

            def emit(spot, start, count, value, piece=piece):
                place = pl.ds(pl.multiple_of(piece * size + start, count), count)
                sum_ref[place, :] = value[:, :wide]
                small_own[place, :] = value[:, wide:]

            works[piece].total(emit)
    for copy in handed:
        copy.wait_recv()
    gains = gains_own[:, pl.ds(pl.multiple_of(ring.me * columns, columns), columns)]
    for k in range(ranks - 1):
        gains = gains + gains_got[k]
    gains_part[...] = gains
    last = []
    for k in far_first:
        for source, target, out_sems, in_sems in (
            (gains_part, gains_z, h_sends, h_recvs),
            (small_own, small_got, s_sends, s_recvs),
        ):
            copy = remote(
                source, target.at[peers - k - 1], "tensor", away[k], out_sems, in_sems, peers - k - 1
            )
            copy.start()
            last.append(copy)
    store.wait()
    for copy in handed:
        copy.wait_send()
    for copy in spread + last:
        copy.wait()
    gains = gains_part[...]
    small = small_own[...]
    for k in range(peers - 1):
        gains = gains + gains_z[k]
        small = small + small_got[k]
    gains_ref[...] = gains
    small_ref[...] = small
    for work in works:
        work.finish()


def finish_grads(part, tokens, gain, grad, gain_grad, weights, ranks, peers, identity):
    half = ranks // 4
    chips = ranks // 2
    block, width = part.shape
    rows = block // peers
    lot = weights.shape[0] // ranks
    total = weights.shape[1]
    tail = 128
    pieces = 4
    size = lot // pieces
    columns = width // ranks
    vmem = pl.BlockSpec(memory_space=pltpu.VMEM)
    low = part.dtype
    dma = pltpu.SemaphoreType.DMA
    return pl.pallas_call(
        functools.partial(final_kernel, ranks, peers),
        out_shape=(
            jax.ShapeDtypeStruct((block, width), low),
            jax.ShapeDtypeStruct((lot, total - tail), jnp.float32),
            jax.ShapeDtypeStruct((lot, tail), jnp.float32),
            jax.ShapeDtypeStruct((8, columns), jnp.float32),
        ),
        in_specs=[vmem] * 6,
        out_specs=(pl.BlockSpec(memory_space=pl.ANY), vmem, vmem, vmem),
        scratch_shapes=[
            pltpu.VMEM((pieces, chips, size, total), low),
            pltpu.VMEM((pieces, chips, size, total), low),
            pltpu.VMEM((pieces, 2 * half, size, total), low),
            pltpu.VMEM((peers - 1, rows, width), low),
            pltpu.VMEM((rows, width), low),
            pltpu.VMEM((lot, tail), jnp.float32),
            pltpu.VMEM((peers - 1, lot, tail), jnp.float32),
            pltpu.VMEM((8, width), jnp.float32),
            pltpu.VMEM((ranks - 1, 8, columns), jnp.float32),
            pltpu.VMEM((8, columns), jnp.float32),
            pltpu.VMEM((peers - 1, 8, columns), jnp.float32),
            dma((pieces * 2 * half,)),
            dma((pieces * 2 * half,)),
            dma((pieces * chips,)),
            dma((pieces * chips,)),
            dma((peers - 1,)),
            dma((peers - 1,)),
            dma((peers - 1,)),
            dma((peers - 1,)),
            dma((peers - 1,)),
            dma((peers - 1,)),
            dma((ranks - 1,)),
            dma((ranks - 1,)),
            dma((peers - 1,)),
            dma((peers - 1,)),
            dma,
        ],
        compiler_params=pltpu.CompilerParams(
            collective_id=identity, has_side_effects=True, vmem_limit_bytes=50 << 20
        ),
        name="finish_grads",
    )(part, tokens, gain, grad, gain_grad, weights)


def dot_rows(left, right):
    return lax.dot_general(
        left, right, (((0,), (0,)), ((), ())), preferred_element_type=jnp.float32
    )


def dot_last(left, right):
    return lax.dot_general(
        left, right, (((1,), (1,)), ((), ())), preferred_element_type=jnp.float32
    )


def forward_rms_norm(values, gain):
    inverse = lax.rsqrt(jnp.mean(values * values, axis=-1, keepdims=True) + EPSILON)
    normed = values * inverse
    return (normed * gain, normed, inverse)


def rope_tables():
    half_dim = HEAD_DIM // 2
    exponent = jnp.arange(half_dim, dtype=jnp.float32) * (2.0 / HEAD_DIM)
    inverse_freq = jnp.exp(-exponent * jnp.log(jnp.float32(1000000.0)))
    angles = jnp.arange(SEQ, dtype=jnp.float32)[:, None] * inverse_freq[None, :]
    return (jnp.cos(angles), jnp.sin(angles))


def rotate(values, cosine, sine, sign):
    half_dim = values.shape[-1] // 2
    first = values[..., :half_dim]
    second = values[..., half_dim:]
    cos_table = cosine[:, None, :]
    sin_table = sine[:, None, :] * sign
    return jnp.concatenate(
        [first * cos_table - second * sin_table, second * cos_table + first * sin_table], axis=-1
    )


def masked_scores(queries, key_rows, segment_row):
    raw = jnp.einsum(
        "qhd,khd->hqk", queries, key_rows, preferred_element_type=jnp.float32
    ) * HEAD_DIM ** (-0.5)
    spots = jnp.arange(segment_row.shape[0], dtype=jnp.int32)
    allowed = (spots[None, :] <= spots[:, None]) & (segment_row[None, :] == segment_row[:, None])
    return jnp.where(allowed[None], raw, -1e30)


def attend_forward(inputs):
    queries, key_rows, value_rows, segment_row = inputs
    scores = masked_scores(queries, key_rows, segment_row)
    exponent = jnp.exp(scores)
    totals = jnp.sum(exponent, axis=-1, keepdims=True)
    probs = (exponent / totals).astype(jnp.bfloat16)
    context = jnp.einsum(
        "hqk,khd->qhd", probs, value_rows, preferred_element_type=jnp.float32
    ).astype(jnp.bfloat16)
    return (context, jnp.log(totals[..., 0]))


def attend_backward(inputs):
    queries, key_rows, value_rows, segment_row, log_total, grad_context = inputs
    scores = masked_scores(queries, key_rows, segment_row)
    probs = jnp.exp(scores - log_total[..., None])
    probs_low = probs.astype(jnp.bfloat16)
    grad_probs = jnp.einsum(
        "qhd,khd->hqk", grad_context, value_rows, preferred_element_type=jnp.float32
    )
    inner = jnp.sum(probs * grad_probs, axis=-1, keepdims=True)
    grad_scores = (probs * (grad_probs - inner)).astype(jnp.bfloat16)
    grad_queries = jnp.einsum(
        "hqk,khd->qhd", grad_scores, key_rows, preferred_element_type=jnp.float32
    ) * HEAD_DIM ** (-0.5)
    grad_keys = jnp.einsum(
        "hqk,qhd->khd", grad_scores, queries, preferred_element_type=jnp.float32
    ) * HEAD_DIM ** (-0.5)
    grad_values = jnp.einsum(
        "hqk,qhd->khd", probs_low, grad_context, preferred_element_type=jnp.float32
    )
    return (grad_queries, grad_keys, grad_values)


def pad_columns(parts, width):
    rows = parts[0].shape[0]
    used = sum(part.shape[1] for part in parts)
    if used < width:
        parts = list(parts) + [jnp.zeros((rows, width - used), parts[0].dtype)]
    return jnp.concatenate(parts, axis=1)


def lanes(count):
    return -(-count // 128) * 128


def gather_rows(values):
    return lax.all_gather(values, "dp", axis=0, tiled=True)


def scatter_rows(values):
    return lax.psum_scatter(values, "dp", scatter_dimension=0, tiled=True)


def spread_columns(values, ranks):
    rows, columns = values.shape
    blocks = values.reshape(rows, ranks, columns // ranks).transpose(1, 0, 2)
    return blocks


def shards(
    tokens,
    w_query,
    w_key,
    w_value,
    w_out,
    gain_attn,
    gain_ffn,
    w_router,
    shared_gate,
    shared_up,
    shared_down,
    shared_switch,
    expert_gate,
    expert_up_weight,
    expert_down,
    routes,
    segments,
    cotangent,
):
    low = jnp.bfloat16
    ranks = lax.axis_size("dp")
    peers = lax.axis_size("tensor")
    me = lax.axis_index("dp")
    token_count, width = tokens.shape
    local_experts, _, expert_hidden = expert_gate.shape
    expert_count = local_experts * ranks
    block = width // ranks
    head_width = w_query.shape[1]
    head_count = head_width // HEAD_DIM
    row_count = token_count // SEQ
    shared_width = shared_gate.shape[1]
    shared_own = shared_width // ranks
    hidden = local_experts * expert_hidden + shared_own
    hidden_pad = lanes(hidden)
    small_pad = 128
    shape_four = (row_count, SEQ, head_count, HEAD_DIM)

    small = pad_columns(
        [w_router, shared_switch[:, None], gain_attn[:, None], gain_ffn[:, None]], small_pad
    )
    gathered = gather_dp([w_query, w_key, w_value, small, w_out.T], ranks, 0)
    qkv_full = gathered[:, : 3 * head_width]
    small_full = gathered[:, 3 * head_width : 3 * head_width + small_pad]
    out_rows = gathered[:, 3 * head_width + small_pad :]
    attn_gain = small_full[:, expert_count + 1].astype(jnp.float32)
    ffn_gain = small_full[:, expert_count + 2].astype(jnp.float32)
    router_columns = jnp.where(
        jnp.arange(small_pad)[None, :] <= expert_count, small_full, jnp.zeros_like(small_full)
    )

    packed = jnp.concatenate(
        [
            spread_columns(shared_gate, ranks),
            spread_columns(shared_up, ranks),
            spread_columns(shared_down.T, ranks),
        ],
        axis=2,
    )
    shared_mine = lax.all_to_all(packed, "dp", split_axis=0, concat_axis=0, tiled=True)
    shared_mine = shared_mine.reshape(width, 3 * shared_own)
    gate_own = shared_mine[:, :shared_own]
    up_own = shared_mine[:, shared_own : 2 * shared_own]
    down_own = shared_mine[:, 2 * shared_own :].T

    gates = pad_columns([expert_gate[j] for j in range(local_experts)] + [gate_own], hidden_pad)
    ups = pad_columns([expert_up_weight[j] for j in range(local_experts)] + [up_own], hidden_pad)
    wide = jnp.concatenate([gates, ups, router_columns], axis=1)
    downs = jnp.concatenate(
        [expert_down[j] for j in range(local_experts)]
        + [down_own, jnp.zeros((hidden_pad - hidden, width), low)],
        axis=0,
    )

    chosen = jnp.sum(
        (routes[:, :, None] == jnp.arange(small_pad, dtype=jnp.int32)[None, None, :]).astype(jnp.float32),
        axis=1,
    ).astype(low)
    cot_chosen = gather_rows(jnp.concatenate([cotangent, chosen], axis=1))
    cot_all = cot_chosen[:, :width]
    chosen_all = cot_chosen[:, width:].astype(jnp.float32)

    cosine, sine = rope_tables()
    inputs = tokens.astype(jnp.float32)
    attn_pre, _, _ = forward_rms_norm(inputs, attn_gain)
    attn_in = attn_pre.astype(low)
    qkv = jnp.dot(attn_in, qkv_full, preferred_element_type=jnp.float32)
    queries = rotate(qkv[:, :head_width].reshape(shape_four), cosine, sine, 1.0).astype(low)
    key_rows = rotate(
        qkv[:, head_width : 2 * head_width].reshape(shape_four), cosine, sine, 1.0
    ).astype(low)
    value_rows = qkv[:, 2 * head_width :].astype(low).reshape(shape_four)
    contexts, log_totals = jax.vmap(attend_forward)((queries, key_rows, value_rows, segments))
    context_flat = contexts.reshape(token_count, head_width)
    attn_part = dot_last(context_flat, out_rows)
    x_all, middle = middle_and_gather(
        attn_part.astype(low), tokens, ffn_gain[None, :], ranks, peers, 1
    )

    pre = jnp.dot(x_all, wide, preferred_element_type=jnp.float32)
    pre_gate = pre[:, :hidden_pad]
    pre_up = pre[:, hidden_pad : 2 * hidden_pad]
    pre_small = pre[:, 2 * hidden_pad :]
    column = jnp.arange(small_pad, dtype=jnp.int32)[None, :]
    exponent = jnp.where(column < expert_count, jnp.exp(jnp.where(column < expert_count, pre_small, 0.0)), 0.0)
    router_probs = exponent / jnp.sum(exponent, axis=-1, keepdims=True)
    switch = lax.logistic(jnp.sum(jnp.where(column == expert_count, pre_small, 0.0), axis=-1, keepdims=True))
    weights, spots = [], []
    for j in range(local_experts):
        spot = column == me * local_experts + j
        spots.append(spot)
        weights.append(jnp.sum(jnp.where(spot, router_probs * chosen_all, 0.0), axis=-1, keepdims=True))
    unit = jnp.arange(hidden_pad, dtype=jnp.int32)[None, :]
    scale = switch
    for j in reversed(range(local_experts)):
        scale = jnp.where(unit < (j + 1) * expert_hidden, weights[j], scale)
    sig = lax.logistic(pre_gate)
    act = pre_gate * sig
    hidden_state = (act * pre_up).astype(low)
    scaled_hidden = (scale * (act * pre_up)).astype(low)
    out_part = jnp.dot(scaled_hidden, downs, preferred_element_type=jnp.float32).astype(low)
    moe = lax.psum_scatter(scatter_rows(out_part), "tensor", scatter_dimension=0, tiled=True)
    output = (middle + moe.astype(jnp.float32)).astype(low)
    output = lax.all_gather(output, "tensor", axis=0, tiled=True)

    cot_hidden = dot_last(cot_all, downs)
    products = hidden_state.astype(jnp.float32) * cot_hidden
    grad_hidden = scale * cot_hidden
    grad_gate = (grad_hidden * pre_up * sig * (1.0 + pre_gate * (1.0 - sig))).astype(low)
    grad_up = (grad_hidden * act).astype(low)
    grad_choice = jnp.zeros_like(router_probs)
    for j in range(local_experts):
        inside = (unit >= j * expert_hidden) & (unit < (j + 1) * expert_hidden)
        total = jnp.sum(jnp.where(inside, products, 0.0), axis=-1, keepdims=True)
        grad_choice = grad_choice + jnp.where(spots[j], chosen_all * total, 0.0)
    switch_total = jnp.sum(
        jnp.where(unit >= local_experts * expert_hidden, products, 0.0), axis=-1, keepdims=True
    )
    grad_logits = router_probs * (
        grad_choice - jnp.sum(router_probs * grad_choice, axis=-1, keepdims=True)
    )
    grad_small = jnp.where(
        column == expert_count, switch_total * switch * (1.0 - switch), grad_logits
    ).astype(low)
    grads_wide = jnp.concatenate([grad_gate, grad_up, grad_small], axis=1)
    back_part = dot_last(grads_wide, wide).astype(low)
    grad_attn_out, grad_middle, grad_gain_ffn = reduce_and_norm(
        back_part, middle, cotangent, ffn_gain[None, :], ranks, peers, 2
    )

    grad_wide = dot_rows(x_all, grads_wide)
    grad_downs = dot_rows(scaled_hidden, cot_all)
    grad_expert_gate = jnp.stack(
        [grad_wide[:, j * expert_hidden : (j + 1) * expert_hidden] for j in range(local_experts)]
    )
    grad_expert_up = jnp.stack(
        [
            grad_wide[:, hidden_pad + j * expert_hidden : hidden_pad + (j + 1) * expert_hidden]
            for j in range(local_experts)
        ]
    )
    grad_expert_down = grad_downs[: local_experts * expert_hidden].reshape(
        local_experts, expert_hidden, width
    )
    first = local_experts * expert_hidden
    grad_shared = jnp.concatenate(
        [
            grad_wide[:, first : first + shared_own].astype(low),
            grad_wide[:, hidden_pad + first : hidden_pad + first + shared_own].astype(low),
            grad_downs[first : first + shared_own].astype(low).T,
        ],
        axis=1,
    ).reshape(ranks, block, 3 * shared_own)
    grad_shared = lax.all_to_all(grad_shared, "dp", split_axis=0, concat_axis=0, tiled=True)

    def whole_columns(part):
        return part.transpose(1, 0, 2).reshape(block, shared_width)

    grad_shared_gate = whole_columns(grad_shared[:, :, :shared_own]).astype(jnp.float32)
    grad_shared_up = whole_columns(grad_shared[:, :, shared_own : 2 * shared_own]).astype(jnp.float32)
    grad_shared_down = whole_columns(grad_shared[:, :, 2 * shared_own :]).T.astype(jnp.float32)

    grad_out_rows = dot_rows(grad_attn_out, context_flat)
    grad_context = jnp.dot(grad_attn_out, out_rows, preferred_element_type=jnp.float32)
    grad_context = grad_context.astype(low).reshape(shape_four)
    grad_queries, grad_keys, grad_values = jax.vmap(attend_backward)(
        (queries, key_rows, value_rows, segments, log_totals, grad_context)
    )
    flat_shape = (token_count, head_width)
    grad_qkv_rows = jnp.concatenate(
        [
            rotate(grad_queries, cosine, sine, -1.0).reshape(flat_shape).astype(low),
            rotate(grad_keys, cosine, sine, -1.0).reshape(flat_shape).astype(low),
            grad_values.reshape(flat_shape).astype(low),
        ],
        axis=1,
    )
    grad_qkv = dot_rows(attn_in, grad_qkv_rows)
    attn_back_part = dot_last(grad_qkv_rows, qkv_full)
    grad_weights = jnp.concatenate(
        [grad_qkv.astype(low), grad_out_rows.astype(low), grad_wide[:, 2 * hidden_pad :].astype(low)],
        axis=1,
    )
    grad_input, grad_four, grad_tail, grad_gains = finish_grads(
        attn_back_part.astype(low),
        tokens,
        attn_gain[None, :],
        grad_middle,
        grad_gain_ffn,
        grad_weights,
        ranks,
        peers,
        3,
    )
    grad_input = grad_input.astype(jnp.float32)
    grad_query = grad_four[:, :head_width]
    grad_key = grad_four[:, head_width : 2 * head_width]
    grad_value = grad_four[:, 2 * head_width : 3 * head_width]
    grad_out_proj = grad_four[:, 3 * head_width :].T
    return (
        output,
        grad_input,
        grad_query,
        grad_key,
        grad_value,
        grad_out_proj,
        grad_gains[0],
        grad_gains[1],
        grad_tail[:, :expert_count],
        grad_shared_gate,
        grad_shared_up,
        grad_shared_down,
        grad_tail[:, expert_count],
        grad_expert_gate,
        grad_expert_up,
        grad_expert_down,
    )


def solution(mesh):
    in_specs = (
        P("dp", None),
        P("dp", "tensor"),
        P("dp", "tensor"),
        P("dp", "tensor"),
        P("tensor", "dp"),
        P("dp"),
        P("dp"),
        P("dp", None),
        P("dp", "tensor"),
        P("dp", "tensor"),
        P("tensor", "dp"),
        P("dp"),
        P("dp", None, "tensor"),
        P("dp", None, "tensor"),
        P("dp", "tensor", None),
        P("dp", None),
        P("dp", None),
        P("dp", None),
    )
    out_specs = (
        P("dp", None),
        P("dp", None),
        P("dp", "tensor"),
        P("dp", "tensor"),
        P("dp", "tensor"),
        P("tensor", "dp"),
        P("dp"),
        P("dp"),
        P("dp", None),
        P("dp", "tensor"),
        P("dp", "tensor"),
        P("tensor", "dp"),
        P("dp"),
        P("dp", None, "tensor"),
        P("dp", None, "tensor"),
        P("dp", "tensor", None),
    )
    return jax.shard_map(shards, mesh=mesh, in_specs=in_specs, out_specs=out_specs, check_vma=False)
```

time: 1500 us -> 661 us (0.44)
  waiting for transfers between devices: 673 us -> 0.14 us
  Pallas kernels: 0 us -> 349 us
  blocking collectives: 335 us -> 0 us
  local copies, waits for them, and re-layouts: 204 us -> 88.9 us
  matrix products: 168 us -> 135 us
  other arithmetic: 76.3 us -> 55.7 us
    pallas_call x0 -> x4, Pallas kernels: none -> 349 us  [the longest x1 98.9 us: gather_dp(): pl.pallas_call(functools.partial(gather_kernel, ranks, counts), out_shape...]
    reduce_scatter x8 -> x2, waiting for transfers between devices: 286 us -> 0.04 us  [the longest x1 0.02 us: shards(): lax.psum_scatter(scatter_rows(out_part), 'tensor', scatter_dimension=0, t...]
    all_gather x4 -> x0, blocking collectives: 216 us -> none  [the longest x1 142 us: shards(): lax.all_gather(shared_switch, 'dp', axis=0, tiled=True)]
    psum x3 -> x0, waiting for transfers between devices: 202 us -> none  [the longest x1 86.7 us: shards(): lax.psum((routed + switch * shared_part).astype(jnp.bfloat16), 'tensor')]
    all_to_all x3 -> x2, waiting for transfers between devices: 94 us -> 0.01 us  [the longest x1 0.01 us: shards(): lax.all_to_all(packed, 'dp', split_axis=0, concat_axis=0, tiled=True)]
    all_gather x7 -> x2, waiting for transfers between devices: 86.8 us -> 0.02 us  [the longest x1 0.02 us: gather_rows(): return lax.all_gather(values, 'dp', axis=0, tiled=True)]
    all_to_all x1 -> x0, blocking collectives: 74.6 us -> none  [dispatch(): return lax.all_to_all(buffer, 'dp', split_axis=1, concat_axis=1, tiled=True)]
    dot_general x18 -> x4, matrix products: 108 us -> 39.6 us  [the longest x1 20.6 us: shards(): pre = jnp.dot(x_all, wide, preferred_element_type=jnp.float32)]
  transfers between devices with their start and end apart: 21 -> 6, of which waited for: 16 -> 0; matrix products, arithmetic and copies ran while one was open for 19% -> 32% of each run, Pallas kernels for 0% -> 53%
where the time goes in v1:
time: 661 us; the launch traced here: 653 us
  Pallas kernels  349 us (53%)
  matrix products  135 us (20%)
  local copies, waits for them, and re-layouts  88.9 us (13%)
  other arithmetic  55.7 us (8%)
  between operations  15.2 us (2%)
  starting transfers between devices  9.72 us (1%)
    pallas_call x1, Pallas kernels, gather_dp(): pl.pallas_call(functools.partial(gather_kernel, ranks, counts), out_shape...  98.9 us
    pallas_call x1, Pallas kernels, reduce_and_norm(): pl.pallas_call(functools.partial(back_kernel, ranks, peers), out_shape=(j...  91.8 us
    pallas_call x1, Pallas kernels, finish_grads(): pl.pallas_call(functools.partial(final_kernel, ranks, peers), out_shape=(...  81.6 us
    pallas_call x1, Pallas kernels, middle_and_gather(): pl.pallas_call(functools.partial(middle_kernel, ranks, peers), out_shape=...  76.6 us
    dot_general x4, matrix products, dot_last(): lax.dot_general(left, right, (((1,), (1,)), ((), ())), preferred_element_...  48.6 us
    dot_general x4, matrix products, dot_rows(): lax.dot_general(left, right, (((0,), (0,)), ((), ())), preferred_element_...  40.4 us
    unnamed x127, local copies, waits for them, and re-layouts  38.1 us
    dot_general x1, matrix products, shards(): pre = jnp.dot(x_all, wide, preferred_element_type=jnp.float32)  20.6 us
  transfers between devices with their start and end apart: 6, of which 0 were waited for; matrix products, arithmetic and copies ran while one was open for 32% of the time, Pallas kernels for 53%

profile of v1, /device:TPU:0, one launch (start us, length us, event | category | flops | bytes accessed | tf_op | source)
XLA Modules:
  0.0 653.2 jit_solution(14981085639796024626)
XLA Ops:
  8.4 1.5 copy.158
  9.8 1.1 pad_maximum_fusion.8
  11.0 1.4 copy.153
  12.7 1.5 pad_maximum_fusion.7
  14.2 5.2 all-to-all-start
  21.6 98.9 %gather_dp.1 = bf16[2048,2176]{1,0:T(8,128)(2,1)} custom-call(bf16[256,512]{1,0:T(8,128)(2,1)} %refs_0_.1, bf16[256,512]{1,0:T(8,128)(2,1)} %refs_1_.1, bf16[256,512]{1,0:T(8,128)(2,1)} %refs_2_.1, bf16[256,128]{1,0:T(8,128)(2,1)} %concatenate.59.refs_3_, bf16[256,512]{1,0:T(8,128)(2,1)} %bitcast.138), custom_call_target="tpu_custom_call" | custom-call | tf_op jit(solution)/shard_map/gather_dp/pallas_call | solution.py:175
  120.5 1.1 slice_select_fusion
  121.8 2.8 convert_reduce_fusion
  124.9 4.6 fusion.8
  129.6 1.1 copy-done.16
  131.2 1.2 broadcast_multiply_fusion
  135.1 1.4 convolution_convert_fusion.6
  137.3 3.3 convolution_convert_fusion.4.part_ref
  140.6 76.6 %middle_and_gather.1 = (bf16[2048,2048]{1,0:T(8,128)(2,1)}, f32[64,2048]{1,0:T(8,128)}) custom-call(bf16[256,2048]{1,0:T(8,128)(2,1)} %convolution_convert_fusion.4.part_ref, bf16[256,2048]{1,0:T(8,128)(2,1)} %tokens_ref.3, f32[1,2048]{1,0:T(1,128)} %bitcast.118), custom_call_target="tpu_custom_call" | custom-call | tf_op jit(solution)/shard_map/middle_and_gather/pallas_call | solution.py:323
  219.4 1.5 bitcast_dynamic-update-slice_fusion.3
  221.0 1.5 bitcast_dynamic-update-slice_fusion.2
  222.5 3.1 copy-done.34
  225.6 1.9 slice_bitcast_fusion.5
  227.5 2.0 copy.197
  231.1 1.2 bitcast_dynamic-update-slice_fusion.1
  232.3 1.2 bitcast_dynamic-update-slice_fusion
  233.6 1.2 slice_dynamic-update-slice_fusion
  236.2 20.6 %fusion.62 = f32[2048,1920]{0,1:T(8,128)S(1)} fusion(bf16[2048,2048]{1,0:T(8,128)(2,1)} %get-tuple-element.26, bf16[2048,1920]{0,1:T(8,128)(2,1)} %constant_dynamic-update-slice_fusion), kind=kOutput, calls=%fused_computation.157 | convolution fusion | flops 16106127360 | bytes 31981568 | tf_op jit(solution)/shard_map/dot_general | solution.py:1072
  256.8 5.4 copy-done.7
  262.6 19.4 %select_reduce_fusion.2 = (f32[2048]{0:T(1024)S(1)}, f32[2048]{0:T(1024)S(1)}, f32[2048]{0:T(1024)S(1)}, f32[2048,896]{0,1:T(8,128)}) fusion(pred[896]{0:T(1024)(128)(4,1)S(1)} %copy-done.46, pred[896]{0:T(1024)(128)(4,1)S(1)} %copy-done.50, pred[896]{0:T(1024)(128)(4,1)S(1)} %get-tuple-element.160, bf16[2048,2176]{0,1:T(8,128)(2,1)} %all-gather.3.cloned.1.call-done, ...), kind=kOutput, calls=%fused_computation.11 | convolution fusion | flops 7556556800 | bytes 34042240 | tf_op jit(solution)/shard_map/dot_general | solution.py:874
  282.0 2.4 multiply_reduce_fusion.1
  284.4 14.0 %multiply_convert_fusion.1 = (bf16[2048,896]{0,1:T(8,128)(2,1)}, bf16[2048,896]{0,1:T(8,128)(2,1)}, bf16[2048,896]{0,1:T(8,128)(2,1)S(1)}) fusion(f32[2048,1920]{0,1:T(8,128)} %copy-done.7, f32[2048,896]{0,1:T(8,128)} %get-tuple-element.154, f32[2048]{0:T(1024)S(1)} %add_divide_fusion.1, f32[2048]{0:T(1024)S(1)} %get-tuple-element.100, ...), kind=kLoop, calls=%fused_computation.14 | loop fusion | flops 34865152 | bytes 33056512 | tf_op jit(solution)/shard_map/convert_element_type | solution.py:1101
  298.4 1.8 copy-done.13
  300.2 11.4 %convolution_convert_fusion.2 = bf16[2048,2048]{1,0:T(8,128)(2,1)} fusion(bf16[2048,896]{0,1:T(8,128)(2,1)S(1)} %get-tuple-element.109, bf16[176,2048]{1,0:T(8,128)(2,1)S(1)} %copy-done.31, bf16[352,2048]{1,0:T(8,128)(2,1)S(1)} %copy-done.18, bf16[352,2048]{1,0:T(8,128)(2,1)S(1)} %copy-done.17, bf16[896]{0:T(1024)(128)(2,1)S(1)} %copy-done.44), kind=kOutput, calls=%fused_computation.4 | convolution fusion | flops 7535067136 | bytes 15664896 | tf_op jit(solution)/shard_map/dot_general | solution.py:1093
  311.7 2.2 select_convert_fusion
  313.9 24.0 %convolution_convert_fusion.1.part_ref = bf16[2048,2048]{1,0:T(8,128)(2,1)} fusion(bf16[2048,1920]{0,1:T(8,128)(2,1)} %constant_dynamic-update-slice_fusion, bf16[2048,128]{0,1:T(8,128)(2,1)S(1)} %select_convert_fusion, bf16[2048,896]{0,1:T(8,128)(2,1)} %get-tuple-element.108, bf16[2048,896]{0,1:T(8,128)(2,1)} %get-tuple-element.107), kind=kOutput, calls=%fused_computation.3 | convolution fusion | flops 16133914624 | bytes 24117248 | tf_op jit(solution)/shard_map/dot_general | solution.py:874
  337.9 91.8 %reduce_and_norm.1 = (bf16[256,2048]{1,0:T(8,128)(2,1)S(1)}, f32[64,2048]{1,0:T(8,128)S(1)}, f32[1,2048]{1,0:T(1,128)S(1)}) custom-call(bf16[2048,2048]{1,0:T(8,128)(2,1)} %convolution_convert_fusion.1.part_ref, f32[64,2048]{1,0:T(8,128)S(1)} %copy-done.3, bf16[256,2048]{1,0:T(8,128)(2,1)S(1)} %copy-done.2, f32[1,2048]{1,0:T(1,128)S(1)} %bitcast.119), custom_call_target="tpu_custom_call" | custom-call | tf_op jit(solution)/shard_map/reduce_and_norm/pallas_call | solution.py:589
  429.7 3.0 fusion.23
  432.7 1.1 copy.194
  433.9 1.4 multiply_reduce_fusion
  435.5 1.5 fusion.22
  437.5 1.2 subtract_convert_fusion.1
  439.5 1.8 copy.164
  441.3 11.3 %fusion = f32[896,2048]{1,0:T(8,128)S(1)} fusion(bf16[2048,896]{0,1:T(8,128)(2,1)} %copy-done.13, bf16[2048,2176]{0,1:T(8,128)(2,1)} %all-gather.3.cloned.1.call-done), kind=kOutput, calls=%fused_computation.5 | convolution fusion | flops 7516192768 | bytes 19398656 | tf_op jit(solution)/shard_map/dot_general | solution.py:868
  452.7 2.9 copy-done.11
  456.5 2.2 copy.195
  458.7 25.0 %fusion.10 = f32[2048,1920]{0,1:T(8,128)} fusion(bf16[2048,2048]{1,0:T(8,128)(2,1)} %get-tuple-element.26, bf16[2048,128]{0,1:T(8,128)(2,1)} %copy-done.32, bf16[2048,896]{0,1:T(8,128)(2,1)} %get-tuple-element.108, bf16[2048,896]{0,1:T(8,128)(2,1)} %get-tuple-element.107), kind=kOutput, calls=%fused_computation.28 | convolution fusion | flops 16129720320 | bytes 31981568 | tf_op jit(solution)/shard_map/dot_general | solution.py:868
  483.7 12.4 %copy.173 = bf16[2048,1920]{1,0:T(8,128)(2,1)} copy(f32[2048,1920]{0,1:T(8,128)} %fusion.10) | data formatting | bytes 23592960 | tf_op jit(solution)/shard_map/dot_general | solution.py:868
  496.1 1.0 convolution_convert_fusion.5
  497.2 2.9 fusion.57
  500.1 3.0 pad_maximum_fusion.6
  503.1 2.1 convolution_convert_fusion.3
  505.2 9.3 %slice_bitcast_fusion.1 = (f32[1,2048,352]{1,2,0:T(8,128)}, f32[1,2048,352]{1,2,0:T(8,128)}, f32[1,2048,352]{1,2,0:T(8,128)}, f32[1,2048,352]{1,2,0:T(8,128)}) fusion(f32[2048,1920]{0,1:T(8,128)} %fusion.10), kind=kLoop, calls=%fused_computation.31 | loop fusion | bytes 23068672 | tf_op jit(solution)/shard_map/stack | solution.py:1128
  514.9 4.4 copy.175
  519.3 4.4 all-to-all-start.1
  523.8 2.0 convolution_convert_fusion
  525.8 4.3 pad_maximum_fusion.weights_ref
  530.1 1.8 fusion.11.part_ref
  531.9 81.6 %finish_grads.1 = (bf16[256,2048]{1,0:T(8,128)(2,1)S(1)}, f32[256,2048]{1,0:T(8,128)}, f32[256,128]{1,0:T(8,128)S(1)}, f32[8,256]{1,0:T(8,128)S(1)}) custom-call(bf16[256,2048]{1,0:T(8,128)(2,1)S(1)} %fusion.11.part_ref, bf16[256,2048]{1,0:T(8,128)(2,1)S(1)} %copy-done.1, f32[1,2048]{1,0:T(1,128)S(1)} %bitcast.117, ...), custom_call_target="tpu_custom_call" | custom-call | tf_op jit(solution)/shard_map/finish_grads/pallas_call | solution.py:822
  613.5 1.7 add_convert_fusion.2
  615.3 2.7 slice_bitcast_fusion.7
  618.0 5.9 slice.237
  624.5 1.6 convert_element_type.219
  628.4 6.4 pad_maximum_fusion.3
  634.8 2.9 pad_maximum_fusion.2
  637.7 3.2 slice_convert_fusion
  640.9 1.5 copy.179
  642.4 1.5 copy.178
  643.9 2.3 copy.241
  (167 shorter events, 19.7 us)
Async XLA Ops:
  7.2 5.2 copy-start.29
  7.2 5.5 copy-start.30
  7.2 255.3 %all-gather.3.cloned.1.call-start = ((), (), s32[]{:S(2)}) async-start(), calls=%async_computation.4 | async-start | bytes 10027008 | tf_op jit(solution)/shard_map/all_gather | solution.py:960
  10.9 8.5 %copy-start.47 = (bf16[256]{0:T(256)(128)(2,1)S(1)}, bf16[256]{0:T(256)(128)(2,1)}, u32[]{:S(2)}) copy-start(bf16[256]{0:T(256)(128)(2,1)} %param.23) | copy-start | bytes 1540
  10.9 8.6 %copy-start.48 = (bf16[256]{0:T(256)(128)(2,1)S(1)}, bf16[256]{0:T(256)(128)(2,1)}, u32[]{:S(2)}) copy-start(bf16[256]{0:T(256)(128)(2,1)} %param.24) | copy-start | bytes 1540
  10.9 8.8 %copy-start.40 = (bf16[256,16]{0,1:T(8,128)(2,1)S(1)}, bf16[256,16]{0,1:T(8,128)(2,1)}, u32[]{:S(2)}) copy-start(bf16[256,16]{0,1:T(8,128)(2,1)} %param.25) | copy-start | bytes 24580
  10.9 8.9 %copy-start.49 = (bf16[256]{0:T(256)(128)(2,1)S(1)}, bf16[256]{0:T(256)(128)(2,1)}, u32[]{:S(2)}) copy-start(bf16[256]{0:T(256)(128)(2,1)} %param.29) | copy-start | bytes 1540
  10.9 9.0 %copy-start.35 = (bf16[512,256]{1,0:T(8,128)(2,1)S(1)}, bf16[512,256]{1,0:T(8,128)(2,1)}, u32[]{:S(2)}) copy-start(bf16[512,256]{1,0:T(8,128)(2,1)} %param.22) | copy-start | bytes 786436
  14.2 213.3 %all-to-all-start = ((bf16[8,256,528]{1,2,0:T(8,128)(2,1)}), bf16[8,256,528]{1,2,0:T(8,128)(2,1)}, u32[]{:S(2)}, u32[]{:S(2)}) async-start(bf16[8,256,528]{1,2,0:T(8,128)(2,1)} %pad_maximum_fusion.7), calls=%async_computation | async-start | bytes 4325376 | tf_op jit(solution)/shard_map/all_to_all | solution.py:1032
  19.4 495.1 %reduce-scatter.3.cloned.1.call-start = ((), (), s32[]{:S(2)}) async-start(), calls=%async_computation.5 | async-start | bytes 9437184 | tf_op jit(solution)/shard_map/reduce_scatter | solution.py:964
  21.6 103.0 %copy-start = (bf16[256,2048]{1,0:T(8,128)(2,1)S(1)}, bf16[256,2048]{1,0:T(8,128)(2,1)}, u32[]{:S(2)}) copy-start(bf16[256,2048]{1,0:T(8,128)(2,1)} %tokens_ref.3) | copy-start | bytes 3145732
  124.5 4.9 copy-start.4
  124.8 4.7 copy-start.38
  124.9 6.2 copy-start.41
  129.5 1.1 copy-start.16
  133.2 0.7 copy-start.28
  133.2 87.7 %copy-start.23 = (bf16[256,4,64]{2,0,1:T(8,128)(2,1)}, bf16[256,4,64]{2,0,1:T(8,128)(2,1)S(1)}, u32[]{:S(2)}) copy-start(bf16[256,4,64]{2,0,1:T(8,128)(2,1)S(1)} %get-tuple-element.129) | copy-start | bytes 393220
  133.2 87.7 %copy-start.25 = (bf16[256,4,64]{2,0,1:T(8,128)(2,1)}, bf16[256,4,64]{2,0,1:T(8,128)(2,1)S(1)}, u32[]{:S(2)}) copy-start(bf16[256,4,64]{2,0,1:T(8,128)(2,1)S(1)} %get-tuple-element.130) | copy-start | bytes 393220
  133.2 87.7 %copy-start.27 = (bf16[256,4,64]{2,0,1:T(8,128)(2,1)}, bf16[256,4,64]{2,0,1:T(8,128)(2,1)S(1)}, u32[]{:S(2)}) copy-start(bf16[256,4,64]{2,0,1:T(8,128)(2,1)S(1)} %get-tuple-element.143) | copy-start | bytes 393220
  136.5 0.7 copy-start.36
  217.2 8.4 %copy-start.14 = (bf16[2,352,2048]{2,1,0:T(8,128)(2,1)S(1)}, bf16[2,352,2048]{2,1,0:T(8,128)(2,1)}, u32[]{:S(2)}) copy-start(bf16[2,352,2048]{2,1,0:T(8,128)(2,1)} %param.32) | copy-start | bytes 8650756
  222.5 3.1 copy-start.34
  227.5 3.6 copy-start.15
  236.2 26.3 %copy-start.17 = (bf16[352,2048]{1,0:T(8,128)(2,1)S(1)}, bf16[352,2048]{1,0:T(8,128)(2,1)}, u32[]{:S(2)}) copy-start(bf16[352,2048]{1,0:T(8,128)(2,1)} %get-tuple-element.116) | copy-start | bytes 4325380
  236.2 26.3 %copy-start.44 = (bf16[896]{0:T(1024)(128)(2,1)S(1)}, bf16[896]{0:T(1024)(128)(2,1)}, u32[]{:S(2)}) copy-start(bf16[896]{0:T(1024)(128)(2,1)} %pad.23.clone) | copy-start | bytes 5380
  236.2 26.3 %copy-start.46 = (pred[896]{0:T(1024)(128)(4,1)S(1)}, pred[896]{0:T(1024)(128)(4,1)}, u32[]{:S(2)}) copy-start(pred[896]{0:T(1024)(128)(4,1)} %get-tuple-element.159) | copy-start | bytes 2692
  236.2 26.3 %copy-start.50 = (pred[896]{0:T(1024)(128)(4,1)S(1)}, pred[896]{0:T(1024)(128)(4,1)}, u32[]{:S(2)}) copy-start(pred[896]{0:T(1024)(128)(4,1)} %fusion.49) | copy-start | bytes 2692
  256.8 5.4 copy-start.7
  262.6 19.4 %copy-start.42 = (pred[128]{0:T(512)(128)(4,1)S(1)}, pred[128]{0:T(512)(128)(4,1)}, u32[]{:S(2)}) copy-start(pred[128]{0:T(512)(128)(4,1)} %get-tuple-element.161) | copy-start | bytes 388
  262.6 19.4 %copy-start.43 = (pred[128]{0:T(512)(128)(4,1)S(1)}, pred[128]{0:T(512)(128)(4,1)}, u32[]{:S(2)}) copy-start(pred[128]{0:T(512)(128)(4,1)} %get-tuple-element.162) | copy-start | bytes 388
  262.6 21.8 %copy-start.45 = (pred[896]{0:T(1024)(128)(4,1)S(1)}, pred[896]{0:T(1024)(128)(4,1)}, u32[]{:S(2)}) copy-start(pred[896]{0:T(1024)(128)(4,1)} %iota_compare_fusion.4) | copy-start | bytes 2692
  284.4 15.9 %copy-start.18 = (bf16[352,2048]{1,0:T(8,128)(2,1)S(1)}, bf16[352,2048]{1,0:T(8,128)(2,1)}, u32[]{:S(2)}) copy-start(bf16[352,2048]{1,0:T(8,128)(2,1)} %get-tuple-element.117) | copy-start | bytes 4325380
  284.4 15.8 %copy-start.31 = (bf16[176,2048]{1,0:T(8,128)(2,1)S(1)}, bf16[176,2048]{1,0:T(8,128)(2,1)}, u32[]{:S(2)}) copy-start(bf16[176,2048]{1,0:T(8,128)(2,1)} %get-tuple-element.122) | copy-start | bytes 2162692
  298.4 1.8 copy-start.13
  311.6 301.9 %reduce-scatter.5.cloned.1.call-start = ((), (), s32[]{:S(2)}) async-start(), calls=%async_computation.6 | async-start | bytes 1310720 | tf_op jit(solution)/shard_map/reduce_scatter | solution.py:1094
  313.9 24.1 %copy-start.32 = (bf16[2048,128]{0,1:T(8,128)(2,1)}, bf16[2048,128]{0,1:T(8,128)(2,1)S(1)}, u32[]{:S(2)}) copy-start(bf16[2048,128]{0,1:T(8,128)(2,1)S(1)} %select_convert_fusion) | copy-start | bytes 1572868
  313.9 24.0 %copy-start.2 = (bf16[256,2048]{1,0:T(8,128)(2,1)S(1)}, bf16[256,2048]{1,0:T(8,128)(2,1)}, u32[]{:S(2)}) copy-start(bf16[256,2048]{1,0:T(8,128)(2,1)} %cot_ref.1) | copy-start | bytes 3145732
  313.9 24.0 %copy-start.3 = (f32[64,2048]{1,0:T(8,128)S(1)}, f32[64,2048]{1,0:T(8,128)}, u32[]{:S(2)}) copy-start(f32[64,2048]{1,0:T(8,128)} %get-tuple-element.25.middle_ref) | copy-start | bytes 1572868
  313.9 24.0 %copy-start.6 = (f32[2048]{0:T(1024)S(1)}, f32[2048]{0:T(1024)}, u32[]{:S(2)}) copy-start(f32[2048]{0:T(1024)} %get-tuple-element.102) | copy-start | bytes 24580
  433.8 3.2 copy-start.24
  433.8 3.2 copy-start.26
  433.9 3.6 copy-start.33
  452.7 2.9 copy-start.11
  496.1 4.0 copy-start.12
  496.1 7.0 %copy-start.37 = (bf16[4,128,256]{2,1,0:T(8,128)(2,1)S(1)}, bf16[4,128,256]{2,1,0:T(8,128)(2,1)}, u32[]{:S(2)}) copy-start(bf16[4,128,256]{2,1,0:T(8,128)(2,1)} %copy-done.36) | copy-start | bytes 786436
  505.2 9.4 %copy-start.21 = (bf16[1,256,4,64]{3,1,2,0:T(8,128)(2,1)S(1)}, bf16[1,256,4,64]{3,1,2,0:T(8,128)(2,1)}, u32[]{:S(2)}) copy-start(bf16[1,256,4,64]{3,1,2,0:T(8,128)(2,1)} %get-tuple-element.141) | copy-start | bytes 393220
  505.2 9.4 %copy-start.22 = (bf16[1,256,4,64]{3,1,2,0:T(8,128)(2,1)S(1)}, bf16[1,256,4,64]{3,1,2,0:T(8,128)(2,1)}, u32[]{:S(2)}) copy-start(bf16[1,256,4,64]{3,1,2,0:T(8,128)(2,1)} %get-tuple-element.142) | copy-start | bytes 393220
  514.5 9.2 %copy-start.1 = (bf16[256,2048]{1,0:T(8,128)(2,1)S(1)}, bf16[256,2048]{1,0:T(8,128)(2,1)}, u32[]{:S(2)}) copy-start(bf16[256,2048]{1,0:T(8,128)(2,1)} %tokens_ref.3) | copy-start | bytes 3145732
  514.5 9.2 %copy-start.5 = (f32[2048]{0:T(1024)S(1)}, f32[2048]{0:T(1024)}, u32[]{:S(2)}) copy-start(f32[2048]{0:T(1024)} %copy-done.4) | copy-start | bytes 24580
  514.5 9.2 %copy-start.19 = (bf16[1,256,4,128]{1,3,2,0:T(8,128)(2,1)S(1)}, bf16[1,256,4,128]{1,3,2,0:T(8,128)(2,1)}, u32[]{:S(2)}) copy-start(bf16[1,256,4,128]{1,3,2,0:T(8,128)(2,1)} %copy.164) | copy-start | bytes 786436
  514.5 9.2 %copy-start.20 = (bf16[4,128,256]{2,1,0:T(8,128)(2,1)S(1)}, bf16[4,128,256]{2,1,0:T(8,128)(2,1)}, u32[]{:S(2)}) copy-start(bf16[4,128,256]{2,1,0:T(8,128)(2,1)} %convolution_convert_fusion.5) | copy-start | bytes 786436
  514.5 9.2 %copy-start.39 = (f32[256]{0:T(256)S(1)}, f32[256]{0:T(256)}, u32[]{:S(2)}) copy-start(f32[256]{0:T(256)} %copy-done.38) | copy-start | bytes 3076
  519.3 118.4 %all-to-all-start.1 = ((bf16[8,256,528]{1,2,0:T(8,128)(2,1)}), bf16[8,256,528]{1,2,0:T(8,128)(2,1)}, u32[]{:S(2)}, u32[]{:S(2)}) async-start(bf16[8,256,528]{1,2,0:T(8,128)(2,1)} %copy.175), calls=%async_computation.3 | async-start | bytes 4325376 | tf_op jit(solution)/shard_map/all_to_all | solution.py:1146
  523.6 2.1 slice-start
  523.6 120.3 %all-gather.5.cloned.1.call-start = ((), (), s32[]{:S(2)}) async-start(), calls=%async_computation.7 | async-start | bytes 1310720 | tf_op jit(solution)/shard_map/all_gather | solution.py:1096
  523.7 2.1 copy-start.10
  523.7 6.3 slice-start.1
  523.8 6.3 slice-start.2
  525.8 4.3 slice-start.3
  627.1 7.7 %copy-start.8 = (f32[1,2048,352]{1,2,0:T(8,128)S(1)}, f32[1,2048,352]{1,2,0:T(8,128)}, u32[]{:S(2)}) copy-start(f32[1,2048,352]{1,2,0:T(8,128)} %get-tuple-element.112) | copy-start | bytes 8650756
  627.1 7.7 %copy-start.9 = (f32[1,2048,352]{1,2,0:T(8,128)S(1)}, f32[1,2048,352]{1,2,0:T(8,128)}, u32[]{:S(2)}) copy-start(f32[1,2048,352]{1,2,0:T(8,128)} %get-tuple-element.113) | copy-start | bytes 8650756
Sparse Core Ops, SparseCore 0:
  11.1 105.1 all-gather.2
  311.8 98.2 reduce-scatter.2
  514.7 29.1 reduce-scatter.4
  615.4 27.1 all-gather.4

commit v2 on v1

--- a/solution.py
+++ b/solution.py
@@ -74,7 +74,7 @@
 
 
 def side_slots(half):
-    return 2 * half + 1
+    return 2 * half
 
 
 class RingGather:
@@ -83,58 +83,76 @@
         self.sends, self.recvs = sends, recvs
         self.side_sends, self.side_recvs = side_sends, side_recvs
         self.base, self.side_base = base, side_base
-        self.started, self.side_sizes = [], []
-
-    def hop(self, source, target, device, slot):
-        copy = remote(source, target, "dp", device, self.sends, self.recvs, self.base + slot)
-        copy.start()
-        self.started.append(copy)
-        return copy
-
-    def share(self, source, target, size):
-        slot = self.side_base + len(self.side_sizes)
-        copy = remote(source, target, "dp", self.ring.sibling, self.side_sends, self.side_recvs, slot)
-        copy.start()
-        self.started.append(copy)
-        self.side_sizes.append(size)
+        self.hops, self.sides = {}, 0
+
+    def hop_copy(self, source, target, device, slot):
+        return remote(source, target, "dp", device, self.sends, self.recvs, self.base + slot)
+
+    def side_copy(self, source, target, slot):
+        return remote(
+            source,
+            target,
+            "dp",
+            self.ring.sibling,
+            self.side_sends,
+            self.side_recvs,
+            self.side_base + slot,
+        )
+
+    def hop(self, source, target, device, slot, size):
+        self.hop_copy(source, target, device, slot).start()
+        self.hops[slot] = size
+
+    def share(self, source, target):
+        self.side_copy(source, target, self.sides).start()
+        self.sides += 1
 
     def begin(self, source):
         ring = self.ring
         target = self.place(ring.me, 0, self.rows)
-        ahead = self.hop(source, target, ring.ahead, 0)
-        behind = self.hop(source, target, ring.behind, ring.half)
-        self.share(source, target, self.rows)
-        self.last = (ahead, behind)
+        self.hop(source, target, ring.ahead, 0, self.rows)
+        self.hop(source, target, ring.behind, ring.half, self.rows)
+        self.share(source, target)
+
+    def wait_hop(self, slot):
+        block = self.place(self.ring.me, 0, self.hops[slot])
+        self.hop_copy(block, block, self.ring.ahead, slot).wait_recv()
 
     def step(self, number):
         ring = self.ring
-        following = []
         for which, sign in enumerate((-1, 1)):
             owner = ring.device(sign * number)
             onward = (ring.ahead, ring.behind)[which]
-            self.last[which].wait_recv()
+            self.wait_hop(which * ring.half + number - 1)
             if number < ring.half:
                 block = self.place(owner, 0, self.rows)
+                size = self.rows
+                part = block
                 if number == ring.half - 1:
-                    part = self.place(owner, (0, self.cut)[which], self.cut)
-                else:
-                    part = block
-                following.append(self.hop(part, part, onward, which * ring.half + number))
-                self.share(block, block, self.rows)
-            else:
-                part = self.place(owner, (0, self.cut)[which], self.cut)
-                self.share(part, part, self.cut)
-        self.last = following
+                    size = self.cut
+                    part = self.place(owner, (0, self.cut)[which], size)
+                self.hop(part, part, onward, which * ring.half + number, size)
+                self.share(block, block)
+        if number == ring.half:
+            block = self.place(ring.device(number), 0, self.rows)
+            self.share(block, block)
+
+    def wait_side(self, index):
+        block = self.place(self.ring.me, 0, self.rows)
+        self.side_copy(block, block, index).wait_recv()
+
+    def sent(self):
+        for slot, size in self.hops.items():
+            block = self.place(self.ring.me, 0, size)
+            self.hop_copy(block, block, self.ring.ahead, slot).wait_send()
+        for index in range(self.sides):
+            block = self.place(self.ring.me, 0, self.rows)
+            self.side_copy(block, block, index).wait_send()
 
     def finish(self):
-        ring = self.ring
-        for copy in self.started:
-            copy.wait_send()
-        for index, size in enumerate(self.side_sizes):
-            block = self.place(ring.me, 0, size)
-            remote(
-                block, block, "dp", ring.sibling, self.side_sends, self.side_recvs, self.side_base + index
-            ).wait_recv()
+        self.sent()
+        for index in range(self.sides):
+            self.wait_side(index)
 
 
 def gather_kernel(ranks, counts, *refs):
@@ -212,17 +230,173 @@
     lax.fori_loop(0, rows // strip, step, 0)
 
 
-def middle_kernel(
+def matmul(left, right):
+    return lax.dot_general(
+        left, right, (((1,), (0,)), ((), ())), preferred_element_type=jnp.float32
+    )
+
+
+def matmul_last(left, right):
+    return lax.dot_general(
+        left, right, (((1,), (1,)), ((), ())), preferred_element_type=jnp.float32
+    )
+
+
+def tiles(width, tile, body):
+    def step(index, carry):
+        body(pl.ds(pl.multiple_of(index * tile, tile), tile))
+        return carry
+
+    lax.fori_loop(0, width // tile, step, 0)
+
+
+class Layout:
+    def __init__(self, local_experts, expert_hidden, shared_own, expert_count):
+        self.local_experts = local_experts
+        self.expert_hidden = expert_hidden
+        self.shared_own = shared_own
+        self.expert_count = expert_count
+        self.part = -(-expert_hidden // 128) * 128
+        self.shared_at = local_experts * self.part
+        self.router_at = self.shared_at + shared_own
+        self.last = -(-(shared_own + expert_count + 1) // 128) * 128
+        self.hidden = self.shared_at + self.last
+        self.router_tile = self.router_at // 128 * 128
+        self.router_lane = self.router_at - self.router_tile
+        self.tile = 256 if self.hidden % 256 == 0 else 128
+
+
+def hidden_tiles(layout, x_ref, gates, ups, pre_gate, pre_up):
+    def body(spot):
+        pre_gate[:, spot] = matmul(x_ref[...], gates[:, spot])
+        pre_up[:, spot] = matmul(x_ref[...], ups[:, spot])
+
+    tiles(layout.hidden, layout.tile, body)
+
+
+def cot_tiles(layout, cot_ref, downs, cot_hidden):
+    def body(spot):
+        cot_hidden[:, spot] = matmul_last(cot_ref[...], downs[spot, :])
+
+    tiles(layout.hidden, layout.tile, body)
+
+
+def gate_strips(layout, first_expert, chosen, pre_gate, pre_up, cot_hidden, scaled, grads):
+    rows = pre_gate.shape[0]
+    count, lane0 = layout.expert_count, layout.router_lane
+    router = slice(layout.router_tile, layout.router_tile + 128)
+    bounds = [(j * layout.part, (j + 1) * layout.part) for j in range(layout.local_experts)]
+    bounds.append((layout.shared_at, layout.hidden))
+    low = scaled.dtype
+
+    def body(spot, start, size):
+        lane = lax.broadcasted_iota(jnp.int32, (size, 128), 1)
+        logits = pre_gate[spot, router]
+        is_router = (lane >= lane0) & (lane < lane0 + count)
+        is_switch = lane == lane0 + count
+        power = jnp.where(is_router, jnp.exp(jnp.where(is_router, logits, 0.0)), 0.0)
+        probs = power / jnp.sum(power, axis=-1, keepdims=True)
+        raw = jnp.sum(jnp.where(is_switch, logits, 0.0), axis=-1, keepdims=True)
+        switch = 1.0 / (1.0 + jnp.exp(-raw))
+        mask = chosen[spot, :].astype(jnp.float32)
+        scales = []
+        for j in range(layout.local_experts):
+            spotted = lane == lane0 + first_expert + j
+            scales.append(jnp.sum(jnp.where(spotted, probs * mask, 0.0), axis=-1, keepdims=True))
+        scales.append(switch)
+        totals = []
+        for (begin, end), scale in zip(bounds, scales):
+            shared = begin == layout.shared_at
+            columns = slice(begin, end)
+            gate, up = pre_gate[spot, columns], pre_up[spot, columns]
+            through = cot_hidden[spot, columns].astype(jnp.float32)
+            sig = 1.0 / (1.0 + jnp.exp(-gate))
+            act = gate * sig
+            state = act * up
+            grad = scale * through
+            totals.append(jnp.sum(state * through, axis=-1, keepdims=True))
+            scaled[spot, columns] = (scale * state).astype(low)
+            grad_gate = grad * up * sig * (1.0 + gate * (1.0 - sig))
+            grads[spot, columns] = grad_gate.astype(low)
+            grads[spot, layout.hidden + begin : layout.hidden + end] = (grad * act).astype(low)
+        choice = jnp.zeros_like(probs)
+        for j in range(layout.local_experts):
+            spotted = lane == lane0 + first_expert + j
+            choice = choice + jnp.where(spotted, mask * totals[j], 0.0)
+        small = probs * (choice - jnp.sum(probs * choice, axis=-1, keepdims=True))
+        small = jnp.where(is_switch, totals[-1] * switch * (1.0 - switch), small)
+        kept = grads[spot, router].astype(jnp.float32)
+        kept = jnp.where(is_router | is_switch, small, kept)
+        grads[spot, router] = kept.astype(low)
+
+    strips(rows, body)
+
+
+def out_tiles(width, scaled, downs, out):
+    def body(spot):
+        out[:, spot] = matmul(scaled[...], downs[:, spot]).astype(out.dtype)
+
+    tiles(width, 256, body)
+
+
+def back_tiles(layout, width, grads, gates, ups, back):
+    hidden = layout.hidden
+
+    def body(spot):
+        total = matmul_last(grads[:, :hidden], gates[spot, :])
+        total = total + matmul_last(grads[:, hidden:], ups[spot, :])
+        back[:, spot] = total.astype(back.dtype)
+
+    tiles(width, 256, body)
+
+
+def layer_kernel(
+    layout,
     ranks,
     peers,
     part_ref,
     tokens_ref,
     gain_ref,
-    all_ref,
+    cot_ref,
+    chosen_ref,
+    small_ref,
+    expert_gate_ref,
+    expert_up_ref,
+    expert_down_ref,
+    shared_in_ref,
+    shared_out_ref,
+    x_all,
+    cot_all,
     middle_ref,
+    scaled_ref,
+    grads_ref,
+    out_ref,
+    back_ref,
+    gates,
+    ups,
+    downs,
+    stage,
+    pair_got,
+    down_got,
     own,
     got,
+    x_block,
+    cot_block,
+    pre_gate,
+    pre_up,
+    cot_hidden,
+    scaled,
+    grads,
+    out,
+    back,
     local_sem,
+    stage_sem,
+    block_sem,
+    store_sem,
+    pair_sends,
+    pair_recvs,
+    down_sends,
+    down_recvs,
     z_sends,
     z_recvs,
     x_sends,
@@ -231,14 +405,24 @@
     recvs,
     side_sends,
     side_recvs,
+    c_sends,
+    c_recvs,
+    c_side_sends,
+    c_side_recvs,
 ):
     ring = Ring(ranks)
     here = lax.axis_index("tensor")
-    block = part_ref.shape[0]
+    block, width = part_ref.shape
     rows = block // peers
+    depth = width // ranks
+    half = ring.half
     away = [(here + k) % peers for k in range(peers)]
-    greet(ring.partners() + [{"tensor": away[k]} for k in range(1, peers)])
+    others = [(ring.me + k) % ranks for k in range(ranks)]
+    greet(
+        [{"dp": others[k]} for k in range(1, ranks)] + [{"tensor": away[k]} for k in range(1, peers)]
+    )
     order = near_first(peers)
+
     exchanged = []
     for k in reversed(order[1:]):
         copy = remote(
@@ -252,6 +436,73 @@
         )
         copy.start()
         exchanged.append(copy)
+
+    handed = []
+    for k in range(1, ranks):
+        for source, target, out_sems, in_sems in (
+            (shared_in_ref, pair_got, pair_sends, pair_recvs),
+            (shared_out_ref, down_got, down_sends, down_recvs),
+        ):
+            copy = remote(
+                source.at[others[k]], target.at[ring.me], "dp", others[k], out_sems, in_sems, ranks - k - 1
+            )
+            copy.start()
+            handed.append(copy)
+    kept = [
+        pltpu.make_async_copy(shared_in_ref.at[ring.me], pair_got.at[ring.me], local_sem.at[0]),
+        pltpu.make_async_copy(shared_out_ref.at[ring.me], down_got.at[ring.me], local_sem.at[1]),
+    ]
+    for copy in kept:
+        copy.start()
+
+    def cot_place(device, start, size):
+        return cot_all.at[pl.ds(device * block + start, size)]
+
+    cots = RingGather(
+        ring, cot_place, block, c_sends, c_recvs, c_side_sends, c_side_recvs, 0, 0
+    )
+    cots.begin(cot_ref)
+    kept_cot = pltpu.make_async_copy(cot_ref, cot_place(ring.me, 0, block), local_sem.at[2])
+    kept_cot.start()
+
+    low = gates.dtype
+    experts, hid = layout.local_experts, layout.expert_hidden
+    last = layout.hidden - layout.shared_at
+    loads = []
+    for j in range(experts):
+        load = pltpu.make_async_copy(
+            expert_down_ref.at[j], downs.at[pl.ds(j * layout.part, hid)], local_sem.at[4 + j]
+        )
+        load.start()
+        loads.append(load)
+        if layout.part > hid:
+            downs[j * layout.part + hid : (j + 1) * layout.part, :] = jnp.zeros(
+                (layout.part - hid, width), low
+            )
+    columns = [(gates, expert_gate_ref, j) for j in range(experts)]
+    columns += [(ups, expert_up_ref, j) for j in range(experts)]
+
+    def fetch(index):
+        return pltpu.make_async_copy(
+            columns[index][1].at[columns[index][2]], stage.at[index % 2], stage_sem.at[index % 2]
+        )
+
+    fetch(0).start()
+    for index, (target, _, j) in enumerate(columns):
+        fetch(index).wait()
+        if index + 1 < len(columns):
+            fetch(index + 1).start()
+
+        def lay(spot, start, size, index=index, target=target, j=j):
+            fill = jnp.zeros((size, layout.part - layout.part // 128 * 128 + 128), low)
+            if layout.part > hid:
+                target[spot, (j + 1) * layout.part - 128 : (j + 1) * layout.part] = fill[:, :128]
+            target[spot, j * layout.part : j * layout.part + hid] = stage[index % 2, spot, :]
+
+        strips(width, lay)
+    for load in loads:
+        load.wait()
+
     for copy in exchanged:
         copy.wait()
     first = here * rows
@@ -270,7 +521,7 @@
 
     def place_of(k):
         def place(device, start, size):
-            return all_ref.at[pl.ds(device * block + away[k] * rows + start, size)]
+            return x_all.at[pl.ds(device * block + away[k] * rows + start, size)]
 
         return place
 
@@ -280,70 +531,230 @@
         copy = remote(own, mine, "tensor", away[k], x_sends, x_recvs, peers - k - 1)
         copy.start()
         forwards.append(copy)
-    half = ring.half
-    works = []
-    for k in range(peers):
-        works.append(
-            RingGather(
-                ring,
-                place_of(k),
-                rows,
-                sends,
-                recvs,
-                side_sends,
-                side_recvs,
-                k * gather_slots(half),
-                k * side_slots(half),
+    works = [
+        RingGather(
+            ring,
+            place_of(k),
+            rows,
+            sends,
+            recvs,
+            side_sends,
+            side_recvs,
+            k * gather_slots(half),
+            k * side_slots(half),
+        )
+        for k in range(peers)
+    ]
+    works[0].begin(own)
+    store = pltpu.make_async_copy(own, mine, local_sem.at[3])
+    store.start()
+
+    for copy in kept:
+        copy.wait()
+    for copy in handed:
+        copy.wait_recv()
+    count, lane0 = layout.expert_count, layout.router_lane
+    units = layout.shared_own
+    for source in range(ranks):
+
+        def lay_own(spot, start, size, source=source):
+            there = pl.ds(pl.multiple_of(source * depth + start, size), size)
+            pair = pair_got[source, spot, :].astype(jnp.float32)
+            zero = jnp.zeros((size, last), low)
+            gates[there, layout.shared_at :] = zero
+            ups[there, layout.shared_at :] = zero
+            gates[there, layout.shared_at : layout.router_at] = pair[:, :units].astype(low)
+            ups[there, layout.shared_at : layout.router_at] = pair[:, units:].astype(low)
+            lane = lax.broadcasted_iota(jnp.int32, (size, 128), 1)
+            inside = (lane >= lane0) & (lane <= lane0 + count)
+            tile = slice(layout.router_tile, layout.router_tile + 128)
+            mixed = jnp.where(
+                inside, small_ref[there, :].astype(jnp.float32), gates[there, tile].astype(jnp.float32)
             )
+            gates[there, tile] = mixed.astype(low)
+
+        strips(depth, lay_own)
+        downs[layout.shared_at : layout.router_at, source * depth : (source + 1) * depth] = down_got[source]
+    downs[layout.router_at :, :] = jnp.zeros((layout.hidden - layout.router_at, width), low)
+
+    events, ready = [], 0
+
+    def begin(k):
+        spot = place_of(k)(ring.me, 0, rows)
+        remote(own, spot, "tensor", away[k], x_sends, x_recvs, k - 1).wait_recv()
+        works[k].begin(spot)
+
+    for index in range(1, peers + half):
+        if index < peers:
+            events.append(functools.partial(begin, order[index]))
+            ready = len(events)
+        for number in range(1, half + 1):
+            if 0 <= index - number < peers:
+                events.append(functools.partial(works[order[index - number]].step, number))
+        if index <= half:
+            events.append(functools.partial(cots.step, index))
+    for event in events[:ready]:
+        event()
+    late = events[ready:]
+    cuts = [len(late) * part // 4 for part in range(5)]
+    store.wait()
+    kept_cot.wait()
+    chip_rows = 2 * block
+    first_expert = ring.me * experts
+
+    def stores(spot):
+        return [
+            pltpu.make_async_copy(source, target.at[spot], store_sem.at[slot])
+            for slot, (source, target) in enumerate(
+                ((scaled, scaled_ref), (grads, grads_ref), (out, out_ref), (back, back_ref))
+            )
+        ]
+
+    def chip_step(turn, carry):
+        offset = (1 - 2 * (turn % 2)) * ((turn + 1) // 2)
+        spot = pl.ds(pl.multiple_of(ring.chip(offset) * chip_rows, chip_rows), chip_rows)
+
+        def run_late(part):
+            @pl.when(turn == 0)
+            def _():
+                for event in late[cuts[part] : cuts[part + 1]]:
+                    event()
+
+        cots.wait_side(turn)
+        load_cot = pltpu.make_async_copy(cot_all.at[spot], cot_block, block_sem.at[0])
+        load_cot.start()
+        for work in works:
+            work.wait_side(turn)
+        load_x = pltpu.make_async_copy(x_all.at[spot], x_block, block_sem.at[1])
+        load_x.start()
+        load_cot.wait()
+        cot_tiles(layout, cot_block, downs, cot_hidden)
+        load_x.wait()
+        run_late(0)
+        hidden_tiles(layout, x_block, gates, ups, pre_gate, pre_up)
+        run_late(1)
+        pending = stores(spot)
+
+        @pl.when(turn > 0)
+        def _():
+            pending[0].wait()
+            pending[1].wait()
+
+        gate_strips(
+            layout, first_expert, chosen_ref.at[spot], pre_gate, pre_up, cot_hidden, scaled, grads
         )
-    works[0].begin(own)
-    store = pltpu.make_async_copy(own, mine, local_sem)
-    store.start()
-    for index in range(len(order) + half):
-        if 0 < index < len(order):
-            k = order[index]
-            spot = place_of(k)(ring.me, 0, rows)
-            remote(own, spot, "tensor", away[k], x_sends, x_recvs, k - 1).wait_recv()
-            works[k].begin(spot)
-        for number in range(1, half + 1):
-            if 0 <= index - number < len(order):
-                works[order[index - number]].step(number)
-    store.wait()
-    for copy in forwards:
+        pending[0].start()
+        pending[1].start()
+        run_late(2)
+
+        @pl.when(turn > 0)
+        def _():
+            pending[2].wait()
+            pending[3].wait()
+
+        out_tiles(width, scaled, downs, out)
+        pending[2].start()
+        run_late(3)
+        back_tiles(layout, width, grads, gates, ups, back)
+        pending[3].start()
+        return carry
+
+    lax.fori_loop(0, ring.chips, chip_step, 0)
+    for copy in stores(pl.ds(0, chip_rows)):
+        copy.wait()
+    for copy in forwards + handed:
         copy.wait_send()
+    cots.sent()
     for work in works:
-        work.finish()
-
-
-def middle_and_gather(part, tokens, gain, ranks, peers, identity):
+        work.sent()
+
+
+def layer_forward_back(
+    layout,
+    part,
+    tokens,
+    gain,
+    cot,
+    chosen,
+    small,
+    expert_gate,
+    expert_up,
+    expert_down,
+    shared_in,
+    shared_out,
+    ranks,
+    peers,
+    identity,
+):
     half = ranks // 4
     block, width = part.shape
     rows = block // peers
+    total = ranks * block
+    depth = width // ranks
+    hidden = layout.hidden
+    chip = 2 * block
+    low = part.dtype
     vmem = pl.BlockSpec(memory_space=pltpu.VMEM)
+    hbm = pl.BlockSpec(memory_space=pl.ANY)
+    dma = pltpu.SemaphoreType.DMA
+    f32 = jnp.float32
     return pl.pallas_call(
-        functools.partial(middle_kernel, ranks, peers),
+        functools.partial(layer_kernel, layout, ranks, peers),
         out_shape=(
-            jax.ShapeDtypeStruct((ranks * block, width), part.dtype),
-            jax.ShapeDtypeStruct((rows, width), jnp.float32),
+            jax.ShapeDtypeStruct((total, width), low),
+            jax.ShapeDtypeStruct((total, width), low),
+            jax.ShapeDtypeStruct((rows, width), f32),
+            jax.ShapeDtypeStruct((total, hidden), low),
+            jax.ShapeDtypeStruct((total, 2 * hidden), low),
+            jax.ShapeDtypeStruct((total, width), low),
+            jax.ShapeDtypeStruct((total, width), low),
         ),
-        in_specs=[vmem, vmem, vmem],
-        out_specs=(pl.BlockSpec(memory_space=pl.ANY), vmem),
+        in_specs=[vmem] * 6 + [hbm] * 5,
+        out_specs=(hbm, hbm, vmem, hbm, hbm, hbm, hbm),
         scratch_shapes=[
-            pltpu.VMEM((rows, width), part.dtype),
-            pltpu.VMEM((peers - 1, rows, width), part.dtype),
-            pltpu.SemaphoreType.DMA,
-            pltpu.SemaphoreType.DMA((peers - 1,)),
-            pltpu.SemaphoreType.DMA((peers - 1,)),
-            pltpu.SemaphoreType.DMA((peers - 1,)),
-            pltpu.SemaphoreType.DMA((peers - 1,)),
-            pltpu.SemaphoreType.DMA((peers * gather_slots(half),)),
-            pltpu.SemaphoreType.DMA((peers * gather_slots(half),)),
-            pltpu.SemaphoreType.DMA((peers * side_slots(half),)),
-            pltpu.SemaphoreType.DMA((peers * side_slots(half),)),
+            pltpu.VMEM((width, hidden), low),
+            pltpu.VMEM((width, hidden), low),
+            pltpu.VMEM((hidden, width), low),
+            pltpu.VMEM((2, width, layout.expert_hidden), low),
+            pltpu.VMEM((ranks, depth, 2 * layout.shared_own), low),
+            pltpu.VMEM((ranks, layout.shared_own, depth), low),
+            pltpu.VMEM((rows, width), low),
+            pltpu.VMEM((peers - 1, rows, width), low),
+            pltpu.VMEM((chip, width), low),
+            pltpu.VMEM((chip, width), low),
+            pltpu.VMEM((chip, hidden), f32),
+            pltpu.VMEM((chip, hidden), f32),
+            pltpu.VMEM((chip, hidden), f32),
+            pltpu.VMEM((chip, hidden), low),
+            pltpu.VMEM((chip, 2 * hidden), low),
+            pltpu.VMEM((chip, width), low),
+            pltpu.VMEM((chip, width), low),
+            dma((4 + layout.local_experts,)),
+            dma((2,)),
+            dma((2,)),
+            dma((4,)),
+            dma((ranks - 1,)),
+            dma((ranks - 1,)),
+            dma((ranks - 1,)),
+            dma((ranks - 1,)),
+            dma((peers - 1,)),
+            dma((peers - 1,)),
+            dma((peers - 1,)),
+            dma((peers - 1,)),
+            dma((peers * gather_slots(half),)),
+            dma((peers * gather_slots(half),)),
+            dma((peers * side_slots(half),)),
+            dma((peers * side_slots(half),)),
+            dma((gather_slots(half),)),
+            dma((gather_slots(half),)),
+            dma((side_slots(half),)),
+            dma((side_slots(half),)),
         ],
-        compiler_params=pltpu.CompilerParams(collective_id=identity, has_side_effects=True),
-        name="middle_and_gather",
-    )(part, tokens, gain)
+        compiler_params=pltpu.CompilerParams(
+            collective_id=identity, has_side_effects=True, vmem_limit_bytes=60 << 20
+        ),
+        name="layer_forward_back",
+    )(part, tokens, gain, cot, chosen, small, expert_gate, expert_up, expert_down, shared_in, shared_out)
 
 
 class RingReduce:
@@ -952,14 +1363,6 @@
     return jnp.concatenate(parts, axis=1)
 
 
-def lanes(count):
-    return -(-count // 128) * 128
-
-
-def gather_rows(values):
-    return lax.all_gather(values, "dp", axis=0, tiled=True)
-
-
 def scatter_rows(values):
     return lax.psum_scatter(values, "dp", scatter_dimension=0, tiled=True)
 
@@ -1003,54 +1406,42 @@
     row_count = token_count // SEQ
     shared_width = shared_gate.shape[1]
     shared_own = shared_width // ranks
-    hidden = local_experts * expert_hidden + shared_own
-    hidden_pad = lanes(hidden)
     small_pad = 128
+    layout = Layout(local_experts, expert_hidden, shared_own, expert_count)
+    part_pad, shared_at, router_at = layout.part, layout.shared_at, layout.router_at
+    hidden_pad, lane0 = layout.hidden, layout.router_lane
     shape_four = (row_count, SEQ, head_count, HEAD_DIM)
 
-    small = pad_columns(
-        [w_router, shared_switch[:, None], gain_attn[:, None], gain_ffn[:, None]], small_pad
-    )
-    gathered = gather_dp([w_query, w_key, w_value, small, w_out.T], ranks, 0)
+    rest = jnp.zeros((block, small_pad - 2 - lane0 - expert_count - 1), low)
+    small = jnp.concatenate(
+        [
+            jnp.zeros((block, lane0), low),
+            w_router,
+            shared_switch[:, None],
+            rest,
+            gain_attn[:, None],
+            gain_ffn[:, None],
+        ],
+        axis=1,
+    )
+    spots = jnp.arange(small_pad, dtype=jnp.int32)[None, None, :] - lane0
+    chosen = jnp.sum((routes[:, :, None] == spots).astype(jnp.float32), axis=1).astype(low)
+    fold = token_count // block
+    chosen = chosen.reshape(fold, block, small_pad).transpose(1, 0, 2).reshape(block, fold * small_pad)
+    gathered = gather_dp([w_query, w_key, w_value, small, w_out.T, chosen], ranks, 0)
     qkv_full = gathered[:, : 3 * head_width]
     small_full = gathered[:, 3 * head_width : 3 * head_width + small_pad]
-    out_rows = gathered[:, 3 * head_width + small_pad :]
-    attn_gain = small_full[:, expert_count + 1].astype(jnp.float32)
-    ffn_gain = small_full[:, expert_count + 2].astype(jnp.float32)
-    router_columns = jnp.where(
-        jnp.arange(small_pad)[None, :] <= expert_count, small_full, jnp.zeros_like(small_full)
-    )
-
-    packed = jnp.concatenate(
-        [
-            spread_columns(shared_gate, ranks),
-            spread_columns(shared_up, ranks),
-            spread_columns(shared_down.T, ranks),
-        ],
-        axis=2,
-    )
-    shared_mine = lax.all_to_all(packed, "dp", split_axis=0, concat_axis=0, tiled=True)
-    shared_mine = shared_mine.reshape(width, 3 * shared_own)
-    gate_own = shared_mine[:, :shared_own]
-    up_own = shared_mine[:, shared_own : 2 * shared_own]
-    down_own = shared_mine[:, 2 * shared_own :].T
-
-    gates = pad_columns([expert_gate[j] for j in range(local_experts)] + [gate_own], hidden_pad)
-    ups = pad_columns([expert_up_weight[j] for j in range(local_experts)] + [up_own], hidden_pad)
-    wide = jnp.concatenate([gates, ups, router_columns], axis=1)
-    downs = jnp.concatenate(
-        [expert_down[j] for j in range(local_experts)]
-        + [down_own, jnp.zeros((hidden_pad - hidden, width), low)],
-        axis=0,
-    )
-
-    chosen = jnp.sum(
-        (routes[:, :, None] == jnp.arange(small_pad, dtype=jnp.int32)[None, None, :]).astype(jnp.float32),
-        axis=1,
-    ).astype(low)
-    cot_chosen = gather_rows(jnp.concatenate([cotangent, chosen], axis=1))
-    cot_all = cot_chosen[:, :width]
-    chosen_all = cot_chosen[:, width:].astype(jnp.float32)
+    out_rows = gathered[:, 3 * head_width + small_pad : 3 * head_width + small_pad + head_width]
+    chosen_all = gathered[:, 3 * head_width + small_pad + head_width :]
+    chosen_all = chosen_all.reshape(ranks, block, fold, small_pad).transpose(0, 2, 1, 3)
+    chosen_all = chosen_all.reshape(ranks * token_count, small_pad)
+    attn_gain = small_full[:, small_pad - 2].astype(jnp.float32)
+    ffn_gain = small_full[:, small_pad - 1].astype(jnp.float32)
+
+    shared_in = jnp.concatenate(
+        [spread_columns(shared_gate, ranks), spread_columns(shared_up, ranks)], axis=2
+    )
+    shared_out = shared_down.reshape(ranks, shared_own, block)
 
     cosine, sine = rope_tables()
     inputs = tokens.astype(jnp.float32)
@@ -1065,81 +1456,51 @@
     contexts, log_totals = jax.vmap(attend_forward)((queries, key_rows, value_rows, segments))
     context_flat = contexts.reshape(token_count, head_width)
     attn_part = dot_last(context_flat, out_rows)
-    x_all, middle = middle_and_gather(
-        attn_part.astype(low), tokens, ffn_gain[None, :], ranks, peers, 1
-    )
-
-    pre = jnp.dot(x_all, wide, preferred_element_type=jnp.float32)
-    pre_gate = pre[:, :hidden_pad]
-    pre_up = pre[:, hidden_pad : 2 * hidden_pad]
-    pre_small = pre[:, 2 * hidden_pad :]
-    column = jnp.arange(small_pad, dtype=jnp.int32)[None, :]
-    exponent = jnp.where(column < expert_count, jnp.exp(jnp.where(column < expert_count, pre_small, 0.0)), 0.0)
-    router_probs = exponent / jnp.sum(exponent, axis=-1, keepdims=True)
-    switch = lax.logistic(jnp.sum(jnp.where(column == expert_count, pre_small, 0.0), axis=-1, keepdims=True))
-    weights, spots = [], []
-    for j in range(local_experts):
-        spot = column == me * local_experts + j
-        spots.append(spot)
-        weights.append(jnp.sum(jnp.where(spot, router_probs * chosen_all, 0.0), axis=-1, keepdims=True))
-    unit = jnp.arange(hidden_pad, dtype=jnp.int32)[None, :]
-    scale = switch
-    for j in reversed(range(local_experts)):
-        scale = jnp.where(unit < (j + 1) * expert_hidden, weights[j], scale)
-    sig = lax.logistic(pre_gate)
-    act = pre_gate * sig
-    hidden_state = (act * pre_up).astype(low)
-    scaled_hidden = (scale * (act * pre_up)).astype(low)
-    out_part = jnp.dot(scaled_hidden, downs, preferred_element_type=jnp.float32).astype(low)
+    x_all, cot_all, middle, scaled_hidden, grads_wide, out_part, back_part = layer_forward_back(
+        layout,
+        attn_part.astype(low),
+        tokens,
+        ffn_gain[None, :],
+        cotangent,
+        chosen_all,
+        small_full,
+        expert_gate,
+        expert_up_weight,
+        expert_down,
+        shared_in,
+        shared_out,
+        ranks,
+        peers,
+        1,
+    )
+    grad_attn_out, grad_middle, grad_gain_ffn = reduce_and_norm(
+        back_part, middle, cotangent, ffn_gain[None, :], ranks, peers, 2
+    )
+
+    out_part, grad_attn_out = lax.optimization_barrier((out_part, grad_attn_out))
     moe = lax.psum_scatter(scatter_rows(out_part), "tensor", scatter_dimension=0, tiled=True)
     output = (middle + moe.astype(jnp.float32)).astype(low)
     output = lax.all_gather(output, "tensor", axis=0, tiled=True)
 
-    cot_hidden = dot_last(cot_all, downs)
-    products = hidden_state.astype(jnp.float32) * cot_hidden
-    grad_hidden = scale * cot_hidden
-    grad_gate = (grad_hidden * pre_up * sig * (1.0 + pre_gate * (1.0 - sig))).astype(low)
-    grad_up = (grad_hidden * act).astype(low)
-    grad_choice = jnp.zeros_like(router_probs)
-    for j in range(local_experts):
-        inside = (unit >= j * expert_hidden) & (unit < (j + 1) * expert_hidden)
-        total = jnp.sum(jnp.where(inside, products, 0.0), axis=-1, keepdims=True)
-        grad_choice = grad_choice + jnp.where(spots[j], chosen_all * total, 0.0)
-    switch_total = jnp.sum(
-        jnp.where(unit >= local_experts * expert_hidden, products, 0.0), axis=-1, keepdims=True
-    )
-    grad_logits = router_probs * (
-        grad_choice - jnp.sum(router_probs * grad_choice, axis=-1, keepdims=True)
-    )
-    grad_small = jnp.where(
-        column == expert_count, switch_total * switch * (1.0 - switch), grad_logits
-    ).astype(low)
-    grads_wide = jnp.concatenate([grad_gate, grad_up, grad_small], axis=1)
-    back_part = dot_last(grads_wide, wide).astype(low)
-    grad_attn_out, grad_middle, grad_gain_ffn = reduce_and_norm(
-        back_part, middle, cotangent, ffn_gain[None, :], ranks, peers, 2
-    )
-
     grad_wide = dot_rows(x_all, grads_wide)
     grad_downs = dot_rows(scaled_hidden, cot_all)
     grad_expert_gate = jnp.stack(
-        [grad_wide[:, j * expert_hidden : (j + 1) * expert_hidden] for j in range(local_experts)]
+        [grad_wide[:, j * part_pad : j * part_pad + expert_hidden] for j in range(local_experts)]
     )
     grad_expert_up = jnp.stack(
         [
-            grad_wide[:, hidden_pad + j * expert_hidden : hidden_pad + (j + 1) * expert_hidden]
+            grad_wide[:, hidden_pad + j * part_pad : hidden_pad + j * part_pad + expert_hidden]
             for j in range(local_experts)
         ]
     )
-    grad_expert_down = grad_downs[: local_experts * expert_hidden].reshape(
-        local_experts, expert_hidden, width
-    )
-    first = local_experts * expert_hidden
+    grad_expert_down = jnp.stack(
+        [grad_downs[j * part_pad : j * part_pad + expert_hidden] for j in range(local_experts)]
+    )
     grad_shared = jnp.concatenate(
         [
-            grad_wide[:, first : first + shared_own].astype(low),
-            grad_wide[:, hidden_pad + first : hidden_pad + first + shared_own].astype(low),
-            grad_downs[first : first + shared_own].astype(low).T,
+            grad_wide[:, shared_at : shared_at + shared_own].astype(low),
+            grad_wide[:, hidden_pad + shared_at : hidden_pad + shared_at + shared_own].astype(low),
+            grad_downs[shared_at : shared_at + shared_own].astype(low).T,
         ],
         axis=1,
     ).reshape(ranks, block, 3 * shared_own)
@@ -1170,7 +1531,7 @@
     grad_qkv = dot_rows(attn_in, grad_qkv_rows)
     attn_back_part = dot_last(grad_qkv_rows, qkv_full)
     grad_weights = jnp.concatenate(
-        [grad_qkv.astype(low), grad_out_rows.astype(low), grad_wide[:, 2 * hidden_pad :].astype(low)],
+        [grad_qkv.astype(low), grad_out_rows.astype(low), pad_columns([grad_wide[:, router_at : router_at + expert_count + 1].astype(low)], small_pad)],
         axis=1,
     )
     grad_input, grad_four, grad_tail, grad_gains = finish_grads(

time: 661 us -> 613 us (0.927)
  matrix products: 135 us -> 64.6 us
  Pallas kernels: 349 us -> 385 us
  other arithmetic: 55.7 us -> 34.1 us
  waiting for transfers between devices: 0.14 us -> 12.7 us
    pallas_call x1, Pallas kernels: 76.6 us -> 191 us  [layer_forward_back(): pl.pallas_call(functools.partial(layer_kernel, layout, ranks, peers), out...]
    pallas_call x1, Pallas kernels: 98.9 us -> 47.9 us  [gather_dp(): pl.pallas_call(functools.partial(gather_kernel, ranks, counts), out_shape...]
    dot_general x4 -> x2, matrix products: 48.6 us -> 8 us  [dot_last(): lax.dot_general(left, right, (((1,), (1,)), ((), ())), preferred_element_...]
    dot_general x2 -> x0, matrix products: 31.9 us -> none  [the longest x1 20.6 us: shards(): pre = jnp.dot(x_all, wide, preferred_element_type=jnp.float32)]
    pallas_call x1, Pallas kernels: 91.8 us -> 63.6 us  [reduce_and_norm(): pl.pallas_call(functools.partial(back_kernel, ranks, peers), out_shape=(j...]
    convert_element_type x3 -> x1, other arithmetic: 18.9 us -> 2.67 us  [shards(): ffn_gain = small_full[:, small_pad - 1].astype(jnp.float32)]
    all_gather x1, waiting for transfers between devices: 0.01 us -> 12.6 us  [shards(): output = lax.all_gather(output, 'tensor', axis=0, tiled=True)]
    concatenate x3 -> x2, local copies, waits for them, and re-layouts: 2.31 us -> 14.5 us  [the longest x1 13.7 us: shards(): jnp.concatenate([grad_qkv.astype(low), grad_out_rows.astype(low), pad_col...]
  transfers between devices with their start and end apart: 6 -> 4, of which waited for: 0 -> 1; matrix products, arithmetic and copies ran while one was open for 32% -> 24% of each run, Pallas kernels for 53% -> 14%
where the time goes in v2:
time: 613 us; the launch traced here: 607 us
  Pallas kernels  385 us (63%)
  local copies, waits for them, and re-layouts  90.8 us (15%)
  matrix products  64.6 us (11%)
  other arithmetic  34.1 us (6%)
  between operations  14.7 us (2%)
  waiting for transfers between devices  12.7 us (2%)
    pallas_call x1, Pallas kernels, layer_forward_back(): pl.pallas_call(functools.partial(layer_kernel, layout, ranks, peers), out...  191 us
    pallas_call x1, Pallas kernels, finish_grads(): pl.pallas_call(functools.partial(final_kernel, ranks, peers), out_shape=(...  81.9 us
    pallas_call x1, Pallas kernels, reduce_and_norm(): pl.pallas_call(functools.partial(back_kernel, ranks, peers), out_shape=(j...  63.6 us
    pallas_call x1, Pallas kernels, gather_dp(): pl.pallas_call(functools.partial(gather_kernel, ranks, counts), out_shape...  47.9 us
    dot_general x4, matrix products, dot_rows(): lax.dot_general(left, right, (((0,), (0,)), ((), ())), preferred_element_...  45.5 us
    unnamed x78, local copies, waits for them, and re-layouts  28.8 us
    dot_general x1, local copies, waits for them, and re-layouts, dot_rows(): lax.dot_general(left, right, (((0,), (0,)), ((), ())), preferred_element_...  14 us
    concatenate x1, local copies, waits for them, and re-layouts, shards(): jnp.concatenate([grad_qkv.astype(low), grad_out_rows.astype(low), pad_col...  13.7 us
  transfers between devices with their start and end apart: 4, of which 1 were waited for; matrix products, arithmetic and copies ran while one was open for 24% of the time, Pallas kernels for 14%

profile of v2, /device:TPU:0, one launch (start us, length us, event | category | flops | bytes accessed | tf_op | source)
XLA Modules:
  0.0 606.5 jit_solution(16713572961047044358)
XLA Ops:
  7.2 0.8 copy.103
  8.1 0.8 broadcast_in_dim.36
  8.8 0.8 broadcast_in_dim.37
  9.6 0.8 broadcast_in_dim.38
  10.3 1.8 copy.107
  12.1 1.5 convert_reduce_fusion.2.refs_5_
  13.7 0.8 concatenate.47.refs_3_
  14.5 47.9 %gather_dp.1 = bf16[2048,2304]{1,0:T(8,128)(2,1)} custom-call(bf16[256,512]{1,0:T(8,128)(2,1)} %refs_0_.1, bf16[256,512]{1,0:T(8,128)(2,1)} %refs_1_.1, bf16[256,512]{1,0:T(8,128)(2,1)} %refs_2_.1, bf16[256,128]{1,0:T(8,128)(2,1)} %concatenate.47.refs_3_, bf16[256,512]{1,0:T(8,128)(2,1)} %bitcast.116, bf16[256,128]{1,0:T(8,128)(2,1)} %convert_reduce_fusion.2.refs_5_), custom_call_target="tpu_custom_call" | custom-call | tf_op jit(solution)/shard_map/gather_dp/pallas_call | solution.py:193
  62.4 2.7 convert_reduce_fusion
  65.1 2.2 fusion.42
  67.6 4.6 fusion.2
  72.7 1.1 broadcast_multiply_fusion
  74.0 0.6 fusion.45
  74.9 0.5 exponential_reduce_fusion
  75.9 0.7 copy-done.25
  76.6 3.3 convolution_convert_fusion.2.part_ref
  80.0 5.1 copy.118.expert_gate_ref
  85.1 4.6 copy.119.expert_up_ref
  90.5 1.4 copy.114
  92.4 1.7 pad_maximum_fusion.4.shared_in_ref
  94.2 191.3 %layer_forward_back.1 = (bf16[2048,2048]{1,0:T(8,128)(2,1)}, bf16[2048,2048]{1,0:T(8,128)(2,1)}, f32[64,2048]{1,0:T(8,128)}, bf16[2048,1024]{1,0:T(8,128)(2,1)},...) custom-call(bf16[256,2048]{1,0:T(8,128)(2,1)} %convolution_convert_fusion.2.part_ref, ...), custom_call_target="tpu_custom_call" | custom-call | tf_op jit(solution)/shard_map/layer_forward_back/pallas_call | solution.py:701
  285.5 1.0 copy-done.3
  286.6 63.6 %reduce_and_norm.1 = (bf16[256,2048]{1,0:T(8,128)(2,1)S(1)}, f32[64,2048]{1,0:T(8,128)S(1)}, f32[1,2048]{1,0:T(1,128)S(1)}) custom-call(bf16[2048,2048]{1,0:T(8,128)(2,1)} %get-tuple-element.34.part_ref, f32[64,2048]{1,0:T(8,128)S(1)} %copy-done.3, bf16[256,2048]{1,0:T(8,128)(2,1)S(1)} %copy-done.2, f32[1,2048]{1,0:T(1,128)S(1)} %bitcast.98), custom_call_target="tpu_custom_call" | custom-call | tf_op jit(solution)/shard_map/reduce_and_norm/pallas_call | solution.py:1000
  350.2 0.8 copy-done.5
  351.0 24.4 %fusion.48 = f32[2048,2048]{0,1:T(8,128)} fusion(bf16[2048,2048]{1,0:T(8,128)(2,1)} %get-tuple-element.40, bf16[2048,2048]{1,0:T(8,128)(2,1)} %get-tuple-element.41), kind=kOutput, calls=%fused_computation.97 | convolution fusion | flops 17179869184 | bytes 33554432 | tf_op jit(solution)/shard_map/dot_general | solution.py:1279
  375.4 14.0 %copy.134 = bf16[2048,2048]{1,0:T(8,128)(2,1)} copy(f32[2048,2048]{0,1:T(8,128)} %fusion.48) | data formatting | bytes 25165824 | tf_op jit(solution)/shard_map/dot_general | solution.py:1279
  389.4 13.4 %fusion.49 = f32[1024,2048]{1,0:T(8,128)S(1)} fusion(bf16[2048,1024]{1,0:T(8,128)(2,1)} %get-tuple-element.46, bf16[2048,2048]{1,0:T(8,128)(2,1)} %get-tuple-element.47), kind=kOutput, calls=%fused_computation.98 | convolution fusion | flops 8589934592 | bytes 20971520 | tf_op jit(solution)/shard_map/dot_general | solution.py:1279
  402.8 3.2 copy-done.10
  406.6 1.7 fusion.43
  408.3 3.1 pad_maximum_fusion.3
  411.4 4.3 copy.136
  415.7 4.5 all-to-all-start
  420.5 2.3 fusion.16
  423.0 1.4 multiply_reduce_fusion
  425.7 1.2 subtract_convert_fusion.1
  426.9 0.8 pad_maximum_fusion.11
  427.7 1.8 copy.129
  429.5 1.9 pad_maximum_fusion.10
  431.4 1.8 copy.125
  433.2 1.0 convolution_convert_fusion.3
  434.2 5.6 convolution_convert_fusion
  439.9 4.7 fusion.4.part_ref
  444.9 2.1 convolution_convert_fusion.1
  447.0 2.0 slice.170
  449.1 0.9 broadcast_in_dim.35
  449.9 13.7 %concatenate.58.weights_ref = bf16[2048,2176]{1,0:T(8,128)(2,1)} concatenate(bf16[2048,1536]{1,0:T(8,128)(2,1)} %convolution_convert_fusion, bf16[2048,512]{1,0:T(8,128)(2,1)} %convolution_convert_fusion.1, bf16[2048,17]{1,0:T(8,128)(2,1)} %slice.170, bf16[2048,111]{1,0:T(8,128)(2,1)} %broadcast_in_dim.35), dimensions={1} | concatenate | bytes 17825792 | tf_op jit(solution)/shard_map/concatenate | solution.py:1533
  463.6 81.9 %finish_grads.1 = (bf16[256,2048]{1,0:T(8,128)(2,1)S(1)}, f32[256,2048]{1,0:T(8,128)}, f32[256,128]{1,0:T(8,128)S(1)}, f32[8,256]{1,0:T(8,128)S(1)}) custom-call(bf16[256,2048]{1,0:T(8,128)(2,1)S(1)} %fusion.4.part_ref, bf16[256,2048]{1,0:T(8,128)(2,1)S(1)} %copy-done.1, f32[1,2048]{1,0:T(1,128)S(1)} %bitcast.96, f32[64,2048]{1,0:T(8,128)S(1)} %copy-done.6, ...), custom_call_target="tpu_custom_call" | custom-call | tf_op jit(solution)/shard_map/finish_grads/pallas_call | solution.py:1233
  545.5 8.6 %slice_bitcast_fusion.3 = (f32[1,2048,352]{1,2,0:T(8,128)S(1)}, f32[1,2048,352]{1,2,0:T(8,128)S(1)}, f32[1,2048,352]{1,2,0:T(8,128)}, f32[1,2048,352]{1,2,0:T(8,128)}) fusion(f32[2048,2048]{0,1:T(8,128)} %fusion.48), kind=kLoop, calls=%fused_computation.12 | loop fusion | bytes 23068672 | tf_op jit(solution)/shard_map/stack | solution.py:1490
  554.1 5.9 pad_maximum_fusion
  560.0 3.2 pad_maximum_fusion.1
  563.2 1.2 slice_bitcast_fusion.6
  564.4 1.6 convert_element_type.183
  566.0 1.0 copy.137
  567.0 0.7 copy.138
  567.6 0.7 slice_reduce_fusion
  568.4 1.7 add_convert_fusion.2
  570.1 0.6 fusion.47
  570.7 3.1 slice_bitcast_fusion.1
  573.8 2.9 pad_maximum_fusion.2
  576.7 3.7 slice_convert_fusion
  580.4 2.9 copy.139
  583.3 1.5 copy.140
  584.8 12.6 %all-gather.2.cloned.1.call-done = bf16[256,2048]{1,0:T(8,128)(2,1)} async-done(((bf16[64,2048]{1,0:T(8,128)(2,1)}), bf16[256,2048]{1,0:T(8,128)(2,1)}) %all-gather.2.cloned.1.call-update) | async-done | bytes 1048592 | tf_op jit(solution)/shard_map/all_gather | solution.py:1483
  597.4 2.3 copy.193
  (93 shorter events, 5.4 us)
Async XLA Ops:
  7.2 437.4 %reduce-scatter.3.cloned.1.call-start = ((), (), s32[]{:S(2)}) async-start(), calls=%async_computation.3 | async-start | bytes 9437184 | tf_op jit(solution)/shard_map/reduce_scatter | solution.py:1367
  62.4 4.9 copy-start
  67.6 4.6 copy-start.28
  72.3 3.2 copy-start.12
  72.3 1.6 copy-start.30
  74.9 1.0 copy-start.15
  74.9 1.0 copy-start.17
  74.9 1.0 copy-start.19
  74.9 1.0 copy-start.21
  75.5 4.5 copy-start.8
  75.5 4.5 copy-start.31
  75.9 0.7 copy-start.25
  85.1 4.7 copy-start.23
  94.2 191.3 %copy-start.2 = (bf16[256,2048]{1,0:T(8,128)(2,1)S(1)}, bf16[256,2048]{1,0:T(8,128)(2,1)}, u32[]{:S(2)}) copy-start(bf16[256,2048]{1,0:T(8,128)(2,1)} %cot_ref.3) | copy-start | bytes 3145732
  94.2 191.4 %copy-start.7 = (f32[2048]{0:T(1024)S(1)}, f32[2048]{0:T(1024)}, u32[]{:S(2)}) copy-start(f32[2048]{0:T(1024)} %get-tuple-element.96) | copy-start | bytes 24580
  285.5 1.0 copy-start.3
  350.2 0.8 copy-start.5
  402.7 3.3 copy-start.10
  415.7 4.8 copy-start.32
  415.7 161.0 %all-to-all-start = ((bf16[8,256,528]{1,2,0:T(8,128)(2,1)}), bf16[8,256,528]{1,2,0:T(8,128)(2,1)}, u32[]{:S(2)}, u32[]{:S(2)}) async-start(bf16[8,256,528]{1,2,0:T(8,128)(2,1)} %copy.136), calls=%async_computation.2 | async-start | bytes 4325376 | tf_op jit(solution)/shard_map/all_to_all | solution.py:1507
  420.2 2.8 copy-start.9
  420.2 148.2 %reduce-scatter.5.cloned.1.call-start = ((), (), s32[]{:S(2)}) async-start(), calls=%async_computation.4 | async-start | bytes 1310720 | tf_op jit(solution)/shard_map/reduce_scatter | solution.py:1481
  420.5 4.0 copy-start.27
  423.0 1.8 copy-start.20
  423.0 1.8 copy-start.22
  423.0 2.2 copy-start.16
  423.0 2.2 copy-start.18
  424.5 1.1 copy-start.24
  426.9 7.3 %copy-start.1 = (bf16[256,2048]{1,0:T(8,128)(2,1)S(1)}, bf16[256,2048]{1,0:T(8,128)(2,1)}, u32[]{:S(2)}) copy-start(bf16[256,2048]{1,0:T(8,128)(2,1)} %tokens_ref.3) | copy-start | bytes 3145732
  426.9 7.3 %copy-start.29 = (f32[256]{0:T(256)S(1)}, f32[256]{0:T(256)}, u32[]{:S(2)}) copy-start(f32[256]{0:T(256)} %copy-done.28) | copy-start | bytes 3076
  434.2 5.7 copy-start.13
  434.2 5.6 copy-start.14
  439.9 5.0 copy-start.26
  444.6 152.8 %all-gather.2.cloned.1.call-start = ((), (), s32[]{:S(2)}) async-start(), calls=%async_computation.5 | async-start | bytes 1310720 | tf_op jit(solution)/shard_map/all_gather | solution.py:1483
  449.9 13.7 %copy-start.6 = (f32[64,2048]{1,0:T(8,128)S(1)}, f32[64,2048]{1,0:T(8,128)}, u32[]{:S(2)}) copy-start(f32[64,2048]{1,0:T(8,128)} %copy-done.5) | copy-start | bytes 1572868
  560.0 3.2 copy-start.11
  564.4 4.0 copy-start.4
Sparse Core Ops, SparseCore 0:
  350.4 76.0 reduce-scatter.2
  444.7 32.1 reduce-scatter.4
  570.2 27.1 all-gather.1

commit v3 on v2

v3 whole, which is shorter than its diff:
```python
import functools

import jax
import jax.numpy as jnp
import numpy as np
from jax import lax
from jax.experimental import pallas as pl
from jax.experimental.pallas import tpu as pltpu
from jax.sharding import PartitionSpec as P

HEAD_DIM = 128
TOP = 4
SEQ = 256


EPSILON = 1e-06
MESH = pl.DeviceIdType.MESH


def ring_chip(position, chips):
    half = chips // 2
    upper = position // half
    return position + upper * (chips - 1 + half - 2 * position)


def ring_spot(chip, chips):
    return ring_chip(chip, chips)


def greet(partners):
    barrier = pltpu.get_barrier_semaphore()
    for partner in partners:
        pl.semaphore_signal(barrier, inc=1, device_id=partner, device_id_type=MESH)
    pl.semaphore_wait(barrier, len(partners))


def remote(source, target, axis, device, sends, recvs, slot):
    return pltpu.make_async_remote_copy(
        src_ref=source,
        dst_ref=target,
        send_sem=sends.at[slot],
        recv_sem=recvs.at[slot],
        device_id={axis: device},
        device_id_type=MESH,
    )


class Ring:
    def __init__(self, ranks):
        self.ranks = ranks
        self.chips = ranks // 2
        self.half = self.chips // 2
        self.me = lax.axis_index("dp")
        self.core = self.me % 2
        self.position = ring_spot(self.me // 2, self.chips)
        self.sibling = self.me + 1 - 2 * self.core
        self.ahead = self.device(1)
        self.behind = self.device(-1)

    def chip(self, offset):
        return ring_chip((self.position + offset + self.chips) % self.chips, self.chips)

    def device(self, offset):
        return self.chip(offset) * 2 + self.core

    def other(self, offset):
        return self.chip(offset) * 2 + 1 - self.core

    def partners(self):
        return [{"dp": self.ahead}, {"dp": self.behind}, {"dp": self.sibling}]


def gather_slots(half):
    return 2 * half


def side_slots(half):
    return 2 * half


class RingGather:
    def __init__(self, ring, place, rows, sends, recvs, side_sends, side_recvs, base, side_base):
        self.ring, self.place, self.rows, self.cut = ring, place, rows, rows // 2
        self.sends, self.recvs = sends, recvs
        self.side_sends, self.side_recvs = side_sends, side_recvs
        self.base, self.side_base = base, side_base
        self.hops, self.sides = {}, 0

    def hop_copy(self, source, target, device, slot):
        return remote(source, target, "dp", device, self.sends, self.recvs, self.base + slot)

    def side_copy(self, source, target, slot):
        return remote(
            source,
            target,
            "dp",
            self.ring.sibling,
            self.side_sends,
            self.side_recvs,
            self.side_base + slot,
        )

    def hop(self, source, target, device, slot, size):
        self.hop_copy(source, target, device, slot).start()
        self.hops[slot] = size

    def share(self, source, target):
        self.side_copy(source, target, self.sides).start()
        self.sides += 1

    def begin(self, source):
        ring = self.ring
        target = self.place(ring.me, 0, self.rows)
        self.hop(source, target, ring.ahead, 0, self.rows)
        self.hop(source, target, ring.behind, ring.half, self.rows)
        self.share(source, target)

    def wait_hop(self, slot):
        block = self.place(self.ring.me, 0, self.hops[slot])
        self.hop_copy(block, block, self.ring.ahead, slot).wait_recv()

    def step(self, number):
        ring = self.ring
        for which, sign in enumerate((-1, 1)):
            owner = ring.device(sign * number)
            onward = (ring.ahead, ring.behind)[which]
            self.wait_hop(which * ring.half + number - 1)
            if number < ring.half:
                block = self.place(owner, 0, self.rows)
                size = self.rows
                part = block
                if number == ring.half - 1:
                    size = self.cut
                    part = self.place(owner, (0, self.cut)[which], size)
                self.hop(part, part, onward, which * ring.half + number, size)
                self.share(block, block)
        if number == ring.half:
            block = self.place(ring.device(number), 0, self.rows)
            self.share(block, block)

    def wait_side(self, index):
        block = self.place(self.ring.me, 0, self.rows)
        self.side_copy(block, block, index).wait_recv()

    def sent(self):
        for slot, size in self.hops.items():
            block = self.place(self.ring.me, 0, size)
            self.hop_copy(block, block, self.ring.ahead, slot).wait_send()
        for index in range(self.sides):
            block = self.place(self.ring.me, 0, self.rows)
            self.side_copy(block, block, index).wait_send()

    def finish(self):
        self.sent()
        for index in range(self.sides):
            self.wait_side(index)


def near_first(peers):
    order = [0]
    for step in range(1, peers // 2 + 1):
        order.append(step)
        if peers - step != step:
            order.append(peers - step)
    return order


STRIP = 64
OUT_FIRST, OUT_NEXT, NORM_DUE = 10, 13, 15


def strips(rows, body):
    strip = min(STRIP, rows)

    def step(index, carry):
        body(pl.ds(pl.multiple_of(index * strip, strip), strip), index * strip, strip)
        return carry

    lax.fori_loop(0, rows // strip, step, 0)


def matmul(left, right):
    return lax.dot_general(
        left, right, (((1,), (0,)), ((), ())), preferred_element_type=jnp.float32
    )


def matmul_last(left, right):
    return lax.dot_general(
        left, right, (((1,), (1,)), ((), ())), preferred_element_type=jnp.float32
    )


def tiles(width, tile, body):
    def step(index, carry):
        body(pl.ds(pl.multiple_of(index * tile, tile), tile))
        return carry

    lax.fori_loop(0, width // tile, step, 0)


class Layout:
    def __init__(self, local_experts, expert_hidden, shared_own, expert_count):
        self.local_experts = local_experts
        self.expert_hidden = expert_hidden
        self.shared_own = shared_own
        self.expert_count = expert_count
        self.part = -(-expert_hidden // 128) * 128
        self.shared_at = local_experts * self.part
        self.router_at = self.shared_at + shared_own
        self.last = -(-(shared_own + expert_count + 1) // 128) * 128
        self.hidden = self.shared_at + self.last
        self.router_tile = self.router_at // 128 * 128
        self.router_lane = self.router_at - self.router_tile
        self.tile = 256 if self.hidden % 256 == 0 else 128


def hidden_tiles(layout, x_ref, gates, ups, pre_gate, pre_up):
    def body(spot):
        pre_gate[:, spot] = matmul_last(x_ref[...], gates[spot, :])
        pre_up[:, spot] = matmul_last(x_ref[...], ups[spot, :])

    tiles(layout.hidden, layout.tile, body)


def cot_tiles(layout, cot_ref, downs, cot_hidden):
    def body(spot):
        cot_hidden[:, spot] = matmul_last(cot_ref[...], downs[spot, :])

    tiles(layout.hidden, layout.tile, body)


def gate_strips(layout, first_expert, chosen, pre_gate, pre_up, cot_hidden, scaled, grads):
    rows = pre_gate.shape[0]
    count, lane0 = layout.expert_count, layout.router_lane
    router = slice(layout.router_tile, layout.router_tile + 128)
    bounds = [(j * layout.part, (j + 1) * layout.part) for j in range(layout.local_experts)]
    bounds.append((layout.shared_at, layout.hidden))
    low = scaled.dtype

    def body(spot, start, size):
        lane = lax.broadcasted_iota(jnp.int32, (size, 128), 1)
        logits = pre_gate[spot, router]
        is_router = (lane >= lane0) & (lane < lane0 + count)
        is_switch = lane == lane0 + count
        power = jnp.where(is_router, jnp.exp(jnp.where(is_router, logits, 0.0)), 0.0)
        probs = power / jnp.sum(power, axis=-1, keepdims=True)
        raw = jnp.sum(jnp.where(is_switch, logits, 0.0), axis=-1, keepdims=True)
        switch = 1.0 / (1.0 + jnp.exp(-raw))
        mask = chosen[spot, :].astype(jnp.float32)
        scales = []
        for j in range(layout.local_experts):
            spotted = lane == lane0 + first_expert + j
            scales.append(jnp.sum(jnp.where(spotted, probs * mask, 0.0), axis=-1, keepdims=True))
        scales.append(switch)
        totals = []
        for (begin, end), scale in zip(bounds, scales):
            shared = begin == layout.shared_at
            columns = slice(begin, end)
            gate, up = pre_gate[spot, columns], pre_up[spot, columns]
            through = cot_hidden[spot, columns].astype(jnp.float32)
            sig = 1.0 / (1.0 + jnp.exp(-gate))
            act = gate * sig
            state = act * up
            grad = scale * through
            totals.append(jnp.sum(state * through, axis=-1, keepdims=True))
            scaled[spot, columns] = (scale * state).astype(low)
            grad_gate = grad * up * sig * (1.0 + gate * (1.0 - sig))
            grads[spot, columns] = grad_gate.astype(low)
            grads[spot, layout.hidden + begin : layout.hidden + end] = (grad * act).astype(low)
        choice = jnp.zeros_like(probs)
        for j in range(layout.local_experts):
            spotted = lane == lane0 + first_expert + j
            choice = choice + jnp.where(spotted, mask * totals[j], 0.0)
        small = probs * (choice - jnp.sum(probs * choice, axis=-1, keepdims=True))
        small = jnp.where(is_switch, totals[-1] * switch * (1.0 - switch), small)
        kept = grads[spot, router].astype(jnp.float32)
        kept = jnp.where(is_router | is_switch, small, kept)
        grads[spot, router] = kept.astype(low)

    strips(rows, body)


def out_tiles(width, scaled, downs, out):
    def body(spot):
        out[:, spot] = matmul(scaled[...], downs[:, spot]).astype(out.dtype)

    tiles(width, 256, body)


def back_tiles(layout, width, grads, gates, ups, back):
    hidden = layout.hidden

    def body(spot):
        total = matmul(grads[:, :hidden], gates[:, spot])
        total = total + matmul(grads[:, hidden:], ups[:, spot])
        back[:, spot] = total.astype(back.dtype)

    tiles(width, 256, body)


def rope(values, cosine, sine, sign):
    return values * cosine + pltpu.roll(values, HEAD_DIM // 2, 1) * (sine * sign)


def attend(heads, qkv, allowed_ref, cos_ref, sin_ref, queries, keys, values, probs_ref, context):
    cosine, sine = cos_ref[...], sin_ref[...]
    allowed = allowed_ref[...] > 0.5
    low = queries.dtype
    for head in range(heads):
        columns = slice(head * HEAD_DIM, (head + 1) * HEAD_DIM)
        query = rope(qkv(head), cosine, sine, 1.0).astype(low)
        key = rope(qkv(heads + head), cosine, sine, 1.0).astype(low)
        value = qkv(2 * heads + head).astype(low)
        queries[:, columns], keys[:, columns], values[:, columns] = query, key, value
        scores = matmul_last(query, key) * HEAD_DIM ** (-0.5)
        power = jnp.where(allowed, jnp.exp(jnp.where(allowed, scores, 0.0)), 0.0)
        probs = power / jnp.sum(power, axis=-1, keepdims=True)
        probs_ref[head] = probs
        context[:, columns] = matmul(probs.astype(low), value).astype(low)


def layer_kernel(
    layout,
    ranks,
    peers,
    query_ref,
    key_ref,
    value_ref,
    chosen_own_ref,
    proj_ref,
    router_ref,
    vectors_ref,
    tokens_ref,
    cot_ref,
    allowed_ref,
    cos_ref,
    sin_ref,
    expert_gate_ref,
    expert_up_ref,
    expert_down_ref,
    shared_gate_ref,
    shared_up_ref,
    shared_down_ref,
    rows_all,
    columns_all,
    attn_in,
    queries,
    keys,
    values,
    context,
    probs_ref,
    x_all,
    cot_all,
    middle_ref,
    scaled_ref,
    grads_ref,
    out_ref,
    back_ref,
    row_stage,
    column_stage,
    rows_full,
    columns_full,
    qkv_raw,
    part_ref,
    gates,
    ups,
    downs,
    shared_got,
    own,
    got,
    x_block,
    cot_block,
    pre_gate,
    pre_up,
    cot_hidden,
    scaled,
    grads,
    out,
    back,
    chosen,
    local_sem,
    gather_sem,
    a_sends,
    a_recvs,
    a_side_sends,
    a_side_recvs,
    block_sem,
    store_sem,
    shared_sends,
    shared_recvs,
    z_sends,
    z_recvs,
    x_sends,
    x_recvs,
    sends,
    recvs,
    side_sends,
    side_recvs,
    c_sends,
    c_recvs,
    c_side_sends,
    c_side_recvs,
):
    ring = Ring(ranks)
    here = lax.axis_index("tensor")
    block, width = tokens_ref.shape
    rows = block // peers
    depth = width // ranks
    half = ring.half
    away = [(here + k) % peers for k in range(peers)]
    others = [(ring.me + k) % ranks for k in range(ranks)]

    count, lane0 = layout.expert_count, layout.router_lane
    head_width = query_ref.shape[1]
    heads = head_width // HEAD_DIM
    lot, wide = row_stage.shape
    height = column_stage.shape[0]
    small_rows = height - head_width
    low = gates.dtype
    loads, start = [], 0
    for index, source in enumerate((query_ref, key_ref, value_ref, chosen_own_ref)):
        size = source.shape[1]
        loads.append(
            pltpu.make_async_copy(source, row_stage.at[:, pl.ds(start, size)], gather_sem.at[index])
        )
        start += size
    loads.append(
        pltpu.make_async_copy(
            proj_ref, column_stage.at[pl.ds(small_rows, head_width)], gather_sem.at[4]
        )
    )
    for load in loads:
        load.start()
    small = jnp.concatenate(
        [
            router_ref[...].astype(jnp.float32),
            vectors_ref[...].astype(jnp.float32),
            jnp.zeros((small_rows - count - vectors_ref.shape[0], depth), jnp.float32),
        ],
        axis=0,
    )
    column_stage[:small_rows, :] = small.astype(low)
    greet(
        [{"dp": others[k]} for k in range(1, ranks)] + [{"tensor": away[k]} for k in range(1, peers)]
    )
    order = near_first(peers)

    def row_place(device, first, size):
        return rows_all.at[pl.ds(device * lot + first, size)]

    def column_place(device, first, size):
        place = pl.ds(pl.multiple_of(device * depth, depth), depth)
        return columns_all.at[pl.ds(first, size), place]

    for load in loads:
        load.wait()
    gathers = [
        RingGather(ring, row_place, lot, a_sends, a_recvs, a_side_sends, a_side_recvs, 0, 0),
        RingGather(
            ring,
            column_place,
            height,
            a_sends,
            a_recvs,
            a_side_sends,
            a_side_recvs,
            gather_slots(half),
            side_slots(half),
        ),
    ]
    stores_own = []
    for index, (gather, stage) in enumerate(zip(gathers, (row_stage, column_stage))):
        gather.begin(stage)
        store = pltpu.make_async_copy(
            stage, gather.place(ring.me, 0, gather.rows), gather_sem.at[5 + index]
        )
        store.start()
        stores_own.append(store)
    for number in range(1, half):
        for gather in gathers:
            gather.step(number)

    shared_refs = (shared_gate_ref, shared_up_ref, shared_down_ref)
    handed, kept = [], []
    for k in range(1, ranks):
        for which, source in enumerate(shared_refs):
            copy = remote(
                source.at[others[k]],
                shared_got.at[which, ring.me],
                "dp",
                others[k],
                shared_sends,
                shared_recvs,
                which * (ranks - 1) + ranks - k - 1,
            )
            copy.start()
            handed.append(copy)
    for which, source in enumerate(shared_refs):
        copy = pltpu.make_async_copy(
            source.at[ring.me], shared_got.at[which, ring.me], local_sem.at[which]
        )
        copy.start()
        kept.append(copy)

    def cot_place(device, start, size):
        return cot_all.at[pl.ds(device * block + start, size)]

    cots = RingGather(
        ring, cot_place, block, c_sends, c_recvs, c_side_sends, c_side_recvs, 0, 0
    )
    cots.begin(cot_ref)
    kept_cot = pltpu.make_async_copy(cot_ref, cot_place(ring.me, 0, block), local_sem.at[3])
    kept_cot.start()

    experts, hid = layout.local_experts, layout.expert_hidden
    wides = (gates, ups, downs)
    loads = []
    for which, (target, source) in enumerate(
        zip(wides, (expert_gate_ref, expert_up_ref, expert_down_ref))
    ):
        for j in range(experts):
            load = pltpu.make_async_copy(
                source.at[j],
                target.at[pl.ds(j * layout.part, hid)],
                local_sem.at[5 + which * experts + j],
            )
            load.start()
            loads.append(load)
            if layout.part > hid:
                target[j * layout.part + hid : (j + 1) * layout.part, :] = jnp.zeros(
                    (layout.part - hid, width), low
                )
        target[layout.router_at :, :] = jnp.zeros((layout.hidden - layout.router_at, width), low)

    for gather in gathers:
        gather.step(half)
    for store in stores_own:
        store.wait()
    for gather in gathers:
        for index in range(gather.sides):
            gather.wait_side(index)
    fetches = [
        pltpu.make_async_copy(rows_all, rows_full, gather_sem.at[7]),
        pltpu.make_async_copy(columns_all, columns_full, gather_sem.at[8]),
    ]
    for fetch in fetches:
        fetch.start()
    fetches[1].wait()
    gates[layout.router_at : layout.router_at + count + 1, :] = columns_full[: count + 1, :]
    vectors = columns_full[:small_rows, :].astype(jnp.float32)
    attn_gain = vectors[count + 1 : count + 2, :]
    ffn_gain = vectors[count + 2 : count + 3, :]

    def norm_in(spot, start, size):
        value = tokens_ref[spot, :].astype(jnp.float32)
        inverse = lax.rsqrt(jnp.mean(value * value, axis=-1, keepdims=True) + EPSILON)
        attn_in[spot, :] = ((value * inverse) * attn_gain).astype(low)

    strips(block, norm_in)
    fetches[0].wait()

    def project(spot):
        qkv_raw[:, spot] = matmul(attn_in[...], rows_full[:, spot])

    tiles(3 * head_width, 256, project)

    def qkv(index):
        return qkv_raw[:, index * HEAD_DIM : (index + 1) * HEAD_DIM]

    attend(heads, qkv, allowed_ref, cos_ref, sin_ref, queries, keys, values, probs_ref, context)

    def project_out(spot):
        part_ref[:, spot] = matmul(context[...], columns_full[small_rows:, spot]).astype(low)

    tiles(width, 256, project_out)

    exchanged = []
    for k in reversed(order[1:]):
        copy = remote(
            part_ref.at[pl.ds(away[k] * rows, rows)],
            got.at[peers - k - 1],
            "tensor",
            away[k],
            z_sends,
            z_recvs,
            peers - k - 1,
        )
        copy.start()
        exchanged.append(copy)

    for copy in exchanged:
        copy.wait()
    first = here * rows

    def norm(spot, start, size):
        mine = pl.ds(pl.multiple_of(first + start, size), size)
        total = part_ref[mine, :].astype(jnp.float32)
        for k in range(peers - 1):
            total = total + got[k, spot, :].astype(jnp.float32)
        middle = tokens_ref[mine, :].astype(jnp.float32) + total
        middle_ref[spot, :] = middle
        inverse = lax.rsqrt(jnp.mean(middle * middle, axis=-1, keepdims=True) + EPSILON)
        own[spot, :] = ((middle * inverse) * ffn_gain).astype(own.dtype)

    strips(rows, norm)

    def place_of(k):
        def place(device, start, size):
            return x_all.at[pl.ds(device * block + away[k] * rows + start, size)]

        return place

    mine = place_of(0)(ring.me, 0, rows)
    forwards = []
    for k in order[1:]:
        copy = remote(own, mine, "tensor", away[k], x_sends, x_recvs, peers - k - 1)
        copy.start()
        forwards.append(copy)
    works = [
        RingGather(
            ring,
            place_of(k),
            rows,
            sends,
            recvs,
            side_sends,
            side_recvs,
            k * gather_slots(half),
            k * side_slots(half),
        )
        for k in range(peers)
    ]
    works[0].begin(own)
    store = pltpu.make_async_copy(own, mine, local_sem.at[4])
    store.start()

    for copy in kept + loads:
        copy.wait()
    for copy in handed:
        copy.wait_recv()
    for which, target in enumerate(wides):
        for source in range(ranks):
            columns = slice(source * depth, (source + 1) * depth)
            target[layout.shared_at : layout.router_at, columns] = shared_got[which, source]

    for k in order[1:]:
        spot = place_of(k)(ring.me, 0, rows)
        remote(own, spot, "tensor", away[k], x_sends, x_recvs, k - 1).wait_recv()
        works[k].begin(spot)
    store.wait()
    kept_cot.wait()
    passing = [cots] + [works[k] for k in order]
    cuts = [part * len(passing) // 5 for part in range(6)]
    chip_rows = 2 * block
    first_expert = ring.me * experts

    def stores(spot):
        return [
            pltpu.make_async_copy(source, target.at[spot], store_sem.at[slot])
            for slot, (source, target) in enumerate(
                ((scaled, scaled_ref), (grads, grads_ref), (out, out_ref), (back, back_ref))
            )
        ]

    def chip_step(turn, carry):
        offset = (1 - 2 * (turn % 2)) * ((turn + 1) // 2)
        spot = pl.ds(pl.multiple_of(ring.chip(offset) * chip_rows, chip_rows), chip_rows)

        def pass_on(part):
            for number in range(1, half + 1):

                @pl.when(turn == 2 * number - 2)
                def _(number=number):
                    for work in passing[cuts[part] : cuts[part + 1]]:
                        work.step(number)

        cots.wait_side(turn)
        load_cot = pltpu.make_async_copy(cot_all.at[spot], cot_block, block_sem.at[0])
        load_cot.start()
        for device in range(2):
            for fold in range(block // lot):
                there = ring.chip(offset) * 2 * lot + device * lot
                first_lane = 3 * head_width + fold * 128
                chosen[device * block + fold * lot : device * block + (fold + 1) * lot, :] = rows_full[
                    pl.ds(pl.multiple_of(there, lot), lot), first_lane : first_lane + 128
                ]
        for work in works:
            work.wait_side(turn)
        load_x = pltpu.make_async_copy(x_all.at[spot], x_block, block_sem.at[1])
        load_x.start()
        load_cot.wait()
        cot_tiles(layout, cot_block, downs, cot_hidden)
        pass_on(0)
        load_x.wait()
        hidden_tiles(layout, x_block, gates, ups, pre_gate, pre_up)
        pass_on(1)
        pending = stores(spot)

        @pl.when(turn > 0)
        def _():
            pending[0].wait()
            pending[1].wait()

        gate_strips(
            layout,
            first_expert,
            chosen,
            pre_gate,
            pre_up,
            cot_hidden,
            scaled,
            grads,
        )
        pending[0].start()
        pending[1].start()
        pass_on(2)

        @pl.when(turn > 0)
        def _():
            pending[2].wait()
            pending[3].wait()

        out_tiles(width, scaled, downs, out)
        pending[2].start()
        pass_on(3)
        back_tiles(layout, width, grads, gates, ups, back)
        pending[3].start()
        pass_on(4)
        return carry

    lax.fori_loop(0, ring.chips, chip_step, 0)
    for copy in stores(pl.ds(0, chip_rows)):
        copy.wait()
    for copy in forwards + handed:
        copy.wait_send()
    for gather in gathers:
        gather.sent()
    cots.sent()
    for work in works:
        work.sent()


def layer_forward_back(
    layout,
    query,
    key,
    value,
    chosen,
    proj,
    router,
    vectors,
    tokens,
    cot,
    allowed,
    cosine,
    sine,
    expert_gate,
    expert_up,
    expert_down,
    shared_gate,
    shared_up,
    shared_down,
    small_rows,
    ranks,
    peers,
    identity,
):
    half = ranks // 4
    block, width = tokens.shape
    rows = block // peers
    total = ranks * block
    depth = width // ranks
    hidden = layout.hidden
    chip = 2 * block
    head_width = query.shape[1]
    wide = 3 * head_width + chosen.shape[1]
    height = small_rows + head_width
    low = tokens.dtype
    vmem = pl.BlockSpec(memory_space=pltpu.VMEM)
    hbm = pl.BlockSpec(memory_space=pl.ANY)
    dma = pltpu.SemaphoreType.DMA
    f32 = jnp.float32
    heads = head_width // HEAD_DIM
    small_ones = [jax.ShapeDtypeStruct((block, head_width), low)] * 4
    return pl.pallas_call(
        functools.partial(layer_kernel, layout, ranks, peers),
        out_shape=(
            jax.ShapeDtypeStruct((width, wide), low),
            jax.ShapeDtypeStruct((height, width), low),
            jax.ShapeDtypeStruct((block, width), low),
            *small_ones,
            jax.ShapeDtypeStruct((heads, block, block), f32),
            jax.ShapeDtypeStruct((total, width), low),
            jax.ShapeDtypeStruct((total, width), low),
            jax.ShapeDtypeStruct((rows, width), f32),
            jax.ShapeDtypeStruct((total, hidden), low),
            jax.ShapeDtypeStruct((total, 2 * hidden), low),
            jax.ShapeDtypeStruct((total, width), low),
            jax.ShapeDtypeStruct((total, width), low),
        ),
        in_specs=[hbm] * 5 + [vmem] * 7 + [hbm] * 6,
        out_specs=(hbm, hbm, *[vmem] * 6, hbm, hbm, vmem, hbm, hbm, hbm, hbm),
        scratch_shapes=[
            pltpu.VMEM((depth, wide), low),
            pltpu.VMEM((height, depth), low),
            pltpu.VMEM((width, wide), low),
            pltpu.VMEM((height, width), low),
            pltpu.VMEM((block, 3 * head_width), f32),
            pltpu.VMEM((block, width), low),
            pltpu.VMEM((hidden, width), low),
            pltpu.VMEM((hidden, width), low),
            pltpu.VMEM((hidden, width), low),
            pltpu.VMEM((3, ranks, layout.shared_own, depth), low),
            pltpu.VMEM((rows, width), low),
            pltpu.VMEM((peers - 1, rows, width), low),
            pltpu.VMEM((chip, width), low),
            pltpu.VMEM((chip, width), low),
            pltpu.VMEM((chip, hidden), f32),
            pltpu.VMEM((chip, hidden), f32),
            pltpu.VMEM((chip, hidden), f32),
            pltpu.VMEM((chip, hidden), low),
            pltpu.VMEM((chip, 2 * hidden), low),
            pltpu.VMEM((chip, width), low),
            pltpu.VMEM((chip, width), low),
            pltpu.VMEM((chip, 128), low),
            dma((5 + 3 * layout.local_experts,)),
            dma((9,)),
            dma((2 * gather_slots(half),)),
            dma((2 * gather_slots(half),)),
            dma((2 * side_slots(half),)),
            dma((2 * side_slots(half),)),
            dma((2,)),
            dma((4,)),
            dma((3 * (ranks - 1),)),
            dma((3 * (ranks - 1),)),
            dma((peers - 1,)),
            dma((peers - 1,)),
            dma((peers - 1,)),
            dma((peers - 1,)),
            dma((peers * gather_slots(half),)),
            dma((peers * gather_slots(half),)),
            dma((peers * side_slots(half),)),
            dma((peers * side_slots(half),)),
            dma((gather_slots(half),)),
            dma((gather_slots(half),)),
            dma((side_slots(half),)),
            dma((side_slots(half),)),
        ],
        compiler_params=pltpu.CompilerParams(
            collective_id=identity, has_side_effects=True, vmem_limit_bytes=62 << 20
        ),
        name="layer_forward_back",
    )(
        query,
        key,
        value,
        chosen,
        proj,
        router,
        vectors,
        tokens,
        cot,
        allowed,
        cosine,
        sine,
        expert_gate,
        expert_up,
        expert_down,
        shared_gate,
        shared_up,
        shared_down,
    )


class RingReduce:
    def __init__(self, ring, source_at, rows, buffers, sems, slot):
        self.ring, self.source_at, self.rows, self.cut = ring, source_at, rows, rows // 2
        self.mine, self.side, self.got = [buffer.at[slot] for buffer in buffers]
        self.loads, self.sends, self.recvs, self.side_sends, self.side_recvs = sems
        self.base, self.side_base = slot * 2 * ring.half, slot * ring.chips
        half = ring.half
        self.order = [half]
        for distance in range(half - 1, 0, -1):
            self.order += [distance, ring.chips - distance]
        self.order.append(0)

    def load(self, offset):
        return pltpu.make_async_copy(
            self.source_at(self.ring.device(offset)),
            self.mine.at[offset],
            self.loads.at[self.side_base + offset],
        )

    def side_copy(self, offset):
        return remote(
            self.source_at(self.ring.other(offset)),
            self.side.at[offset],
            "dp",
            self.ring.sibling,
            self.side_sends,
            self.side_recvs,
            self.side_base + offset,
        )

    def hand_over(self, offset):
        self.side_copy(offset).start()
        self.load(offset).start()

    def ready(self, offset):
        self.load(offset).wait()
        self.side_copy(offset).wait_recv()

    def hop(self, which, number):
        ring, half, cut = self.ring, self.ring.half, self.cut
        distance = half - number
        offset = distance if which == 0 else ring.chips - distance
        place = pl.ds((0, cut)[which], cut) if number == 0 else pl.ds(0, self.rows)
        return remote(
            self.mine.at[offset, place],
            self.got.at[which * half + number, place],
            "dp",
            (ring.ahead, ring.behind)[which],
            self.sends,
            self.recvs,
            self.base + which * half + number,
        )

    def add(self, offset, extra, first, size):
        def total(spot):
            mine = self.mine[offset, spot, :].astype(jnp.float32)
            return mine + self.side[offset, spot, :].astype(jnp.float32)

        def more(spot, start, count):
            here = pl.ds(pl.multiple_of(first + start, count), count)
            value = total(here) + extra[here, :].astype(jnp.float32)
            self.mine[offset, here, :] = value.astype(self.mine.dtype)

        rest, begin = self.rows - size, 0 if first else size

        def plain(spot, start, count):
            here = pl.ds(pl.multiple_of(begin + start, count), count)
            self.mine[offset, here, :] = total(here).astype(self.mine.dtype)

        if size:
            strips(size, more)
        if rest:
            strips(rest, plain)

    def step(self, number):
        ring, half, cut = self.ring, self.ring.half, self.cut
        if number == 0:
            self.ready(half)
            self.add(half, None, 0, 0)
            self.hop(0, 0).start()
            self.hop(1, 0).start()
            return
        for which in range(2):
            distance = half - number
            offset = distance if which == 0 else ring.chips - distance
            self.ready(offset)
            self.hop(which, number - 1).wait_recv()
            extra = self.got.at[which * half + number - 1]
            if number == 1:
                self.add(offset, extra, (0, cut)[which], cut)
            else:
                self.add(offset, extra, 0, self.rows)
            self.hop(which, number).start()

    def total(self, emit):
        half = self.ring.half
        self.ready(0)
        self.hop(0, half - 1).wait_recv()
        self.hop(1, half - 1).wait_recv()

        def body(spot, start, size):
            value = self.mine[0, spot, :].astype(jnp.float32) + self.side[0, spot, :].astype(jnp.float32)
            value = value + self.got[half - 1, spot, :].astype(jnp.float32)
            value = value + self.got[2 * half - 1, spot, :].astype(jnp.float32)
            emit(spot, start, size, value)

        strips(self.rows, body)

    def finish(self):
        for offset in range(self.ring.chips):
            self.side_copy(offset).wait_send()
        for number in range(self.ring.half):
            for which in range(2):
                self.hop(which, number).wait_send()


def reduce_buffers(pieces, chips, rows, width, low):
    return [pltpu.VMEM((pieces, chips, rows, width), low)] * 3


def reduce_sems(pieces, chips):
    dma = pltpu.SemaphoreType.DMA
    return [dma((pieces * chips,))] * 5


def back_kernel(
    layout,
    ranks,
    peers,
    with_out,
    part_ref,
    out_part_ref,
    middle_ref,
    cot_ref,
    gain_ref,
    x_ref,
    cots_ref,
    grads_ref,
    scaled_ref,
    low_all_ref,
    grad_ref,
    small_ref,
    out_sum_ref,
    gate_grads_ref,
    up_grads_ref,
    down_grads_ref,
    shared_grads_ref,
    *refs,
):
    z_stage, z_got, low_ref, right, left, turned, product, experts_low, gain_grad = refs[:9]
    z_sends, z_recvs, x_sends, x_recvs, local_sem, right_sem, left_sem, product_sem = refs[9:17]
    back_buffers, back_sems = refs[17:20], refs[20:25]
    out_buffers, out_sems = refs[25:28], refs[28:]
    ring = Ring(ranks)
    here = lax.axis_index("tensor")
    block, width = cot_ref.shape
    rows = block // peers
    half = ring.half
    away = [(here + k) % peers for k in range(peers)]
    greet(ring.partners() + [{"tensor": away[k]} for k in range(1, peers)])
    order = list(reversed(near_first(peers)))
    hidden = layout.hidden

    def reducer(source, buffers, sems, k):
        def source_at(device):
            return source.at[pl.ds(device * block + away[k] * rows, rows)]

        return RingReduce(ring, source_at, rows, buffers, sems, k)

    backs = {k: reducer(part_ref, back_buffers, back_sems, k) for k in order}
    outs = {}
    if with_out:
        outs = {k: reducer(out_part_ref, out_buffers, out_sems, k) for k in order}
    for offset in backs[0].order:
        for k in order:
            backs[k].hand_over(offset)

    def fetch_right(source, slot):
        return pltpu.make_async_copy(source, right, right_sem)

    def fetch_left(wide):
        source = scaled_ref if wide == 2 else grads_ref.at[:, pl.ds(wide * hidden, hidden)]
        return pltpu.make_async_copy(source, left, left_sem)

    fetch_right(x_ref, 0).start()
    fetch_left(0).start()
    for number in range(half):
        for k in order:
            backs[k].step(number)
    for offset in backs[0].order:
        for k in outs:
            outs[k].hand_over(offset)

    def pass_z(k):
        def emit(spot, start, size, value):
            z_stage[k, spot, :] = value.astype(z_stage.dtype)

        backs[k].total(emit)
        z_copy(k).start()

    def z_copy(k):
        return remote(
            z_stage.at[k], z_got.at[peers - k - 1], "tensor", away[k], z_sends, z_recvs, peers - k - 1
        )

    tile = 256
    blocks = width // tile
    steps = 3 * blocks

    def results(step, wide):
        slot = step % 2
        columns = pl.ds(pl.multiple_of(step % blocks * tile, tile), tile)
        copies = [
            pltpu.make_async_copy(
                product.at[slot, pl.ds(j * layout.part, layout.expert_hidden)],
                (gate_grads_ref, up_grads_ref, down_grads_ref)[wide].at[j, :, columns],
                product_sem.at[slot * (layout.local_experts + 1) + j],
            )
            for j in range(layout.local_experts)
        ]
        copies.append(
            pltpu.make_async_copy(
                experts_low.at[slot],
                shared_grads_ref.at[wide, :, columns],
                product_sem.at[slot * (layout.local_experts + 1) + layout.local_experts],
            )
        )
        return copies

    def grad_step(step, carry):
        wide, turn, slot = step // blocks, step % blocks, step % 2
        for number in range(3):

            @pl.when(step == number * blocks)
            def _(number=number):
                fetch_left(number).wait()
                if number == 0:
                    fetch_right(x_ref, 0).wait()

                def turn_over(index, carry):
                    spot = pl.ds(pl.multiple_of(index * tile, tile), tile)
                    turned[:, spot] = left[spot, :].T
                    return carry

                lax.fori_loop(0, left.shape[0] // tile, turn_over, 0)
                if number < 2:
                    fetch_left(number + 1).start()
                else:
                    fetch_right(cots_ref, 0).start()
                    fetch_right(cots_ref, 0).wait()

        @pl.when(step > 1)
        def _():
            for copy in results(step, 0):
                copy.wait()

        columns = pl.ds(pl.multiple_of(turn * tile, tile), tile)
        value = matmul(turned[...], right[:, columns])
        product[slot] = value[: layout.shared_at].astype(product.dtype)
        experts_low[slot] = value[layout.shared_at : layout.router_at].astype(product.dtype)

        @pl.when(wide == 0)
        def _():
            small = small_ref.shape[0]
            small_ref[:, columns] = value[layout.router_at : layout.router_at + small]

        for number in range(3):

            @pl.when(wide == number)
            def _(number=number):
                for copy in results(step, number):
                    copy.start()

        for due, event in events:

            @pl.when(step == due)
            def _(event=event):
                event()

        return carry

    first = here * rows
    spare = layout.expert_count + 2
    gain_grad[...] = jnp.zeros_like(gain_grad)

    def norm(spot, start, size, value):
        for k in range(peers - 1):
            value = value + z_got[k, spot, :].astype(jnp.float32)
        middle = middle_ref[spot, :]
        inverse = lax.rsqrt(jnp.mean(middle * middle, axis=-1, keepdims=True) + EPSILON)
        normed = middle * inverse
        scaled = value * gain_ref[...]
        back = inverse * (scaled - normed * jnp.mean(scaled * normed, axis=-1, keepdims=True))
        mine = pl.ds(pl.multiple_of(first + start, size), size)
        grad = cot_ref[mine, :].astype(jnp.float32) + back
        grad_ref[spot, :] = grad
        low_ref[spot, :] = grad.astype(low_ref.dtype)
        gain_grad[...] += jnp.sum(value * normed, axis=0, keepdims=True)

    mine = low_all_ref.at[pl.ds(here * rows, rows)]
    store = pltpu.make_async_copy(low_ref, mine, local_sem)

    def spread():
        return [
            remote(low_ref, mine, "tensor", away[k], x_sends, x_recvs, peers - k - 1)
            for k in near_first(peers)[:0:-1]
        ]

    def finish_norm():
        for k in order[:-1]:
            z_copy(k).wait_recv()
        backs[0].total(norm)
        for copy in spread():
            copy.start()
        store.start()

    gap = 12 // (peers - 1)
    events = [(3 + gap * index, functools.partial(pass_z, k)) for index, k in enumerate(order[:-1])]
    for k in outs:
        events.append((OUT_FIRST, functools.partial(outs[k].step, 0)))
    for number in range(1, half):
        for index, k in enumerate(outs):
            events.append((OUT_NEXT + number, functools.partial(outs[k].step, number)))
    events.append((NORM_DUE, finish_norm))
    lax.fori_loop(0, steps, grad_step, 0)
    for step in (steps - 2, steps - 1):
        for copy in results(step, 0):
            copy.wait()
    small_ref[spare - 1 : spare, :] = jnp.zeros((1, width), jnp.float32)
    small_ref[spare : spare + 1, :] = gain_grad[...]
    if not with_out:
        out_sum_ref[...] = jnp.zeros_like(out_sum_ref)
    for k in outs:

        def emit_out(spot, start, size, value, k=k):
            there = pl.ds(pl.multiple_of(away[k] * rows + start, size), size)
            out_sum_ref[there, :] = value.astype(out_sum_ref.dtype)

        outs[k].total(emit_out)
    store.wait()
    for k in order[:-1]:
        z_copy(k).wait_send()
    for copy in spread():
        copy.wait()
    for k in order:
        backs[k].finish()
    for k in outs:
        outs[k].finish()


def reduce_and_norm(
    layout,
    part,
    out_part,
    middle,
    cotangent,
    gain,
    x_all,
    cot_all,
    grads,
    scaled,
    small_rows,
    ranks,
    peers,
    identity,
):
    chips = ranks // 2
    block, width = cotangent.shape
    total = x_all.shape[0]
    rows = block // peers
    hidden = layout.hidden
    experts = layout.local_experts
    vmem = pl.BlockSpec(memory_space=pltpu.VMEM)
    hbm = pl.BlockSpec(memory_space=pl.ANY)
    dma = pltpu.SemaphoreType.DMA
    low, f32 = part.dtype, jnp.float32
    with_out = chips == 4
    return pl.pallas_call(
        functools.partial(back_kernel, layout, ranks, peers, with_out),
        out_shape=(
            jax.ShapeDtypeStruct((block, width), low),
            jax.ShapeDtypeStruct((rows, width), f32),
            jax.ShapeDtypeStruct((small_rows, width), f32),
            jax.ShapeDtypeStruct((block, width), low),
            jax.ShapeDtypeStruct((experts, layout.expert_hidden, width), low),
            jax.ShapeDtypeStruct((experts, layout.expert_hidden, width), low),
            jax.ShapeDtypeStruct((experts, layout.expert_hidden, width), low),
            jax.ShapeDtypeStruct((3, layout.shared_own, width), low),
        ),
        in_specs=[hbm, hbm] + [vmem] * 3 + [hbm] * 4,
        out_specs=(hbm, vmem, vmem, vmem, hbm, hbm, hbm, hbm),
        scratch_shapes=[
            pltpu.VMEM((peers, rows, width), low),
            pltpu.VMEM((peers - 1, rows, width), low),
            pltpu.VMEM((rows, width), low),
            pltpu.VMEM((total, width), low),
            pltpu.VMEM((total, hidden), low),
            pltpu.VMEM((hidden, total), low),
            pltpu.VMEM((2, layout.shared_at, 256), low),
            pltpu.VMEM((2, layout.shared_own, 256), low),
            pltpu.VMEM((1, width), f32),
            dma((peers - 1,)),
            dma((peers - 1,)),
            dma((peers - 1,)),
            dma((peers - 1,)),
            dma,
            dma,
            dma,
            dma((2 * (experts + 1),)),
        ]
        + (reduce_buffers(peers, chips, rows, width, low) + reduce_sems(peers, chips))
        * (1 + with_out),
        compiler_params=pltpu.CompilerParams(
            collective_id=identity, has_side_effects=True, vmem_limit_bytes=62 << 20
        ),
        name="reduce_and_norm",
    )(part, out_part, middle, cotangent, gain, x_all, cot_all, grads, scaled)


def final_kernel(
    layout,
    ranks,
    peers,
    part_ref,
    out_sum_ref,
    middle_ref,
    tokens_ref,
    gain_ref,
    grad_ref,
    small_ref,
    qkv_ref,
    proj_ref,
    shared_ref,
    input_ref,
    output_ref,
    qkv_sum_ref,
    proj_sum_ref,
    small_sum_ref,
    shared_got_ref,
    z_got,
    o_got,
    low_ref,
    out_low,
    small_own,
    small_got,
    small_part,
    small_z,
    kept,
    z_sends,
    z_recvs,
    o_sends,
    o_recvs,
    x_sends,
    x_recvs,
    y_sends,
    y_recvs,
    g_sends,
    g_recvs,
    h_sends,
    h_recvs,
    s_sends,
    s_recvs,
    local_sem,
    *refs,
):
    ring = Ring(ranks)
    here = lax.axis_index("tensor")
    block, width = part_ref.shape
    rows = block // peers
    half = ring.half
    pieces = refs[0].shape[0]
    lot, size = qkv_sum_ref.shape[0], refs[0].shape[2]
    proj_size = refs[8].shape[2]
    columns = width // ranks
    away = [(here + k) % peers for k in range(peers)]
    others = [(ring.me + k) % ranks for k in range(ranks)]
    greet(
        [{"dp": others[k]} for k in range(1, ranks)] + [{"tensor": away[k]} for k in range(1, peers)]
    )
    far_first = near_first(peers)[:0:-1]

    def to_peers(source_of, target_of, sends, recvs):
        copies = []
        for k in far_first:
            slot = peers - k - 1
            copy = remote(source_of(k), target_of(slot), "tensor", away[k], sends, recvs, slot)
            copy.start()
            copies.append(copy)
        return copies

    exchanged = to_peers(
        lambda k: part_ref.at[pl.ds(away[k] * rows, rows)], lambda slot: z_got.at[slot], z_sends, z_recvs
    )
    summed = to_peers(
        lambda k: out_sum_ref.at[pl.ds(away[k] * rows, rows)],
        lambda slot: o_got.at[slot],
        o_sends,
        o_recvs,
    )

    def slice_of(device):
        return pl.ds(pl.multiple_of(device * columns, columns), columns)

    works = []
    for piece in range(pieces):

        def qkv_at(device, piece=piece):
            return qkv_ref.at[pl.ds(device * lot + piece * size, size)]

        def proj_at(device, piece=piece):
            return proj_ref.at[pl.ds(piece * proj_size, proj_size), slice_of(device)]

        works.append(RingReduce(ring, qkv_at, size, refs[0:3], refs[3:8], piece))
        works.append(RingReduce(ring, proj_at, proj_size, refs[8:11], refs[11:16], piece))
    for offset in works[0].order:
        for work in works:
            work.hand_over(offset)
    shared = []
    for k in range(1, ranks):
        copy = remote(
            shared_ref.at[:, :, slice_of(others[k])],
            shared_got_ref.at[ring.me],
            "dp",
            others[k],
            s_sends,
            s_recvs,
            ranks - k - 1,
        )
        copy.start()
        shared.append(copy)
    keep = pltpu.make_async_copy(shared_ref.at[:, :, slice_of(ring.me)], kept, local_sem.at[0])
    keep.start()
    for number in range(half):
        for work in works:
            work.step(number)
    keep.wait()
    keep = pltpu.make_async_copy(kept, shared_got_ref.at[ring.me], local_sem.at[0])
    keep.start()

    first = here * rows
    small_own[...] = small_ref[...]
    spot_row = layout.expert_count + 1

    def norm(spot, start, count):
        mine = pl.ds(pl.multiple_of(first + start, count), count)
        value = part_ref[mine, :].astype(jnp.float32)
        for k in range(peers - 1):
            value = value + z_got[k, spot, :].astype(jnp.float32)
        inputs = tokens_ref[mine, :].astype(jnp.float32)
        inverse = lax.rsqrt(jnp.mean(inputs * inputs, axis=-1, keepdims=True) + EPSILON)
        normed = inputs * inverse
        scaled = value * gain_ref[...]
        back = inverse * (scaled - normed * jnp.mean(scaled * normed, axis=-1, keepdims=True))
        low_ref[spot, :] = (grad_ref[spot, :] + back).astype(low_ref.dtype)
        small_own[spot_row : spot_row + 1, :] += jnp.sum(value * normed, axis=0, keepdims=True)

    for copy in exchanged:
        copy.wait_recv()
    strips(rows, norm)
    mine = input_ref.at[pl.ds(here * rows, rows)]
    spread = to_peers(lambda k: low_ref, lambda slot: mine, x_sends, x_recvs)
    stores = [pltpu.make_async_copy(low_ref, mine, local_sem.at[1])]
    stores[0].start()
    handed = []
    for k in range(1, ranks):
        copy = remote(
            small_own.at[:, slice_of(others[k])],
            small_got.at[ranks - k - 1],
            "dp",
            others[k],
            g_sends,
            g_recvs,
            ranks - k - 1,
        )
        copy.start()
        handed.append(copy)

    def finish_rows(spot, start, count):
        there = pl.ds(pl.multiple_of(first + start, count), count)
        value = out_sum_ref[there, :].astype(jnp.float32)
        for k in range(peers - 1):
            value = value + o_got[k, spot, :].astype(jnp.float32)
        out_low[spot, :] = (middle_ref[spot, :] + value).astype(out_low.dtype)

    for copy in summed:
        copy.wait_recv()
    strips(rows, finish_rows)
    out_mine = output_ref.at[pl.ds(here * rows, rows)]
    spread += to_peers(lambda k: out_low, lambda slot: out_mine, y_sends, y_recvs)
    stores.append(pltpu.make_async_copy(out_low, out_mine, local_sem.at[2]))
    stores[1].start()
    for piece in range(pieces):

        def emit_qkv(spot, start, count, value, piece=piece):
            qkv_sum_ref[pl.ds(pl.multiple_of(piece * size + start, count), count), :] = value

        def emit_proj(spot, start, count, value, piece=piece):
            proj_sum_ref[pl.ds(pl.multiple_of(piece * proj_size + start, count), count), :] = value

        works[2 * piece].total(emit_qkv)
        works[2 * piece + 1].total(emit_proj)
    for copy in handed:
        copy.wait_recv()
    value = small_own[:, slice_of(ring.me)]
    for k in range(ranks - 1):
        value = value + small_got[k]
    small_part[...] = value
    last = to_peers(lambda k: small_part, lambda slot: small_z.at[slot], h_sends, h_recvs)
    for copy in last:
        copy.wait_recv()
    value = small_part[...]
    for k in range(peers - 1):
        value = value + small_z[k]
    small_sum_ref[...] = value
    keep.wait()
    for copy in stores:
        copy.wait()
    for copy in exchanged + summed + handed + last:
        copy.wait_send()
    for copy in shared + spread:
        copy.wait()
    for work in works:
        work.finish()


def finish_grads(
    layout,
    part,
    out_sum,
    middle,
    tokens,
    gain,
    grad,
    small,
    grad_qkv,
    grad_proj,
    shared_grads,
    ranks,
    peers,
    identity,
):
    chips = ranks // 2
    block, width = part.shape
    rows = block // peers
    lot, wide = grad_qkv.shape[0] // ranks, grad_qkv.shape[1]
    columns = width // ranks
    height = grad_proj.shape[0]
    pieces = 4
    small_rows = small.shape[0]
    own = layout.shared_own
    vmem = pl.BlockSpec(memory_space=pltpu.VMEM)
    hbm = pl.BlockSpec(memory_space=pl.ANY)
    low, f32 = part.dtype, jnp.float32
    dma = pltpu.SemaphoreType.DMA
    return pl.pallas_call(
        functools.partial(final_kernel, layout, ranks, peers),
        out_shape=(
            jax.ShapeDtypeStruct((block, width), low),
            jax.ShapeDtypeStruct((block, width), low),
            jax.ShapeDtypeStruct((lot, wide), f32),
            jax.ShapeDtypeStruct((height, columns), f32),
            jax.ShapeDtypeStruct((small_rows, columns), f32),
            jax.ShapeDtypeStruct((ranks, 3, own, columns), low),
        ),
        in_specs=[vmem] * 7 + [hbm] * 3,
        out_specs=(hbm, hbm, vmem, vmem, vmem, hbm),
        scratch_shapes=[
            pltpu.VMEM((peers - 1, rows, width), low),
            pltpu.VMEM((peers - 1, rows, width), low),
            pltpu.VMEM((rows, width), low),
            pltpu.VMEM((rows, width), low),
            pltpu.VMEM((small_rows, width), f32),
            pltpu.VMEM((ranks - 1, small_rows, columns), f32),
            pltpu.VMEM((small_rows, columns), f32),
            pltpu.VMEM((peers - 1, small_rows, columns), f32),
            pltpu.VMEM((3, own, columns), low),
        ]
        + [dma((peers - 1,))] * 8
        + [dma((ranks - 1,))] * 2
        + [dma((peers - 1,))] * 2
        + [dma((ranks - 1,))] * 2
        + [dma((3,))]
        + reduce_buffers(pieces, chips, lot // pieces, wide, low)
        + reduce_sems(pieces, chips)
        + reduce_buffers(pieces, chips, height // pieces, columns, low)
        + reduce_sems(pieces, chips),
        compiler_params=pltpu.CompilerParams(
            collective_id=identity, has_side_effects=True, vmem_limit_bytes=60 << 20
        ),
        name="finish_grads",
    )(part, out_sum, middle, tokens, gain, grad, small, grad_qkv, grad_proj, shared_grads)


def dot_rows(left, right):
    return lax.dot_general(
        left, right, (((0,), (0,)), ((), ())), preferred_element_type=jnp.float32
    )


def dot_last(left, right):
    return lax.dot_general(
        left, right, (((1,), (1,)), ((), ())), preferred_element_type=jnp.float32
    )


def rope_tables():
    half_dim = HEAD_DIM // 2
    exponent = np.arange(half_dim, dtype=np.float32) * np.float32(2.0 / HEAD_DIM)
    inverse_freq = np.exp(-exponent * np.log(np.float32(1000000.0)))
    angles = np.arange(SEQ, dtype=np.float32)[:, None] * inverse_freq[None, :]
    cosine, sine = np.cos(angles), np.sin(angles)
    return (
        jnp.asarray(np.concatenate([cosine, cosine], axis=1)),
        jnp.asarray(np.concatenate([-sine, sine], axis=1)),
    )


def rotate_back(values, cosine, sine):
    swapped = jnp.roll(values, HEAD_DIM // 2, axis=-1)
    return values * cosine[:, None, :] - swapped * sine[:, None, :]


def attend_backward(queries, key_rows, value_rows, probs, grad_context):
    probs_low = probs.astype(jnp.bfloat16)
    grad_probs = jnp.einsum(
        "qhd,khd->hqk", grad_context, value_rows, preferred_element_type=jnp.float32
    )
    inner = jnp.sum(probs * grad_probs, axis=-1, keepdims=True)
    grad_scores = (probs * (grad_probs - inner)).astype(jnp.bfloat16)
    grad_queries = jnp.einsum(
        "hqk,khd->qhd", grad_scores, key_rows, preferred_element_type=jnp.float32
    ) * HEAD_DIM ** (-0.5)
    grad_keys = jnp.einsum(
        "hqk,qhd->khd", grad_scores, queries, preferred_element_type=jnp.float32
    ) * HEAD_DIM ** (-0.5)
    grad_values = jnp.einsum(
        "hqk,qhd->khd", probs_low, grad_context, preferred_element_type=jnp.float32
    )
    return (grad_queries, grad_keys, grad_values)


def scatter_rows(values):
    return lax.psum_scatter(values, "dp", scatter_dimension=0, tiled=True)


def shards(
    tokens,
    w_query,
    w_key,
    w_value,
    w_out,
    gain_attn,
    gain_ffn,
    w_router,
    shared_gate,
    shared_up,
    shared_down,
    shared_switch,
    expert_gate,
    expert_up_weight,
    expert_down,
    routes,
    segments,
    cotangent,
):
    low = jnp.bfloat16
    ranks = lax.axis_size("dp")
    peers = lax.axis_size("tensor")
    me = lax.axis_index("dp")
    token_count, width = tokens.shape
    local_experts, _, expert_hidden = expert_gate.shape
    expert_count = local_experts * ranks
    block = width // ranks
    head_width = w_query.shape[1]
    head_count = head_width // HEAD_DIM
    shared_width = shared_gate.shape[1]
    shared_own = shared_width // ranks
    small_pad = 128
    layout = Layout(local_experts, expert_hidden, shared_own, expert_count)
    lane0 = layout.router_lane

    small_rows = -(-(expert_count + 3) // 16) * 16
    spots = jnp.arange(small_pad, dtype=jnp.int32)[None, None, :] - lane0
    chosen = jnp.sum((routes[:, :, None] == spots).astype(jnp.float32), axis=1).astype(low)
    fold = token_count // block
    chosen = chosen.reshape(fold, block, small_pad).transpose(1, 0, 2).reshape(block, fold * small_pad)
    vectors = jnp.stack([shared_switch, gain_attn, gain_ffn])
    cosine, sine = rope_tables()
    spots = jnp.arange(SEQ, dtype=jnp.int32)
    allowed = (spots[None, :] <= spots[:, None]) & (segments[0][None, :] == segments[0][:, None])

    (
        qkv_full,
        columns_full,
        attn_in,
        queries,
        key_rows,
        value_rows,
        context_flat,
        probs,
        x_all,
        cot_all,
        middle,
        scaled_hidden,
        grads_wide,
        out_part,
        back_part,
    ) = layer_forward_back(
        layout,
        w_query,
        w_key,
        w_value,
        chosen,
        w_out,
        w_router.T,
        vectors,
        tokens,
        cotangent,
        allowed.astype(jnp.float32),
        cosine,
        sine,
        expert_gate.swapaxes(1, 2),
        expert_up_weight.swapaxes(1, 2),
        expert_down,
        shared_gate.T.reshape(ranks, shared_own, block),
        shared_up.T.reshape(ranks, shared_own, block),
        shared_down.reshape(ranks, shared_own, block),
        small_rows,
        ranks,
        peers,
        1,
    )
    qkv_full = qkv_full[:, : 3 * head_width]
    out_full = columns_full[small_rows:]
    attn_gain = columns_full[expert_count + 1].astype(jnp.float32)
    ffn_gain = columns_full[expert_count + 2].astype(jnp.float32)
    grad_attn_out, grad_middle, grad_small, out_sum, *grad_experts, grad_shared = reduce_and_norm(
        layout,
        back_part,
        out_part,
        middle,
        cotangent,
        ffn_gain[None, :],
        x_all,
        cot_all,
        grads_wide,
        scaled_hidden,
        small_rows,
        ranks,
        peers,
        2,
    )
    if ranks != 8:
        out_sum = scatter_rows(out_part)
    grad_experts = [grads.astype(jnp.float32) for grads in grad_experts]

    grad_proj = dot_rows(context_flat, grad_attn_out).astype(low)
    grad_context = dot_last(grad_attn_out, out_full)
    shape_three = (SEQ, head_count, HEAD_DIM)
    grad_queries, grad_keys, grad_values = attend_backward(
        queries.reshape(shape_three),
        key_rows.reshape(shape_three),
        value_rows.reshape(shape_three),
        probs,
        grad_context.astype(low).reshape(shape_three),
    )
    flat_shape = (token_count, head_width)
    grad_qkv_rows = jnp.concatenate(
        [
            rotate_back(grad_queries, cosine, sine).reshape(flat_shape).astype(low),
            rotate_back(grad_keys, cosine, sine).reshape(flat_shape).astype(low),
            grad_values.reshape(flat_shape).astype(low),
        ],
        axis=1,
    )
    grad_qkv = dot_rows(attn_in, grad_qkv_rows)
    attn_back_part = dot_last(grad_qkv_rows, qkv_full)
    grad_input, output, grad_qkv, grad_proj, grad_small, grad_shared = finish_grads(
        layout,
        attn_back_part.astype(low),
        out_sum,
        middle,
        tokens,
        attn_gain[None, :],
        grad_middle,
        grad_small,
        grad_qkv.astype(low),
        grad_proj,
        grad_shared,
        ranks,
        peers,
        3,
    )
    grad_shared = grad_shared.astype(jnp.float32)
    return (
        output,
        grad_input.astype(jnp.float32),
        grad_qkv[:, :head_width],
        grad_qkv[:, head_width : 2 * head_width],
        grad_qkv[:, 2 * head_width :],
        grad_proj,
        grad_small[expert_count + 1],
        grad_small[expert_count + 2],
        grad_small[:expert_count].T,
        grad_shared[:, 0].reshape(shared_width, block).T,
        grad_shared[:, 1].reshape(shared_width, block).T,
        grad_shared[:, 2].reshape(shared_width, block),
        grad_small[expert_count],
        grad_experts[0].swapaxes(1, 2),
        grad_experts[1].swapaxes(1, 2),
        grad_experts[2],
    )


def solution(mesh):
    in_specs = (
        P("dp", None),
        P("dp", "tensor"),
        P("dp", "tensor"),
        P("dp", "tensor"),
        P("tensor", "dp"),
        P("dp"),
        P("dp"),
        P("dp", None),
        P("dp", "tensor"),
        P("dp", "tensor"),
        P("tensor", "dp"),
        P("dp"),
        P("dp", None, "tensor"),
        P("dp", None, "tensor"),
        P("dp", "tensor", None),
        P("dp", None),
        P("dp", None),
        P("dp", None),
    )
    out_specs = (
        P("dp", None),
        P("dp", None),
        P("dp", "tensor"),
        P("dp", "tensor"),
        P("dp", "tensor"),
        P("tensor", "dp"),
        P("dp"),
        P("dp"),
        P("dp", None),
        P("dp", "tensor"),
        P("dp", "tensor"),
        P("tensor", "dp"),
        P("dp"),
        P("dp", None, "tensor"),
        P("dp", None, "tensor"),
        P("dp", "tensor", None),
    )
    return jax.shard_map(shards, mesh=mesh, in_specs=in_specs, out_specs=out_specs, check_vma=False)
```

time: 613 us -> 452 us (0.74)
  local copies, waits for them, and re-layouts: 90.8 us -> 20.7 us
  matrix products: 64.6 us -> 16.3 us
  other arithmetic: 34.1 us -> 18.4 us
  between operations: 14.7 us -> 0.86 us
  waiting for transfers between devices: 12.7 us -> 0 us
  Pallas kernels: 385 us -> 395 us
    dot_general x4 -> x2, matrix products: 45.5 us -> 6.57 us  [dot_rows(): lax.dot_general(left, right, (((0,), (0,)), ((), ())), preferred_element_...]
    unnamed x78 -> x32, local copies, waits for them, and re-layouts: 28.8 us -> 3.97 us
    concatenate x4 -> x0, local copies, waits for them, and re-layouts: 18.1 us -> none  [the longest x1 13.7 us: shards(): jnp.concatenate([grad_qkv.astype(low), grad_out_rows.astype(low), pad_col...]
    pallas_call x1, Pallas kernels: 191 us -> 208 us  [layer_forward_back(): pl.pallas_call(functools.partial(layer_kernel, layout, ranks, peers), out...]
    dot_general x1 -> x0, local copies, waits for them, and re-layouts: 14 us -> none  [dot_rows(): lax.dot_general(left, right, (((0,), (0,)), ((), ())), preferred_element_...]
    another operation x4 -> x1, other arithmetic: 13.3 us -> 0.59 us  [shards(): vectors = jnp.stack([shared_switch, gain_attn, gain_ffn])]
    all_gather x1 -> x0, waiting for transfers between devices: 12.6 us -> none  [shards(): output = lax.all_gather(output, 'tensor', axis=0, tiled=True)]
    dot_general x4 -> x0, matrix products: 7.82 us -> none  [the longest x1 4.61 us: shards(): qkv = jnp.dot(attn_in, qkv_full, preferred_element_type=jnp.float32)]
  transfers between devices with their start and end apart: 4 -> 0, of which waited for: 1 -> 0; matrix products, arithmetic and copies ran while one was open for 24% -> 0% of each run, Pallas kernels for 14% -> 0%
where the time goes in v3:
time: 452 us; the launch traced here: 451 us
  Pallas kernels  395 us (87%)
  local copies, waits for them, and re-layouts  20.7 us (5%)
  other arithmetic  18.4 us (4%)
  matrix products  16.3 us (4%)
    pallas_call x1, Pallas kernels, layer_forward_back(): pl.pallas_call(functools.partial(layer_kernel, layout, ranks, peers), out...  208 us
    pallas_call x1, Pallas kernels, finish_grads(): pl.pallas_call(functools.partial(final_kernel, layout, ranks, peers), out...  104 us
    pallas_call x1, Pallas kernels, reduce_and_norm(): pl.pallas_call(functools.partial(back_kernel, layout, ranks, peers, with_...  82.9 us

profile of v3, /device:TPU:0, one launch (start us, length us, event | category | flops | bytes accessed | tf_op | source)
XLA Modules:
  0.0 451.5 jit_solution(4655167187814804657)
XLA Ops:
  0.6 0.0 copy-start.8
  0.7 0.7 stack.13
  1.4 0.7 stack.14
  2.1 0.7 stack.12
  2.7 0.6 pad_maximum_fusion.3.vectors_ref
  3.3 1.5 convert_reduce_fusion.chosen_own_ref
  4.8 1.6 fusion.19.allowed_ref
  6.4 2.2 copy.49
  8.6 0.0 copy-done.8
  8.6 1.1 copy.50
  9.8 208.0 %layer_forward_back.1 = (bf16[2048,1664]{1,0:T(8,128)(2,1)}, bf16[544,2048]{1,0:T(8,128)(2,1)}, bf16[256,2048]{1,0:T(8,128)(2,1)}, bf16[256,512]{1,0:T(8,128)(2,...) custom-call(bf16[256,512]{1,0:T(8,128)(2,1)} %query_ref.1, ...), custom_call_target="tpu_custom_call" | custom-call | tf_op jit(solution)/shard_map/layer_forward_back/pallas_call | solution.py:786
  217.8 1.1 copy.62
  218.9 1.4 slice_convert_fusion
  220.3 82.9 %reduce_and_norm.1 = (bf16[256,2048]{1,0:T(8,128)(2,1)}, f32[64,2048]{1,0:T(8,128)}, f32[32,2048]{1,0:T(8,128)}, bf16[256,2048]{1,0:T(8,128)(2,1)}, bf16[2,352,2...) custom-call(bf16[2048,2048]{1,0:T(8,128)(2,1)} %get-tuple-element.47, ...), custom_call_target="tpu_custom_call" | custom-call | tf_op jit(solution)/shard_map/reduce_and_norm/pallas_call | solution.py:1253
  303.2 0.0 copy-start
  303.2 0.0 copy-start.12
  303.2 2.8 fusion.7
  306.0 0.0 copy-start.11
  306.0 0.1 copy.64
  306.1 0.0 copy-done
  306.1 0.2 convolution_convert_fusion.2
  306.4 0.0 copy-done.12
  306.4 0.1 copy.63
  306.5 0.4 copy-done.11
  306.9 0.4 multiply_reduce_fusion
  307.4 0.2 multiply_convert_fusion
  307.6 0.2 broadcast_multiply_fusion
  307.9 0.0 copy-start.13
  307.9 0.0 copy-start.14
  307.9 0.3 broadcast_multiply_fusion.1
  308.2 0.1 fusion.24
  308.3 0.5 copy-done.13
  308.8 0.1 copy-done.14
  308.8 0.2 fusion.11
  309.1 0.0 copy-start.7
  309.1 0.0 copy-start.9
  309.1 5.7 %fusion.2.part_ref = bf16[256,2048]{1,0:T(8,128)(2,1)} fusion(bf16[2048,1664]{1,0:T(8,128)(2,1)} %get-tuple-element.58, bf16[256,512]{0,1:T(8,128)(2,1)S(1)} %bitcast.67, bf16[256,512]{0,1:T(8,128)(2,1)S(1)} %bitcast.71, bf16[256,512]{0,1:T(8,128)(2,1)S(1)} %bitcast.69), kind=kOutput, calls=%fused_computation.6 | convolution fusion | flops 1613496320 | bytes 8126464 | tf_op jit(solution)/shard_map/dot_general | solution.py:1576
  314.8 0.0 copy-done.7
  314.8 0.0 copy-done.9
  314.8 0.0 copy-start.4
  314.8 2.1 convolution_convert_fusion.1.proj_ref
  316.9 0.0 copy-done.4
  316.9 4.5 %convolution_convert_fusion.qkv_ref = bf16[2048,1536]{1,0:T(8,128)(2,1)} fusion(bf16[256,2048]{1,0:T(8,128)(2,1)S(1)} %copy-done.4, bf16[256,512]{0,1:T(8,128)(2,1)S(1)} %bitcast.68, bf16[256,512]{0,1:T(8,128)(2,1)S(1)} %bitcast.72, bf16[256,512]{0,1:T(8,128)(2,1)S(1)} %bitcast.70), kind=kOutput, calls=%fused_computation | convolution fusion | flops 1616117760 | bytes 8126464 | tf_op jit(solution)/shard_map/dot_general | solution.py:1570
  321.4 104.4 %finish_grads.1 = (bf16[256,2048]{1,0:T(8,128)(2,1)}, bf16[256,2048]{1,0:T(8,128)(2,1)}, f32[256,1536]{1,0:T(8,128)}, f32[512,256]{1,0:T(8,128)}, f32[32,256]{1,0:T(8,128)}, /*index=5*/bf16[8,3,176,256]{3,2,1,0:T(8,128)(2,1)}) custom-call(bf16[256,2048]{1,0:T(8,128)(2,1)} %fusion.2.part_ref, bf16[256,2048]{1,0:T(8,128)(2,1)} %get-tuple-element.59.out_sum_ref, ...), custom_call_target="tpu_custom_call" | custom-call | tf_op jit(solution)/shard_map/finish_grads/pallas_call | solution.py:1530
  425.8 0.0 copy-start.5
  425.8 1.4 fusion.26
  427.2 1.3 slice_bitcast_fusion
  428.5 2.5 fusion.23
  431.0 0.0 copy-start.1
  431.0 0.0 copy-done.5
  431.0 1.6 convert_element_type.85
  432.6 0.8 copy-done.1
  433.4 1.6 fusion.22
  435.0 1.5 copy.60
  436.5 1.5 copy.59
  438.1 0.0 copy-start.2
  438.1 5.3 %convert_element_type.87 = f32[2,352,2048]{2,1,0:T(8,128)} convert(bf16[2,352,2048]{2,1,0:T(8,128)(2,1)} %get-tuple-element.73) | non-fusion elementwise | flops 1441792 | bytes 8650752 | tf_op jit(solution)/shard_map/convert_element_type | solution.py:1730
  443.3 0.0 copy-done.2
  443.3 0.0 copy-done.3
  443.3 5.9 %convert_bitcast_fusion = (f32[2,2048,352]{1,2,0:T(8,128)}, f32[2,2048,352]{1,2,0:T(8,128)}) fusion(bf16[2,352,2048]{2,1,0:T(8,128)(2,1)S(1)} %copy-done.3, bf16[2,352,2048]{2,1,0:T(8,128)(2,1)S(1)} %copy-done.2), kind=kLoop, calls=%fused_computation.3 | loop fusion | flops 2883584 | bytes 17301504 | tf_op jit(solution)/shard_map/transpose | solution.py:1785
  449.3 0.0 copy-done.6
  449.3 1.0 copy.74
  450.3 0.4 copy-done.10
  450.7 0.8 copy.75
  (4 shorter events, 0.0 us)
Async XLA Ops:
  0.6 8.0 %copy-start.8 = (bf16[256,1408]{1,0:T(8,128)(2,1)S(1)}, bf16[256,1408]{1,0:T(8,128)(2,1)}, u32[]{:S(2)}) copy-start(bf16[256,1408]{1,0:T(8,128)(2,1)} %param.29) | copy-start | bytes 2162692
  303.2 2.9 copy-start
  303.2 3.2 copy-start.12
  306.0 1.0 copy-start.11
  307.9 0.9 copy-start.13
  307.9 1.0 copy-start.14
  309.1 5.7 %copy-start.7 = (bf16[256,2048]{1,0:T(8,128)(2,1)S(1)}, bf16[256,2048]{1,0:T(8,128)(2,1)}, u32[]{:S(2)}) copy-start(bf16[256,2048]{1,0:T(8,128)(2,1)} %get-tuple-element.55) | copy-start | bytes 3145732
  309.1 5.7 %copy-start.9 = (bf16[256,512]{1,0:T(8,128)(2,1)S(1)}, bf16[256,512]{1,0:T(8,128)(2,1)}, u32[]{:S(2)}) copy-start(bf16[256,512]{1,0:T(8,128)(2,1)} %get-tuple-element.63) | copy-start | bytes 786436
  314.8 2.1 copy-start.4
  425.8 5.3 %copy-start.5 = (bf16[256,2048]{1,0:T(8,128)(2,1)S(1)}, bf16[256,2048]{1,0:T(8,128)(2,1)}, u32[]{:S(2)}) copy-start(bf16[256,2048]{1,0:T(8,128)(2,1)} %get-tuple-element.66) | copy-start | bytes 3145732
  431.0 2.4 copy-start.1
  438.1 5.3 %copy-start.2 = (bf16[2,352,2048]{2,1,0:T(8,128)(2,1)S(1)}, bf16[2,352,2048]{2,1,0:T(8,128)(2,1)}, u32[]{:S(2)}) copy-start(bf16[2,352,2048]{2,1,0:T(8,128)(2,1)} %get-tuple-element.71) | copy-start | bytes 8650756
  438.1 5.3 %copy-start.3 = (bf16[2,352,2048]{2,1,0:T(8,128)(2,1)S(1)}, bf16[2,352,2048]{2,1,0:T(8,128)(2,1)}, u32[]{:S(2)}) copy-start(bf16[2,352,2048]{2,1,0:T(8,128)(2,1)} %get-tuple-element.72) | copy-start | bytes 8650756
  443.3 5.9 %copy-start.6 = (bf16[256,2048]{1,0:T(8,128)(2,1)S(1)}, bf16[256,2048]{1,0:T(8,128)(2,1)}, u32[]{:S(2)}) copy-start(bf16[256,2048]{1,0:T(8,128)(2,1)} %get-tuple-element.117) | copy-start | bytes 3145732
  449.3 1.4 copy-start.10

commit v4 on v3

--- a/solution.py
+++ b/solution.py
@@ -166,7 +166,7 @@
 
 
 STRIP = 64
-OUT_FIRST, OUT_NEXT, NORM_DUE = 10, 13, 15
+OUT_DUE, NORM_DUE = 10, 15
 
 
 def strips(rows, body):
@@ -177,6 +177,9 @@
         return carry
 
     lax.fori_loop(0, rows // strip, step, 0)
+
+
+HIDDEN_TILE, OUT_TILE, BACK_TILE = 1024, 1024, 1024
 
 
 def matmul(left, right):
@@ -212,7 +215,7 @@
         self.hidden = self.shared_at + self.last
         self.router_tile = self.router_at // 128 * 128
         self.router_lane = self.router_at - self.router_tile
-        self.tile = 256 if self.hidden % 256 == 0 else 128
+        self.tile = next(size for size in (HIDDEN_TILE, 256, 128) if self.hidden % size == 0)
 
 
 def hidden_tiles(layout, x_ref, gates, ups, pre_gate, pre_up):
@@ -225,7 +228,7 @@
 
 def cot_tiles(layout, cot_ref, downs, cot_hidden):
     def body(spot):
-        cot_hidden[:, spot] = matmul_last(cot_ref[...], downs[spot, :])
+        cot_hidden[:, spot] = matmul_last(cot_ref[...], downs[spot, :]).astype(cot_hidden.dtype)
 
     tiles(layout.hidden, layout.tile, body)
 
@@ -285,7 +288,7 @@
     def body(spot):
         out[:, spot] = matmul(scaled[...], downs[:, spot]).astype(out.dtype)
 
-    tiles(width, 256, body)
+    tiles(width, OUT_TILE, body)
 
 
 def back_tiles(layout, width, grads, gates, ups, back):
@@ -296,7 +299,7 @@
         total = total + matmul(grads[:, hidden:], ups[:, spot])
         back[:, spot] = total.astype(back.dtype)
 
-    tiles(width, 256, body)
+    tiles(width, BACK_TILE, body)
 
 
 def rope(values, cosine, sine, sign):
@@ -481,6 +484,29 @@
         for gather in gathers:
             gather.step(number)
 
+    experts, hid = layout.local_experts, layout.expert_hidden
+    wides = (gates, ups, downs)
+    loads = []
+    for which, (target, source) in enumerate(
+        zip(wides, (expert_gate_ref, expert_up_ref, expert_down_ref))
+    ):
+        for j in range(experts):
+            load = pltpu.make_async_copy(
+                source.at[j],
+                target.at[pl.ds(j * layout.part, hid)],
+                local_sem.at[5 + which * experts + j],
+            )
+            load.start()
+            loads.append(load)
+            if layout.part > hid:
+                target[j * layout.part + hid : (j + 1) * layout.part, :] = jnp.zeros(
+                    (layout.part - hid, width), low
+                )
+        target[layout.router_at :, :] = jnp.zeros((layout.hidden - layout.router_at, width), low)
+
+    for gather in gathers:
+        gather.step(half)
+
     shared_refs = (shared_gate_ref, shared_up_ref, shared_down_ref)
     handed, kept = [], []
     for k in range(1, ranks):
@@ -513,28 +539,6 @@
     kept_cot = pltpu.make_async_copy(cot_ref, cot_place(ring.me, 0, block), local_sem.at[3])
     kept_cot.start()
 
-    experts, hid = layout.local_experts, layout.expert_hidden
-    wides = (gates, ups, downs)
-    loads = []
-    for which, (target, source) in enumerate(
-        zip(wides, (expert_gate_ref, expert_up_ref, expert_down_ref))
-    ):
-        for j in range(experts):
-            load = pltpu.make_async_copy(
-                source.at[j],
-                target.at[pl.ds(j * layout.part, hid)],
-                local_sem.at[5 + which * experts + j],
-            )
-            load.start()
-            loads.append(load)
-            if layout.part > hid:
-                target[j * layout.part + hid : (j + 1) * layout.part, :] = jnp.zeros(
-                    (layout.part - hid, width), low
-                )
-        target[layout.router_at :, :] = jnp.zeros((layout.hidden - layout.router_at, width), low)
-
-    for gather in gathers:
-        gather.step(half)
     for store in stores_own:
         store.wait()
     for gather in gathers:
@@ -588,6 +592,31 @@
         )
         copy.start()
         exchanged.append(copy)
+
+    for copy in kept + loads:
+        copy.wait()
+    for copy in handed:
+        copy.wait_recv()
+    for which, target in enumerate(wides):
+        for source in range(ranks):
+            columns = slice(source * depth, (source + 1) * depth)
+            target[layout.shared_at : layout.router_at, columns] = shared_got[which, source]
+
+    chip_rows = 2 * block
+
+    def chip_spot(turn):
+        offset = (1 - 2 * (turn % 2)) * ((turn + 1) // 2)
+        return pl.ds(pl.multiple_of(ring.chip(offset) * chip_rows, chip_rows), chip_rows)
+
+    def cot_turn(turn, slot):
+        cots.wait_side(turn)
+        load_cot = pltpu.make_async_copy(cot_all.at[chip_spot(turn)], cot_block, block_sem.at[0])
+        load_cot.start()
+        load_cot.wait()
+        cot_tiles(layout, cot_block, downs, cot_hidden.at[slot])
+
+    kept_cot.wait()
+    cot_turn(0, 0)
 
     for copy in exchanged:
         copy.wait()
@@ -635,24 +664,18 @@
     store = pltpu.make_async_copy(own, mine, local_sem.at[4])
     store.start()
 
-    for copy in kept + loads:
-        copy.wait()
-    for copy in handed:
-        copy.wait_recv()
-    for which, target in enumerate(wides):
-        for source in range(ranks):
-            columns = slice(source * depth, (source + 1) * depth)
-            target[layout.shared_at : layout.router_at, columns] = shared_got[which, source]
-
-    for k in order[1:]:
+    for index, k in enumerate(order[1:]):
         spot = place_of(k)(ring.me, 0, rows)
         remote(own, spot, "tensor", away[k], x_sends, x_recvs, k - 1).wait_recv()
         works[k].begin(spot)
+        if index == 0:
+            cots.step(1)
+            cot_turn(1, 1)
+        if index == 1:
+            cot_turn(2, 2)
     store.wait()
-    kept_cot.wait()
-    passing = [cots] + [works[k] for k in order]
-    cuts = [part * len(passing) // 5 for part in range(6)]
-    chip_rows = 2 * block
+    passing = [works[k] for k in order]
+    cuts = [part * len(passing) // 4 for part in range(5)]
     first_expert = ring.me * experts
 
     def stores(spot):
@@ -665,19 +688,19 @@
 
     def chip_step(turn, carry):
         offset = (1 - 2 * (turn % 2)) * ((turn + 1) // 2)
-        spot = pl.ds(pl.multiple_of(ring.chip(offset) * chip_rows, chip_rows), chip_rows)
+        spot = chip_spot(turn)
+        slot = turn - turn // 4 * (turn - 3)
 
         def pass_on(part):
             for number in range(1, half + 1):
 
                 @pl.when(turn == 2 * number - 2)
                 def _(number=number):
+                    if part == 0 and number > 1:
+                        cots.step(number)
                     for work in passing[cuts[part] : cuts[part + 1]]:
                         work.step(number)
 
-        cots.wait_side(turn)
-        load_cot = pltpu.make_async_copy(cot_all.at[spot], cot_block, block_sem.at[0])
-        load_cot.start()
         for device in range(2):
             for fold in range(block // lot):
                 there = ring.chip(offset) * 2 * lot + device * lot
@@ -689,12 +712,14 @@
             work.wait_side(turn)
         load_x = pltpu.make_async_copy(x_all.at[spot], x_block, block_sem.at[1])
         load_x.start()
-        load_cot.wait()
-        cot_tiles(layout, cot_block, downs, cot_hidden)
-        pass_on(0)
         load_x.wait()
         hidden_tiles(layout, x_block, gates, ups, pre_gate, pre_up)
-        pass_on(1)
+        pass_on(0)
+
+        @pl.when(turn > 2)
+        def _():
+            cot_turn(turn, 3)
+
         pending = stores(spot)
 
         @pl.when(turn > 0)
@@ -708,13 +733,13 @@
             chosen,
             pre_gate,
             pre_up,
-            cot_hidden,
+            cot_hidden.at[slot],
             scaled,
             grads,
         )
         pending[0].start()
         pending[1].start()
-        pass_on(2)
+        pass_on(1)
 
         @pl.when(turn > 0)
         def _():
@@ -723,10 +748,10 @@
 
         out_tiles(width, scaled, downs, out)
         pending[2].start()
-        pass_on(3)
+        pass_on(2)
         back_tiles(layout, width, grads, gates, ups, back)
         pending[3].start()
-        pass_on(4)
+        pass_on(3)
         return carry
 
     lax.fori_loop(0, ring.chips, chip_step, 0)
@@ -818,7 +843,7 @@
             pltpu.VMEM((chip, width), low),
             pltpu.VMEM((chip, hidden), f32),
             pltpu.VMEM((chip, hidden), f32),
-            pltpu.VMEM((chip, hidden), f32),
+            pltpu.VMEM((4, chip, hidden), low),
             pltpu.VMEM((chip, hidden), low),
             pltpu.VMEM((chip, 2 * hidden), low),
             pltpu.VMEM((chip, width), low),
@@ -998,51 +1023,159 @@
     return [dma((pieces * chips,))] * 5
 
 
-def back_kernel(
+def attend_back(heads, queries, keys, values, probs_ref, grad_context, cos_ref, sin_ref, grads):
+    cosine, sine = cos_ref[...], sin_ref[...]
+    low = grads.dtype
+    scale = HEAD_DIM ** (-0.5)
+    for head in range(heads):
+        columns = slice(head * HEAD_DIM, (head + 1) * HEAD_DIM)
+        probs, through = probs_ref[head], grad_context[:, columns]
+        grad_probs = matmul_last(through, values[:, columns])
+        inner = jnp.sum(probs * grad_probs, axis=-1, keepdims=True)
+        grad_scores = (probs * (grad_probs - inner)).astype(low)
+        parts = (
+            rope(matmul(grad_scores, keys[:, columns]) * scale, cosine, sine, -1.0),
+            rope(matmul(grad_scores.T, queries[:, columns]) * scale, cosine, sine, -1.0),
+            matmul(probs.astype(low).T, through),
+        )
+        for index, part in enumerate(parts):
+            first = (index * heads + head) * HEAD_DIM
+            grads[:, first : first + HEAD_DIM] = part.astype(low)
+
+
+def rear_kernel(
     layout,
     ranks,
     peers,
     with_out,
     part_ref,
     out_part_ref,
-    middle_ref,
-    cot_ref,
-    gain_ref,
     x_ref,
     cots_ref,
     grads_ref,
     scaled_ref,
-    low_all_ref,
-    grad_ref,
-    small_ref,
-    out_sum_ref,
+    rows_all,
+    columns_all,
+    middle_ref,
+    cot_ref,
+    tokens_ref,
+    attn_in,
+    queries,
+    keys,
+    values,
+    context,
+    probs_ref,
+    cos_ref,
+    sin_ref,
+    input_ref,
+    output_ref,
+    qkv_sum_ref,
+    proj_sum_ref,
+    small_sum_ref,
     gate_grads_ref,
     up_grads_ref,
     down_grads_ref,
     shared_grads_ref,
+    shared_got_ref,
+    cot_rows,
+    token_rows,
+    small_vec,
+    grad_ref,
+    small_own,
+    small_got,
+    small_part,
+    small_z,
+    z_stage,
+    z_got,
+    a_got,
+    o_got,
+    low_ref,
+    gm_all,
+    right,
+    left,
+    turned,
+    product,
+    shared_low,
+    gain_grad,
+    qkv_full,
+    grad_context,
+    grad_rows,
+    attn_part,
+    out_sum,
+    kept,
+    z_sends,
+    z_recvs,
+    m_sends,
+    m_recvs,
+    a_sends,
+    a_recvs,
+    o_sends,
+    o_recvs,
+    x_sends,
+    x_recvs,
+    y_sends,
+    y_recvs,
+    h_sends,
+    h_recvs,
+    g_sends,
+    g_recvs,
+    s_sends,
+    s_recvs,
+    local_sem,
+    left_sem,
+    right_sem,
+    product_sem,
+    reuse_sem,
     *refs,
 ):
-    z_stage, z_got, low_ref, right, left, turned, product, experts_low, gain_grad = refs[:9]
-    z_sends, z_recvs, x_sends, x_recvs, local_sem, right_sem, left_sem, product_sem = refs[9:17]
-    back_buffers, back_sems = refs[17:20], refs[20:25]
-    out_buffers, out_sems = refs[25:28], refs[28:]
+    buffers = refs[0:3]
+    back_sems, qkv_sems, proj_buffers, proj_sems = refs[3:8], refs[8:13], refs[13:16], refs[16:21]
+    out_buffers, out_sems = refs[21:24], refs[24:]
+    out_low = z_stage.at[0]
     ring = Ring(ranks)
     here = lax.axis_index("tensor")
     block, width = cot_ref.shape
     rows = block // peers
     half = ring.half
+    low = low_ref.dtype
+    columns = width // ranks
+    hidden = layout.hidden
+    head_width = queries.shape[1]
+    heads = head_width // HEAD_DIM
+    small_rows = small_vec.shape[0]
     away = [(here + k) % peers for k in range(peers)]
-    greet(ring.partners() + [{"tensor": away[k]} for k in range(1, peers)])
+    others = [(ring.me + k) % ranks for k in range(ranks)]
+    greet(
+        [{"dp": others[k]} for k in range(1, ranks)] + [{"tensor": away[k]} for k in range(1, peers)]
+    )
+    first = here * rows
     order = list(reversed(near_first(peers)))
-    hidden = layout.hidden
-
-    def reducer(source, buffers, sems, k):
+    far_first = order[:-1]
+
+    def slice_of(device):
+        return pl.ds(pl.multiple_of(device * columns, columns), columns)
+
+    def to_peers(source_of, target_of, sends, recvs):
+        return [
+            remote(
+                source_of(k),
+                target_of(peers - k - 1),
+                "tensor",
+                away[k],
+                sends,
+                recvs,
+                peers - k - 1,
+            )
+            for k in far_first
+        ]
+
+    def reducer(source, where, sems, k):
         def source_at(device):
             return source.at[pl.ds(device * block + away[k] * rows, rows)]
 
-        return RingReduce(ring, source_at, rows, buffers, sems, k)
-
-    backs = {k: reducer(part_ref, back_buffers, back_sems, k) for k in order}
+        return RingReduce(ring, source_at, rows, where, sems, k)
+
+    backs = {k: reducer(part_ref, buffers, back_sems, k) for k in order}
     outs = {}
     if with_out:
         outs = {k: reducer(out_part_ref, out_buffers, out_sems, k) for k in order}
@@ -1050,391 +1183,281 @@
         for k in order:
             backs[k].hand_over(offset)
 
-    def fetch_right(source, slot):
-        return pltpu.make_async_copy(source, right, right_sem)
+    tile = right.shape[2]
+    blocks = width // tile
+    steps = 3 * blocks
 
     def fetch_left(wide):
         source = scaled_ref if wide == 2 else grads_ref.at[:, pl.ds(wide * hidden, hidden)]
         return pltpu.make_async_copy(source, left, left_sem)
 
-    fetch_right(x_ref, 0).start()
+    def fetch_right(step, late):
+        spot = pl.ds(pl.multiple_of(step % blocks * tile, tile), tile)
+        source = cots_ref if late else x_ref
+        return pltpu.make_async_copy(source.at[:, spot], right.at[step % 2], right_sem.at[step % 2])
+
+    fetch_right(0, False).start()
     fetch_left(0).start()
+    vec_load = pltpu.make_async_copy(columns_all.at[pl.ds(0, small_rows)], small_vec, local_sem.at[0])
+    vec_load.start()
+    row_loads = [
+        pltpu.make_async_copy(source.at[pl.ds(first, rows)], target, local_sem.at[slot])
+        for source, target, slot in ((cot_ref, cot_rows, 5), (tokens_ref, token_rows, 6))
+    ]
+    for load in row_loads:
+        load.start()
+    qkv_load = pltpu.make_async_copy(
+        rows_all.at[:, pl.ds(0, 3 * head_width)], qkv_full, local_sem.at[1]
+    )
+    qkv_load.start()
+    if not with_out:
+        out_load = pltpu.make_async_copy(out_part_ref, out_sum, local_sem.at[2])
+        out_load.start()
     for number in range(half):
         for k in order:
             backs[k].step(number)
     for offset in backs[0].order:
         for k in outs:
             outs[k].hand_over(offset)
+    vec_load.wait()
+    for load in row_loads:
+        load.wait()
+    count = layout.expert_count
+    vectors = small_vec[...].astype(jnp.float32)
+    attn_gain = vectors[count + 1 : count + 2, :]
+    ffn_gain = vectors[count + 2 : count + 3, :]
+
+    def z_copy(k):
+        slot = peers - k - 1
+        return remote(z_stage.at[k], z_got.at[slot], "tensor", away[k], z_sends, z_recvs, slot)
 
     def pass_z(k):
         def emit(spot, start, size, value):
-            z_stage[k, spot, :] = value.astype(z_stage.dtype)
+            z_stage[k, spot, :] = value.astype(low)
 
         backs[k].total(emit)
         z_copy(k).start()
 
-    def z_copy(k):
-        return remote(
-            z_stage.at[k], z_got.at[peers - k - 1], "tensor", away[k], z_sends, z_recvs, peers - k - 1
-        )
-
-    tile = 256
-    blocks = width // tile
-    steps = 3 * blocks
-
     def results(step, wide):
         slot = step % 2
-        columns = pl.ds(pl.multiple_of(step % blocks * tile, tile), tile)
+        spot = pl.ds(pl.multiple_of(step % blocks * tile, tile), tile)
+        base = slot * (layout.local_experts + 1)
         copies = [
             pltpu.make_async_copy(
                 product.at[slot, pl.ds(j * layout.part, layout.expert_hidden)],
-                (gate_grads_ref, up_grads_ref, down_grads_ref)[wide].at[j, :, columns],
-                product_sem.at[slot * (layout.local_experts + 1) + j],
+                (gate_grads_ref, up_grads_ref, down_grads_ref)[wide].at[j, :, spot],
+                product_sem.at[base + j],
             )
             for j in range(layout.local_experts)
         ]
         copies.append(
             pltpu.make_async_copy(
-                experts_low.at[slot],
-                shared_grads_ref.at[wide, :, columns],
-                product_sem.at[slot * (layout.local_experts + 1) + layout.local_experts],
+                shared_low.at[slot],
+                shared_grads_ref.at[wide, :, spot],
+                product_sem.at[base + layout.local_experts],
             )
         )
         return copies
 
-    def grad_step(step, carry):
-        wide, turn, slot = step // blocks, step % blocks, step % 2
-        for number in range(3):
-
-            @pl.when(step == number * blocks)
-            def _(number=number):
-                fetch_left(number).wait()
-                if number == 0:
-                    fetch_right(x_ref, 0).wait()
-
-                def turn_over(index, carry):
-                    spot = pl.ds(pl.multiple_of(index * tile, tile), tile)
-                    turned[:, spot] = left[spot, :].T
-                    return carry
-
-                lax.fori_loop(0, left.shape[0] // tile, turn_over, 0)
-                if number < 2:
-                    fetch_left(number + 1).start()
-                else:
-                    fetch_right(cots_ref, 0).start()
-                    fetch_right(cots_ref, 0).wait()
-
-        @pl.when(step > 1)
-        def _():
-            for copy in results(step, 0):
-                copy.wait()
-
-        columns = pl.ds(pl.multiple_of(turn * tile, tile), tile)
-        value = matmul(turned[...], right[:, columns])
-        product[slot] = value[: layout.shared_at].astype(product.dtype)
-        experts_low[slot] = value[layout.shared_at : layout.router_at].astype(product.dtype)
-
-        @pl.when(wide == 0)
-        def _():
-            small = small_ref.shape[0]
-            small_ref[:, columns] = value[layout.router_at : layout.router_at + small]
-
-        for number in range(3):
-
-            @pl.when(wide == number)
-            def _(number=number):
-                for copy in results(step, number):
-                    copy.start()
-
-        for due, event in events:
-
-            @pl.when(step == due)
-            def _(event=event):
-                event()
-
-        return carry
-
-    first = here * rows
-    spare = layout.expert_count + 2
     gain_grad[...] = jnp.zeros_like(gain_grad)
 
-    def norm(spot, start, size, value):
+    def norm_middle(spot, start, size, value):
         for k in range(peers - 1):
             value = value + z_got[k, spot, :].astype(jnp.float32)
         middle = middle_ref[spot, :]
         inverse = lax.rsqrt(jnp.mean(middle * middle, axis=-1, keepdims=True) + EPSILON)
         normed = middle * inverse
-        scaled = value * gain_ref[...]
+        scaled = value * ffn_gain
         back = inverse * (scaled - normed * jnp.mean(scaled * normed, axis=-1, keepdims=True))
         mine = pl.ds(pl.multiple_of(first + start, size), size)
-        grad = cot_ref[mine, :].astype(jnp.float32) + back
+        grad = cot_rows[spot, :].astype(jnp.float32) + back
         grad_ref[spot, :] = grad
-        low_ref[spot, :] = grad.astype(low_ref.dtype)
+        low_ref[spot, :] = grad.astype(low)
+        gm_all[mine, :] = grad.astype(low)
         gain_grad[...] += jnp.sum(value * normed, axis=0, keepdims=True)
 
-    mine = low_all_ref.at[pl.ds(here * rows, rows)]
-    store = pltpu.make_async_copy(low_ref, mine, local_sem)
-
     def spread():
-        return [
-            remote(low_ref, mine, "tensor", away[k], x_sends, x_recvs, peers - k - 1)
-            for k in near_first(peers)[:0:-1]
-        ]
+        mine = gm_all.at[pl.ds(first, rows)]
+        return to_peers(lambda k: low_ref, lambda slot: mine, m_sends, m_recvs)
 
     def finish_norm():
-        for k in order[:-1]:
+        for k in far_first:
             z_copy(k).wait_recv()
-        backs[0].total(norm)
+        backs[0].total(norm_middle)
         for copy in spread():
             copy.start()
-        store.start()
 
     gap = 12 // (peers - 1)
-    events = [(3 + gap * index, functools.partial(pass_z, k)) for index, k in enumerate(order[:-1])]
-    for k in outs:
-        events.append((OUT_FIRST, functools.partial(outs[k].step, 0)))
-    for number in range(1, half):
-        for index, k in enumerate(outs):
-            events.append((OUT_NEXT + number, functools.partial(outs[k].step, number)))
+    events = [(3 + gap * index, functools.partial(pass_z, k)) for index, k in enumerate(far_first)]
+    for number in range(half):
+        for k in outs:
+            events.append((OUT_DUE + 3 * number, functools.partial(outs[k].step, number)))
     events.append((NORM_DUE, finish_norm))
+
+    def grad_step(step, carry):
+        wide, slot = step // blocks, step % 2
+        for number in range(3):
+
+            @pl.when(step == number * blocks)
+            def _(number=number):
+                fetch_left(number).wait()
+
+                def turn_over(index, carry):
+                    spot = pl.ds(pl.multiple_of(index * 256, 256), 256)
+                    turned[:, spot] = left[spot, :].T
+                    return carry
+
+                lax.fori_loop(0, left.shape[0] // 256, turn_over, 0)
+                if number < 2:
+                    fetch_left(number + 1).start()
+
+        fetch_right(step, False).wait()
+
+        @pl.when(step + 1 < 2 * blocks)
+        def _():
+            fetch_right(step + 1, False).start()
+
+        @pl.when((step + 1 >= 2 * blocks) & (step + 1 < steps))
+        def _():
+            fetch_right(step + 1, True).start()
+
+        @pl.when(step > 1)
+        def _():
+            for copy in results(step, 0):
+                copy.wait()
+
+        value = matmul(turned[...], right[slot])
+        product[slot] = value[: layout.shared_at].astype(low)
+        shared_low[slot] = value[layout.shared_at : layout.router_at].astype(low)
+
+        @pl.when(wide == 0)
+        def _():
+            spot = pl.ds(pl.multiple_of(step % blocks * tile, tile), tile)
+            small_own[:, spot] = value[layout.router_at : layout.router_at + small_rows]
+
+        for number in range(3):
+
+            @pl.when(wide == number)
+            def _(number=number):
+                for copy in results(step, number):
+                    copy.start()
+
+        for due, event in events:
+
+            @pl.when(step == due)
+            def _(event=event):
+                event()
+
+        return carry
+
     lax.fori_loop(0, steps, grad_step, 0)
+    proj_load = pltpu.make_async_copy(
+        columns_all.at[pl.ds(small_rows, head_width)],
+        turned.at[pl.ds(head_width, head_width), pl.ds(0, width)],
+        local_sem.at[3],
+    )
+    proj_load.start()
     for step in (steps - 2, steps - 1):
         for copy in results(step, 0):
             copy.wait()
-    small_ref[spare - 1 : spare, :] = jnp.zeros((1, width), jnp.float32)
-    small_ref[spare : spare + 1, :] = gain_grad[...]
+    small_own[count + 1 : count + 2, :] = jnp.zeros((1, width), jnp.float32)
+    small_own[count + 2 : count + 3, :] = gain_grad[...]
+
     if not with_out:
-        out_sum_ref[...] = jnp.zeros_like(out_sum_ref)
+        out_load.wait()
     for k in outs:
 
         def emit_out(spot, start, size, value, k=k):
             there = pl.ds(pl.multiple_of(away[k] * rows + start, size), size)
-            out_sum_ref[there, :] = value.astype(out_sum_ref.dtype)
+            out_sum[there, :] = value.astype(low)
 
         outs[k].total(emit_out)
-    store.wait()
-    for k in order[:-1]:
-        z_copy(k).wait_send()
+    summed = to_peers(
+        lambda k: out_sum.at[pl.ds(away[k] * rows, rows)], lambda slot: o_got.at[slot], o_sends, o_recvs
+    )
+    for copy in summed:
+        copy.start()
+
     for copy in spread():
         copy.wait()
+    proj_load.wait()
+    out_weights = turned.at[pl.ds(head_width, head_width), pl.ds(0, width)]
+    grad_context[...] = matmul_last(gm_all[...], out_weights[...]).astype(low)
+    attend_back(heads, queries, keys, values, probs_ref, grad_context, cos_ref, sin_ref, grad_rows)
+    qkv_load.wait()
+
+    def through_qkv(spot):
+        attn_part[:, spot] = matmul_last(grad_rows[...], qkv_full[spot, :]).astype(low)
+
+    tiles(width, 256, through_qkv)
+    exchanged = to_peers(
+        lambda k: attn_part.at[pl.ds(away[k] * rows, rows)], lambda slot: a_got.at[slot], a_sends, a_recvs
+    )
+    for copy in exchanged:
+        copy.start()
+
+    def weight_tiles(spot):
+        qkv_full[spot, :] = matmul(attn_in[:, spot].T, grad_rows[...]).astype(low)
+
+    tiles(width, 256, weight_tiles)
+
+    def proj_tiles(spot):
+        turned[:head_width, spot] = matmul(context[...].T, gm_all[:, spot]).astype(low)
+
+    tiles(width, 256, proj_tiles)
+
     for k in order:
         backs[k].finish()
-    for k in outs:
-        outs[k].finish()
-
-
-def reduce_and_norm(
-    layout,
-    part,
-    out_part,
-    middle,
-    cotangent,
-    gain,
-    x_all,
-    cot_all,
-    grads,
-    scaled,
-    small_rows,
-    ranks,
-    peers,
-    identity,
-):
-    chips = ranks // 2
-    block, width = cotangent.shape
-    total = x_all.shape[0]
-    rows = block // peers
-    hidden = layout.hidden
-    experts = layout.local_experts
-    vmem = pl.BlockSpec(memory_space=pltpu.VMEM)
-    hbm = pl.BlockSpec(memory_space=pl.ANY)
-    dma = pltpu.SemaphoreType.DMA
-    low, f32 = part.dtype, jnp.float32
-    with_out = chips == 4
-    return pl.pallas_call(
-        functools.partial(back_kernel, layout, ranks, peers, with_out),
-        out_shape=(
-            jax.ShapeDtypeStruct((block, width), low),
-            jax.ShapeDtypeStruct((rows, width), f32),
-            jax.ShapeDtypeStruct((small_rows, width), f32),
-            jax.ShapeDtypeStruct((block, width), low),
-            jax.ShapeDtypeStruct((experts, layout.expert_hidden, width), low),
-            jax.ShapeDtypeStruct((experts, layout.expert_hidden, width), low),
-            jax.ShapeDtypeStruct((experts, layout.expert_hidden, width), low),
-            jax.ShapeDtypeStruct((3, layout.shared_own, width), low),
-        ),
-        in_specs=[hbm, hbm] + [vmem] * 3 + [hbm] * 4,
-        out_specs=(hbm, vmem, vmem, vmem, hbm, hbm, hbm, hbm),
-        scratch_shapes=[
-            pltpu.VMEM((peers, rows, width), low),
-            pltpu.VMEM((peers - 1, rows, width), low),
-            pltpu.VMEM((rows, width), low),
-            pltpu.VMEM((total, width), low),
-            pltpu.VMEM((total, hidden), low),
-            pltpu.VMEM((hidden, total), low),
-            pltpu.VMEM((2, layout.shared_at, 256), low),
-            pltpu.VMEM((2, layout.shared_own, 256), low),
-            pltpu.VMEM((1, width), f32),
-            dma((peers - 1,)),
-            dma((peers - 1,)),
-            dma((peers - 1,)),
-            dma((peers - 1,)),
-            dma,
-            dma,
-            dma,
-            dma((2 * (experts + 1),)),
-        ]
-        + (reduce_buffers(peers, chips, rows, width, low) + reduce_sems(peers, chips))
-        * (1 + with_out),
-        compiler_params=pltpu.CompilerParams(
-            collective_id=identity, has_side_effects=True, vmem_limit_bytes=62 << 20
-        ),
-        name="reduce_and_norm",
-    )(part, out_part, middle, cotangent, gain, x_all, cot_all, grads, scaled)
-
-
-def final_kernel(
-    layout,
-    ranks,
-    peers,
-    part_ref,
-    out_sum_ref,
-    middle_ref,
-    tokens_ref,
-    gain_ref,
-    grad_ref,
-    small_ref,
-    qkv_ref,
-    proj_ref,
-    shared_ref,
-    input_ref,
-    output_ref,
-    qkv_sum_ref,
-    proj_sum_ref,
-    small_sum_ref,
-    shared_got_ref,
-    z_got,
-    o_got,
-    low_ref,
-    out_low,
-    small_own,
-    small_got,
-    small_part,
-    small_z,
-    kept,
-    z_sends,
-    z_recvs,
-    o_sends,
-    o_recvs,
-    x_sends,
-    x_recvs,
-    y_sends,
-    y_recvs,
-    g_sends,
-    g_recvs,
-    h_sends,
-    h_recvs,
-    s_sends,
-    s_recvs,
-    local_sem,
-    *refs,
-):
-    ring = Ring(ranks)
-    here = lax.axis_index("tensor")
-    block, width = part_ref.shape
-    rows = block // peers
-    half = ring.half
-    pieces = refs[0].shape[0]
-    lot, size = qkv_sum_ref.shape[0], refs[0].shape[2]
-    proj_size = refs[8].shape[2]
-    columns = width // ranks
-    away = [(here + k) % peers for k in range(peers)]
-    others = [(ring.me + k) % ranks for k in range(ranks)]
-    greet(
-        [{"dp": others[k]} for k in range(1, ranks)] + [{"tensor": away[k]} for k in range(1, peers)]
-    )
-    far_first = near_first(peers)[:0:-1]
-
-    def to_peers(source_of, target_of, sends, recvs):
-        copies = []
-        for k in far_first:
-            slot = peers - k - 1
-            copy = remote(source_of(k), target_of(slot), "tensor", away[k], sends, recvs, slot)
-            copy.start()
-            copies.append(copy)
-        return copies
-
-    exchanged = to_peers(
-        lambda k: part_ref.at[pl.ds(away[k] * rows, rows)], lambda slot: z_got.at[slot], z_sends, z_recvs
-    )
-    summed = to_peers(
-        lambda k: out_sum_ref.at[pl.ds(away[k] * rows, rows)],
-        lambda slot: o_got.at[slot],
-        o_sends,
-        o_recvs,
-    )
-
-    def slice_of(device):
-        return pl.ds(pl.multiple_of(device * columns, columns), columns)
-
+    for partner in ring.partners():
+        pl.semaphore_signal(reuse_sem, inc=1, device_id=partner, device_id_type=MESH)
+    pl.semaphore_wait(reuse_sem, 3)
+    pieces = proj_buffers[0].shape[0]
+    lot, size = qkv_sum_ref.shape[0], qkv_sum_ref.shape[0] // pieces
+    proj_size = proj_buffers[0].shape[2]
+    narrow = [
+        buffer.at[pl.ds(0, pieces), :, pl.ds(0, size), pl.ds(0, 3 * head_width)] for buffer in buffers
+    ]
     works = []
     for piece in range(pieces):
 
         def qkv_at(device, piece=piece):
-            return qkv_ref.at[pl.ds(device * lot + piece * size, size)]
+            return qkv_full.at[pl.ds(device * lot + piece * size, size)]
 
         def proj_at(device, piece=piece):
-            return proj_ref.at[pl.ds(piece * proj_size, proj_size), slice_of(device)]
-
-        works.append(RingReduce(ring, qkv_at, size, refs[0:3], refs[3:8], piece))
-        works.append(RingReduce(ring, proj_at, proj_size, refs[8:11], refs[11:16], piece))
+            return turned.at[pl.ds(piece * proj_size, proj_size), slice_of(device)]
+
+        works.append(RingReduce(ring, qkv_at, size, narrow, qkv_sems, piece))
+        works.append(RingReduce(ring, proj_at, proj_size, proj_buffers, proj_sems, piece))
     for offset in works[0].order:
         for work in works:
             work.hand_over(offset)
-    shared = []
-    for k in range(1, ranks):
-        copy = remote(
-            shared_ref.at[:, :, slice_of(others[k])],
-            shared_got_ref.at[ring.me],
-            "dp",
-            others[k],
-            s_sends,
-            s_recvs,
-            ranks - k - 1,
-        )
-        copy.start()
-        shared.append(copy)
-    keep = pltpu.make_async_copy(shared_ref.at[:, :, slice_of(ring.me)], kept, local_sem.at[0])
-    keep.start()
     for number in range(half):
         for work in works:
             work.step(number)
-    keep.wait()
-    keep = pltpu.make_async_copy(kept, shared_got_ref.at[ring.me], local_sem.at[0])
-    keep.start()
-
-    first = here * rows
-    small_own[...] = small_ref[...]
-    spot_row = layout.expert_count + 1
-
-    def norm(spot, start, count):
-        mine = pl.ds(pl.multiple_of(first + start, count), count)
-        value = part_ref[mine, :].astype(jnp.float32)
+
+    spot_row = count + 1
+
+    def norm_tokens(spot, start, size):
+        mine = pl.ds(pl.multiple_of(first + start, size), size)
+        value = attn_part[mine, :].astype(jnp.float32)
         for k in range(peers - 1):
-            value = value + z_got[k, spot, :].astype(jnp.float32)
-        inputs = tokens_ref[mine, :].astype(jnp.float32)
+            value = value + a_got[k, spot, :].astype(jnp.float32)
+        inputs = token_rows[spot, :].astype(jnp.float32)
         inverse = lax.rsqrt(jnp.mean(inputs * inputs, axis=-1, keepdims=True) + EPSILON)
         normed = inputs * inverse
-        scaled = value * gain_ref[...]
+        scaled = value * attn_gain
         back = inverse * (scaled - normed * jnp.mean(scaled * normed, axis=-1, keepdims=True))
-        low_ref[spot, :] = (grad_ref[spot, :] + back).astype(low_ref.dtype)
+        low_ref[spot, :] = (grad_ref[spot, :] + back).astype(low)
         small_own[spot_row : spot_row + 1, :] += jnp.sum(value * normed, axis=0, keepdims=True)
 
     for copy in exchanged:
         copy.wait_recv()
-    strips(rows, norm)
-    mine = input_ref.at[pl.ds(here * rows, rows)]
-    spread = to_peers(lambda k: low_ref, lambda slot: mine, x_sends, x_recvs)
-    stores = [pltpu.make_async_copy(low_ref, mine, local_sem.at[1])]
+    strips(rows, norm_tokens)
+    mine = input_ref.at[pl.ds(first, rows)]
+    inputs_out = to_peers(lambda k: low_ref, lambda slot: mine, x_sends, x_recvs)
+    for copy in inputs_out:
+        copy.start()
+    stores = [pltpu.make_async_copy(low_ref, mine, local_sem.at[5])]
     stores[0].start()
     handed = []
     for k in range(1, ranks):
@@ -1450,30 +1473,37 @@
         copy.start()
         handed.append(copy)
 
-    def finish_rows(spot, start, count):
-        there = pl.ds(pl.multiple_of(first + start, count), count)
-        value = out_sum_ref[there, :].astype(jnp.float32)
+    shared = []
+    for k in range(1, ranks):
+        copy = remote(
+            shared_grads_ref.at[:, :, slice_of(others[k])],
+            shared_got_ref.at[ring.me],
+            "dp",
+            others[k],
+            s_sends,
+            s_recvs,
+            ranks - k - 1,
+        )
+        copy.start()
+        shared.append(copy)
+    keep = pltpu.make_async_copy(
+        shared_grads_ref.at[:, :, slice_of(ring.me)], kept, local_sem.at[4]
+    )
+    keep.start()
+
+    def finish_rows(spot, start, size):
+        there = pl.ds(pl.multiple_of(first + start, size), size)
+        value = out_sum[there, :].astype(jnp.float32)
         for k in range(peers - 1):
             value = value + o_got[k, spot, :].astype(jnp.float32)
-        out_low[spot, :] = (middle_ref[spot, :] + value).astype(out_low.dtype)
+        out_low[spot, :] = (middle_ref[spot, :] + value).astype(low)
 
     for copy in summed:
         copy.wait_recv()
     strips(rows, finish_rows)
-    out_mine = output_ref.at[pl.ds(here * rows, rows)]
-    spread += to_peers(lambda k: out_low, lambda slot: out_mine, y_sends, y_recvs)
-    stores.append(pltpu.make_async_copy(out_low, out_mine, local_sem.at[2]))
-    stores[1].start()
-    for piece in range(pieces):
-
-        def emit_qkv(spot, start, count, value, piece=piece):
-            qkv_sum_ref[pl.ds(pl.multiple_of(piece * size + start, count), count), :] = value
-
-        def emit_proj(spot, start, count, value, piece=piece):
-            proj_sum_ref[pl.ds(pl.multiple_of(piece * proj_size + start, count), count), :] = value
-
-        works[2 * piece].total(emit_qkv)
-        works[2 * piece + 1].total(emit_proj)
+    keep.wait()
+    keep = pltpu.make_async_copy(kept, shared_got_ref.at[ring.me], local_sem.at[4])
+    keep.start()
     for copy in handed:
         copy.wait_recv()
     value = small_own[:, slice_of(ring.me)]
@@ -1481,6 +1511,24 @@
         value = value + small_got[k]
     small_part[...] = value
     last = to_peers(lambda k: small_part, lambda slot: small_z.at[slot], h_sends, h_recvs)
+    for copy in last:
+        copy.start()
+    out_mine = output_ref.at[pl.ds(first, rows)]
+    outputs_out = to_peers(lambda k: out_low, lambda slot: out_mine, y_sends, y_recvs)
+    for copy in outputs_out:
+        copy.start()
+    stores.append(pltpu.make_async_copy(out_low, out_mine, local_sem.at[6]))
+    stores[1].start()
+    for piece in range(pieces):
+
+        def emit_qkv(spot, start, count, value, piece=piece):
+            qkv_sum_ref[pl.ds(pl.multiple_of(piece * size + start, count), count), :] = value
+
+        def emit_proj(spot, start, count, value, piece=piece):
+            proj_sum_ref[pl.ds(pl.multiple_of(piece * proj_size + start, count), count), :] = value
+
+        works[2 * piece].total(emit_qkv)
+        works[2 * piece + 1].total(emit_proj)
     for copy in last:
         copy.wait_recv()
     value = small_part[...]
@@ -1490,91 +1538,141 @@
     keep.wait()
     for copy in stores:
         copy.wait()
+    for k in far_first:
+        z_copy(k).wait_send()
     for copy in exchanged + summed + handed + last:
         copy.wait_send()
-    for copy in shared + spread:
+    for copy in shared + inputs_out + outputs_out:
         copy.wait()
+    for k in outs:
+        outs[k].finish()
     for work in works:
         work.finish()
 
 
-def finish_grads(
+def rear(
     layout,
-    part,
-    out_sum,
+    back_part,
+    out_part,
+    x_all,
+    cot_all,
+    grads,
+    scaled,
+    rows_all,
+    columns_all,
     middle,
+    cotangent,
     tokens,
-    gain,
-    grad,
-    small,
-    grad_qkv,
-    grad_proj,
-    shared_grads,
+    attn_in,
+    queries,
+    keys,
+    values,
+    context,
+    probs,
+    cosine,
+    sine,
+    small_rows,
+    with_out,
     ranks,
     peers,
     identity,
 ):
     chips = ranks // 2
-    block, width = part.shape
+    block, width = tokens.shape
+    total = x_all.shape[0]
     rows = block // peers
-    lot, wide = grad_qkv.shape[0] // ranks, grad_qkv.shape[1]
+    hidden, own = layout.hidden, layout.shared_own
+    experts, units = layout.local_experts, layout.expert_hidden
+    head_width = queries.shape[1]
     columns = width // ranks
-    height = grad_proj.shape[0]
     pieces = 4
-    small_rows = small.shape[0]
-    own = layout.shared_own
+    tile = 256
     vmem = pl.BlockSpec(memory_space=pltpu.VMEM)
     hbm = pl.BlockSpec(memory_space=pl.ANY)
-    low, f32 = part.dtype, jnp.float32
     dma = pltpu.SemaphoreType.DMA
+    low, f32 = tokens.dtype, jnp.float32
+    shape = jax.ShapeDtypeStruct
     return pl.pallas_call(
-        functools.partial(final_kernel, layout, ranks, peers),
+        functools.partial(rear_kernel, layout, ranks, peers, with_out),
         out_shape=(
-            jax.ShapeDtypeStruct((block, width), low),
-            jax.ShapeDtypeStruct((block, width), low),
-            jax.ShapeDtypeStruct((lot, wide), f32),
-            jax.ShapeDtypeStruct((height, columns), f32),
-            jax.ShapeDtypeStruct((small_rows, columns), f32),
-            jax.ShapeDtypeStruct((ranks, 3, own, columns), low),
+            shape((block, width), low),
+            shape((block, width), low),
+            shape((columns, 3 * head_width), f32),
+            shape((head_width, columns), f32),
+            shape((small_rows, columns), f32),
+            *[shape((experts, units, width), low)] * 3,
+            shape((3, own, width), low),
+            shape((ranks, 3, own, columns), low),
         ),
-        in_specs=[vmem] * 7 + [hbm] * 3,
-        out_specs=(hbm, hbm, vmem, vmem, vmem, hbm),
+        in_specs=[hbm] * 8 + [vmem] + [hbm] * 2 + [vmem] * 8,
+        out_specs=(hbm, hbm, vmem, vmem, vmem, hbm, hbm, hbm, hbm, hbm),
         scratch_shapes=[
-            pltpu.VMEM((peers - 1, rows, width), low),
-            pltpu.VMEM((peers - 1, rows, width), low),
             pltpu.VMEM((rows, width), low),
             pltpu.VMEM((rows, width), low),
+            pltpu.VMEM((small_rows, width), low),
+            pltpu.VMEM((rows, width), f32),
             pltpu.VMEM((small_rows, width), f32),
             pltpu.VMEM((ranks - 1, small_rows, columns), f32),
             pltpu.VMEM((small_rows, columns), f32),
             pltpu.VMEM((peers - 1, small_rows, columns), f32),
+            pltpu.VMEM((peers, rows, width), low),
+            pltpu.VMEM((peers - 1, rows, width), low),
+            pltpu.VMEM((peers - 1, rows, width), low),
+            pltpu.VMEM((peers - 1, rows, width), low),
+            pltpu.VMEM((rows, width), low),
+            pltpu.VMEM((block, width), low),
+            pltpu.VMEM((2, total, tile), low),
+            pltpu.VMEM((total, hidden), low),
+            pltpu.VMEM((hidden, total), low),
+            pltpu.VMEM((2, layout.shared_at, tile), low),
+            pltpu.VMEM((2, own, tile), low),
+            pltpu.VMEM((1, width), f32),
+            pltpu.VMEM((width, 3 * head_width), low),
+            pltpu.VMEM((block, head_width), low),
+            pltpu.VMEM((block, 3 * head_width), low),
+            pltpu.VMEM((block, width), low),
+            pltpu.VMEM((block, width), low),
             pltpu.VMEM((3, own, columns), low),
         ]
-        + [dma((peers - 1,))] * 8
-        + [dma((ranks - 1,))] * 2
-        + [dma((peers - 1,))] * 2
-        + [dma((ranks - 1,))] * 2
-        + [dma((3,))]
-        + reduce_buffers(pieces, chips, lot // pieces, wide, low)
+        + [dma((peers - 1,))] * 14
+        + [dma((ranks - 1,))] * 4
+        + [
+            dma((7,)),
+            dma,
+            dma((2,)),
+            dma((2 * (experts + 1),)),
+            pltpu.SemaphoreType.REGULAR,
+        ]
+        + reduce_buffers(peers, chips, rows, width, low)
+        + reduce_sems(peers, chips)
         + reduce_sems(pieces, chips)
-        + reduce_buffers(pieces, chips, height // pieces, columns, low)
-        + reduce_sems(pieces, chips),
+        + reduce_buffers(pieces, chips, head_width // pieces, columns, low)
+        + reduce_sems(pieces, chips)
+        + (reduce_buffers(peers, chips, rows, width, low) + reduce_sems(peers, chips)) * with_out,
         compiler_params=pltpu.CompilerParams(
-            collective_id=identity, has_side_effects=True, vmem_limit_bytes=60 << 20
+            collective_id=identity, has_side_effects=True, vmem_limit_bytes=67043328
         ),
-        name="finish_grads",
-    )(part, out_sum, middle, tokens, gain, grad, small, grad_qkv, grad_proj, shared_grads)
-
-
-def dot_rows(left, right):
-    return lax.dot_general(
-        left, right, (((0,), (0,)), ((), ())), preferred_element_type=jnp.float32
-    )
-
-
-def dot_last(left, right):
-    return lax.dot_general(
-        left, right, (((1,), (1,)), ((), ())), preferred_element_type=jnp.float32
+        name="rear",
+    )(
+        back_part,
+        out_part,
+        x_all,
+        cot_all,
+        grads,
+        scaled,
+        rows_all,
+        columns_all,
+        middle,
+        cotangent,
+        tokens,
+        attn_in,
+        queries,
+        keys,
+        values,
+        context,
+        probs,
+        cosine,
+        sine,
     )
 
 
@@ -1588,30 +1686,6 @@
         jnp.asarray(np.concatenate([cosine, cosine], axis=1)),
         jnp.asarray(np.concatenate([-sine, sine], axis=1)),
     )
-
-
-def rotate_back(values, cosine, sine):
-    swapped = jnp.roll(values, HEAD_DIM // 2, axis=-1)
-    return values * cosine[:, None, :] - swapped * sine[:, None, :]
-
-
-def attend_backward(queries, key_rows, value_rows, probs, grad_context):
-    probs_low = probs.astype(jnp.bfloat16)
-    grad_probs = jnp.einsum(
-        "qhd,khd->hqk", grad_context, value_rows, preferred_element_type=jnp.float32
-    )
-    inner = jnp.sum(probs * grad_probs, axis=-1, keepdims=True)
-    grad_scores = (probs * (grad_probs - inner)).astype(jnp.bfloat16)
-    grad_queries = jnp.einsum(
-        "hqk,khd->qhd", grad_scores, key_rows, preferred_element_type=jnp.float32
-    ) * HEAD_DIM ** (-0.5)
-    grad_keys = jnp.einsum(
-        "hqk,qhd->khd", grad_scores, queries, preferred_element_type=jnp.float32
-    ) * HEAD_DIM ** (-0.5)
-    grad_values = jnp.einsum(
-        "hqk,qhd->khd", probs_low, grad_context, preferred_element_type=jnp.float32
-    )
-    return (grad_queries, grad_keys, grad_values)
 
 
 def scatter_rows(values):
@@ -1641,13 +1715,11 @@
     low = jnp.bfloat16
     ranks = lax.axis_size("dp")
     peers = lax.axis_size("tensor")
-    me = lax.axis_index("dp")
     token_count, width = tokens.shape
     local_experts, _, expert_hidden = expert_gate.shape
     expert_count = local_experts * ranks
     block = width // ranks
     head_width = w_query.shape[1]
-    head_count = head_width // HEAD_DIM
     shared_width = shared_gate.shape[1]
     shared_own = shared_width // ranks
     small_pad = 128
@@ -1705,67 +1777,35 @@
         peers,
         1,
     )
-    qkv_full = qkv_full[:, : 3 * head_width]
-    out_full = columns_full[small_rows:]
-    attn_gain = columns_full[expert_count + 1].astype(jnp.float32)
-    ffn_gain = columns_full[expert_count + 2].astype(jnp.float32)
-    grad_attn_out, grad_middle, grad_small, out_sum, *grad_experts, grad_shared = reduce_and_norm(
+    with_out = ranks == 8
+    grad_input, output, grad_qkv, grad_proj, grad_small, *grad_experts, _, grad_shared = rear(
         layout,
         back_part,
-        out_part,
-        middle,
-        cotangent,
-        ffn_gain[None, :],
+        out_part if with_out else scatter_rows(out_part),
         x_all,
         cot_all,
         grads_wide,
         scaled_hidden,
+        qkv_full,
+        columns_full,
+        middle,
+        cotangent,
+        tokens,
+        attn_in,
+        queries,
+        key_rows,
+        value_rows,
+        context_flat,
+        probs,
+        cosine,
+        sine,
         small_rows,
+        with_out,
         ranks,
         peers,
         2,
     )
-    if ranks != 8:
-        out_sum = scatter_rows(out_part)
     grad_experts = [grads.astype(jnp.float32) for grads in grad_experts]
-
-    grad_proj = dot_rows(context_flat, grad_attn_out).astype(low)
-    grad_context = dot_last(grad_attn_out, out_full)
-    shape_three = (SEQ, head_count, HEAD_DIM)
-    grad_queries, grad_keys, grad_values = attend_backward(
-        queries.reshape(shape_three),
-        key_rows.reshape(shape_three),
-        value_rows.reshape(shape_three),
-        probs,
-        grad_context.astype(low).reshape(shape_three),
-    )
-    flat_shape = (token_count, head_width)
-    grad_qkv_rows = jnp.concatenate(
-        [
-            rotate_back(grad_queries, cosine, sine).reshape(flat_shape).astype(low),
-            rotate_back(grad_keys, cosine, sine).reshape(flat_shape).astype(low),
-            grad_values.reshape(flat_shape).astype(low),
-        ],
-        axis=1,
-    )
-    grad_qkv = dot_rows(attn_in, grad_qkv_rows)
-    attn_back_part = dot_last(grad_qkv_rows, qkv_full)
-    grad_input, output, grad_qkv, grad_proj, grad_small, grad_shared = finish_grads(
-        layout,
-        attn_back_part.astype(low),
-        out_sum,
-        middle,
-        tokens,
-        attn_gain[None, :],
-        grad_middle,
-        grad_small,
-        grad_qkv.astype(low),
-        grad_proj,
-        grad_shared,
-        ranks,
-        peers,
-        3,
-    )
     grad_shared = grad_shared.astype(jnp.float32)
     return (
         output,

time: 452 us -> 404 us (0.89)
  Pallas kernels: 395 us -> 365 us
  matrix products: 16.3 us -> 0 us
    pallas_call x1, Pallas kernels: 208 us -> 187 us  [layer_forward_back(): pl.pallas_call(functools.partial(layer_kernel, layout, ranks, peers), out...]
    dot_general x8 -> x0, matrix products: 16.3 us -> none  [the longest x2 8.46 us: dot_last(): lax.dot_general(left, right, (((1,), (1,)), ((), ())), preferred_element_...]
    pallas_call x2 -> x1, Pallas kernels: 187 us -> 179 us  [rear(): pl.pallas_call(functools.partial(rear_kernel, layout, ranks, peers, with_...]
where the time goes in v4:
time: 404 us; the launch traced here: 401 us
  Pallas kernels  365 us (90%)
  local copies, waits for them, and re-layouts  18.3 us (5%)
  other arithmetic  16.5 us (4%)
    pallas_call x1, Pallas kernels, layer_forward_back(): pl.pallas_call(functools.partial(layer_kernel, layout, ranks, peers), out...  187 us
    pallas_call x1, Pallas kernels, rear(): pl.pallas_call(functools.partial(rear_kernel, layout, ranks, peers, with_...  179 us

profile of v4, /device:TPU:0, one launch (start us, length us, event | category | flops | bytes accessed | tf_op | source)
XLA Modules:
  0.0 400.6 jit_solution(14191236724077627900)
XLA Ops:
  0.7 0.7 stack.13
  1.3 0.7 stack.14
  2.0 0.7 stack.12
  2.6 0.6 pad_maximum_fusion.vectors_ref
  3.2 1.5 convert_reduce_fusion.chosen_own_ref
  4.8 1.6 fusion.1.allowed_ref
  6.3 2.2 copy.41
  8.6 2.2 copy.42
  10.8 186.6 %layer_forward_back.1 = (bf16[2048,1664]{1,0:T(8,128)(2,1)}, bf16[544,2048]{1,0:T(8,128)(2,1)}, bf16[256,2048]{1,0:T(8,128)(2,1)}, bf16[256,512]{1,0:T(8,128)(2,...) custom-call(bf16[256,512]{1,0:T(8,128)(2,1)} %query_ref.1, ...), custom_call_target="tpu_custom_call" | custom-call | tf_op jit(solution)/shard_map/layer_forward_back/pallas_call | solution.py:811
  197.4 178.6 %rear.1 = (bf16[256,2048]{1,0:T(8,128)(2,1)}, bf16[256,2048]{1,0:T(8,128)(2,1)}, f32[256,1536]{1,0:T(8,128)}, f32[512,256]{1,0:T(8,128)}, f32[32,256]{1,0:T(8,12...) custom-call(bf16[2048,2048]{1,0:T(8,128)(2,1)} %get-tuple-element.40, ...), custom_call_target="tpu_custom_call" | custom-call | tf_op jit(solution)/shard_map/rear/pallas_call | solution.py:1595
  376.0 0.0 copy-start.3
  376.0 1.4 fusion.4
  377.4 1.3 slice_bitcast_fusion
  378.7 0.0 copy-start
  378.7 2.7 fusion.3
  381.4 0.0 copy-done.3
  381.4 1.6 convert_element_type.23
  382.9 0.0 copy-done
  382.9 1.6 fusion.2
  384.5 1.5 copy.44
  386.1 1.5 copy.43
  387.6 0.0 copy-start.1
  387.6 0.0 copy-start.2
  387.6 5.3 %convert_element_type.25 = f32[2,352,2048]{2,1,0:T(8,128)} convert(bf16[2,352,2048]{2,1,0:T(8,128)(2,1)} %get-tuple-element.63) | non-fusion elementwise | flops 1441792 | bytes 8650752 | tf_op jit(solution)/shard_map/convert_element_type | solution.py:1808
  392.9 0.0 copy-done.1
  392.9 0.0 copy-done.2
  392.9 0.0 copy-start.4
  392.9 0.0 copy-start.5
  392.9 5.9 %convert_bitcast_fusion = (f32[2,2048,352]{1,2,0:T(8,128)}, f32[2,2048,352]{1,2,0:T(8,128)}) fusion(bf16[2,352,2048]{2,1,0:T(8,128)(2,1)S(1)} %copy-done.2, bf16[2,352,2048]{2,1,0:T(8,128)(2,1)S(1)} %copy-done.1), kind=kLoop, calls=%fused_computation | loop fusion | flops 2883584 | bytes 17301504 | tf_op jit(solution)/shard_map/transpose | solution.py:1825
  398.8 0.0 copy-done.4
  398.8 1.0 copy.47
  399.8 0.0 copy-done.5
  399.8 0.8 copy.48
  (1 shorter events, 0.0 us)
Async XLA Ops:
  376.0 5.4 %copy-start.3 = (bf16[256,2048]{1,0:T(8,128)(2,1)S(1)}, bf16[256,2048]{1,0:T(8,128)(2,1)}, u32[]{:S(2)}) copy-start(bf16[256,2048]{1,0:T(8,128)(2,1)} %get-tuple-element.56) | copy-start | bytes 3145732
  378.7 4.2 %copy-start = (bf16[8,3,176,256]{3,2,1,0:T(8,128)(2,1)S(1)}, bf16[8,3,176,256]{3,2,1,0:T(8,128)(2,1)}, u32[]{:S(2)}) copy-start(bf16[8,3,176,256]{3,2,1,0:T(8,128)(2,1)} %get-tuple-element.60) | copy-start | bytes 6488068
  387.6 5.3 %copy-start.1 = (bf16[2,352,2048]{2,1,0:T(8,128)(2,1)S(1)}, bf16[2,352,2048]{2,1,0:T(8,128)(2,1)}, u32[]{:S(2)}) copy-start(bf16[2,352,2048]{2,1,0:T(8,128)(2,1)} %get-tuple-element.61) | copy-start | bytes 8650756
  387.6 5.3 %copy-start.2 = (bf16[2,352,2048]{2,1,0:T(8,128)(2,1)S(1)}, bf16[2,352,2048]{2,1,0:T(8,128)(2,1)}, u32[]{:S(2)}) copy-start(bf16[2,352,2048]{2,1,0:T(8,128)(2,1)} %get-tuple-element.62) | copy-start | bytes 8650756
  392.9 6.0 %copy-start.4 = (bf16[256,2048]{1,0:T(8,128)(2,1)S(1)}, bf16[256,2048]{1,0:T(8,128)(2,1)}, u32[]{:S(2)}) copy-start(bf16[256,2048]{1,0:T(8,128)(2,1)} %get-tuple-element.91) | copy-start | bytes 3145732
  392.9 6.9 %copy-start.5 = (f32[512,256]{1,0:T(8,128)S(1)}, f32[512,256]{1,0:T(8,128)}, u32[]{:S(2)}) copy-start(f32[512,256]{1,0:T(8,128)} %get-tuple-element.96) | copy-start | bytes 1572868

commit v5 on v4

--- a/solution.py
+++ b/solution.py
@@ -84,7 +84,7 @@
         self.sends, self.recvs = sends, recvs
         self.side_sends, self.side_recvs = side_sends, side_recvs
         self.base, self.side_base = base, side_base
-        self.hops, self.sides = {}, 0
+        self.sides = side_slots(ring.half)
 
     def hop_copy(self, source, target, device, slot):
         return remote(source, target, "dp", device, self.sends, self.recvs, self.base + slot)
@@ -100,23 +100,19 @@
             self.side_base + slot,
         )
 
-    def hop(self, source, target, device, slot, size):
-        self.hop_copy(source, target, device, slot).start()
-        self.hops[slot] = size
-
-    def share(self, source, target):
-        self.side_copy(source, target, self.sides).start()
-        self.sides += 1
+    def hop_size(self, slot):
+        number = slot % self.ring.half
+        return self.cut if number and number == self.ring.half - 1 else self.rows
 
     def begin(self, source):
         ring = self.ring
         target = self.place(ring.me, 0, self.rows)
-        self.hop(source, target, ring.ahead, 0, self.rows)
-        self.hop(source, target, ring.behind, ring.half, self.rows)
-        self.share(source, target)
+        self.hop_copy(source, target, ring.ahead, 0).start()
+        self.hop_copy(source, target, ring.behind, ring.half).start()
+        self.side_copy(source, target, 0).start()
 
     def wait_hop(self, slot):
-        block = self.place(self.ring.me, 0, self.hops[slot])
+        block = self.place(self.ring.me, 0, self.hop_size(slot))
         self.hop_copy(block, block, self.ring.ahead, slot).wait_recv()
 
     def step(self, number):
@@ -127,33 +123,26 @@
             self.wait_hop(which * ring.half + number - 1)
             if number < ring.half:
                 block = self.place(owner, 0, self.rows)
-                size = self.rows
-                part = block
-                if number == ring.half - 1:
-                    size = self.cut
-                    part = self.place(owner, (0, self.cut)[which], size)
-                self.hop(part, part, onward, which * ring.half + number, size)
-                self.share(block, block)
+                slot = which * ring.half + number
+                size = self.hop_size(slot)
+                part = block if size == self.rows else self.place(owner, (0, self.cut)[which], size)
+                self.hop_copy(part, part, onward, slot).start()
+                self.side_copy(block, block, 2 * number - 1 + which).start()
         if number == ring.half:
             block = self.place(ring.device(number), 0, self.rows)
-            self.share(block, block)
+            self.side_copy(block, block, 2 * ring.half - 1).start()
 
     def wait_side(self, index):
         block = self.place(self.ring.me, 0, self.rows)
         self.side_copy(block, block, index).wait_recv()
 
     def sent(self):
-        for slot, size in self.hops.items():
-            block = self.place(self.ring.me, 0, size)
+        for slot in range(2 * self.ring.half):
+            block = self.place(self.ring.me, 0, self.hop_size(slot))
             self.hop_copy(block, block, self.ring.ahead, slot).wait_send()
         for index in range(self.sides):
             block = self.place(self.ring.me, 0, self.rows)
             self.side_copy(block, block, index).wait_send()
-
-    def finish(self):
-        self.sent()
-        for index in range(self.sides):
-            self.wait_side(index)
 
 
 def near_first(peers):
@@ -166,7 +155,7 @@
 
 
 STRIP = 64
-OUT_DUE, NORM_DUE = 10, 15
+BACK_DUE = (0, 5, 11, 11, 17)
 
 
 def strips(rows, body):
@@ -389,6 +378,7 @@
     a_side_sends,
     a_side_recvs,
     block_sem,
+    x_sem,
     store_sem,
     shared_sends,
     shared_recvs,
@@ -546,11 +536,21 @@
             gather.wait_side(index)
     fetches = [
         pltpu.make_async_copy(rows_all, rows_full, gather_sem.at[7]),
-        pltpu.make_async_copy(columns_all, columns_full, gather_sem.at[8]),
+        pltpu.make_async_copy(
+            columns_all.at[pl.ds(small_rows, head_width)],
+            columns_full.at[pl.ds(small_rows, head_width)],
+            gather_sem.at[8],
+        ),
     ]
+    first_rows = pltpu.make_async_copy(
+        columns_all.at[pl.ds(0, small_rows)],
+        columns_full.at[pl.ds(0, small_rows)],
+        gather_sem.at[9],
+    )
+    first_rows.start()
     for fetch in fetches:
         fetch.start()
-    fetches[1].wait()
+    first_rows.wait()
     gates[layout.router_at : layout.router_at + count + 1, :] = columns_full[: count + 1, :]
     vectors = columns_full[:small_rows, :].astype(jnp.float32)
     attn_gain = vectors[count + 1 : count + 2, :]
@@ -573,6 +573,8 @@
         return qkv_raw[:, index * HEAD_DIM : (index + 1) * HEAD_DIM]
 
     attend(heads, qkv, allowed_ref, cos_ref, sin_ref, queries, keys, values, probs_ref, context)
+
+    fetches[1].wait()
 
     def project_out(spot):
         part_ref[:, spot] = matmul(context[...], columns_full[small_rows:, spot]).astype(low)
@@ -641,11 +643,12 @@
         return place
 
     mine = place_of(0)(ring.me, 0, rows)
-    forwards = []
-    for k in order[1:]:
-        copy = remote(own, mine, "tensor", away[k], x_sends, x_recvs, peers - k - 1)
-        copy.start()
-        forwards.append(copy)
+
+    def peer_place(device, start, size):
+        return x_all.at[pl.ds(ring.me * block + device * rows + start, size)]
+
+    forwards = TensorGather(peers, own, peer_place, rows, x_sends, x_recvs)
+    forwards.begin()
     works = [
         RingGather(
             ring,
@@ -664,15 +667,13 @@
     store = pltpu.make_async_copy(own, mine, local_sem.at[4])
     store.start()
 
-    for index, k in enumerate(order[1:]):
-        spot = place_of(k)(ring.me, 0, rows)
-        remote(own, spot, "tensor", away[k], x_sends, x_recvs, k - 1).wait_recv()
-        works[k].begin(spot)
-        if index == 0:
+    half_peers = peers // 2
+    for number in range(1, half_peers + 1):
+        forwards.step(number)
+        for k in sorted({peers - number, number}):
+            works[k].begin(place_of(k)(ring.me, 0, rows))
+        if number == 1:
             cots.step(1)
-            cot_turn(1, 1)
-        if index == 1:
-            cot_turn(2, 2)
     store.wait()
     passing = [works[k] for k in order]
     cuts = [part * len(passing) // 4 for part in range(5)]
@@ -686,20 +687,38 @@
             )
         ]
 
+    def fetch_x(turn):
+        return pltpu.make_async_copy(
+            x_all.at[chip_spot(turn)], x_block.at[turn % 2], x_sem.at[turn % 2]
+        )
+
+    for work in works:
+        work.wait_side(0)
+    fetch_x(0).start()
+
     def chip_step(turn, carry):
         offset = (1 - 2 * (turn % 2)) * ((turn + 1) // 2)
         spot = chip_spot(turn)
         slot = turn - turn // 4 * (turn - 3)
 
         def pass_on(part):
-            for number in range(1, half + 1):
+            @pl.when(turn == 0)
+            def _():
+                for work in passing[cuts[part] : cuts[part + 1]]:
+                    work.step(1)
+
+        def pass_on_far():
+            for number in range(2, half + 1):
 
                 @pl.when(turn == 2 * number - 2)
                 def _(number=number):
-                    if part == 0 and number > 1:
-                        cots.step(number)
-                    for work in passing[cuts[part] : cuts[part + 1]]:
+                    for work in [cots] + passing:
                         work.step(number)
+
+        def fetch_next():
+            for work in works:
+                work.wait_side(turn + 1)
+            fetch_x(turn + 1).start()
 
         for device in range(2):
             for fold in range(block // lot):
@@ -708,13 +727,14 @@
                 chosen[device * block + fold * lot : device * block + (fold + 1) * lot, :] = rows_full[
                     pl.ds(pl.multiple_of(there, lot), lot), first_lane : first_lane + 128
                 ]
-        for work in works:
-            work.wait_side(turn)
-        load_x = pltpu.make_async_copy(x_all.at[spot], x_block, block_sem.at[1])
-        load_x.start()
-        load_x.wait()
-        hidden_tiles(layout, x_block, gates, ups, pre_gate, pre_up)
+        fetch_x(turn).wait()
+        hidden_tiles(layout, x_block.at[turn % 2], gates, ups, pre_gate, pre_up)
         pass_on(0)
+        pass_on_far()
+
+        @pl.when(turn == 0)
+        def _():
+            cot_turn(1, 1)
 
         @pl.when(turn > 2)
         def _():
@@ -748,16 +768,32 @@
 
         out_tiles(width, scaled, downs, out)
         pending[2].start()
+
+        @pl.when(turn == 0)
+        def _():
+            cot_turn(2, 2)
+
         pass_on(2)
+
+        @pl.when((turn > 0) & (turn + 1 < ring.chips))
+        def _():
+            fetch_next()
+
         back_tiles(layout, width, grads, gates, ups, back)
         pending[3].start()
         pass_on(3)
+
+        @pl.when(turn == 0)
+        def _():
+            fetch_next()
+
         return carry
 
     lax.fori_loop(0, ring.chips, chip_step, 0)
     for copy in stores(pl.ds(0, chip_rows)):
         copy.wait()
-    for copy in forwards + handed:
+    forwards.sent()
+    for copy in handed:
         copy.wait_send()
     for gather in gathers:
         gather.sent()
@@ -839,7 +875,7 @@
             pltpu.VMEM((3, ranks, layout.shared_own, depth), low),
             pltpu.VMEM((rows, width), low),
             pltpu.VMEM((peers - 1, rows, width), low),
-            pltpu.VMEM((chip, width), low),
+            pltpu.VMEM((2, chip, width), low),
             pltpu.VMEM((chip, width), low),
             pltpu.VMEM((chip, hidden), f32),
             pltpu.VMEM((chip, hidden), f32),
@@ -850,19 +886,20 @@
             pltpu.VMEM((chip, width), low),
             pltpu.VMEM((chip, 128), low),
             dma((5 + 3 * layout.local_experts,)),
-            dma((9,)),
+            dma((10,)),
             dma((2 * gather_slots(half),)),
             dma((2 * gather_slots(half),)),
             dma((2 * side_slots(half),)),
             dma((2 * side_slots(half),)),
+            dma((2,)),
             dma((2,)),
             dma((4,)),
             dma((3 * (ranks - 1),)),
             dma((3 * (ranks - 1),)),
             dma((peers - 1,)),
             dma((peers - 1,)),
-            dma((peers - 1,)),
-            dma((peers - 1,)),
+            dma((peers,)),
+            dma((peers,)),
             dma((peers * gather_slots(half),)),
             dma((peers * gather_slots(half),)),
             dma((peers * side_slots(half),)),
@@ -1021,6 +1058,109 @@
 def reduce_sems(pieces, chips):
     dma = pltpu.SemaphoreType.DMA
     return [dma((pieces * chips,))] * 5
+
+
+class TensorSum:
+    def __init__(self, peers, own_at, got, sends, recvs):
+        self.peers, self.half = peers, peers // 2
+        self.here = lax.axis_index("tensor")
+        self.own_at, self.got, self.sends, self.recvs = own_at, got, sends, recvs
+        self.rows = got.shape[1]
+
+    def hop(self, which, number):
+        peers, half = self.peers, self.half
+        cut = self.rows // 2
+        distance = half - number
+        k = distance if which == 0 else peers - distance
+        if number == 0:
+            place, slot = pl.ds((0, cut)[which], cut), 0
+        else:
+            place, slot = pl.ds(0, self.rows), which * (half - 1) + number
+        device = (self.here + (1, peers - 1)[which]) % peers
+        return remote(
+            self.own_at(k).at[place],
+            self.got.at[slot, place],
+            "tensor",
+            device,
+            self.sends,
+            self.recvs,
+            which * half + number,
+        )
+
+    def begin(self):
+        self.hop(0, 0).start()
+        self.hop(1, 0).start()
+
+    def send(self, k):
+        half = self.half
+        if k == half:
+            self.begin()
+            return
+        which = 0 if k < half else 1
+        number = half - (k if which == 0 else self.peers - k)
+        self.hop(which, number - 1).wait_recv()
+        own = self.own_at(k)
+        cut = self.rows // 2
+        first, size, slot = 0, self.rows, which * (half - 1) + number - 1
+        if number == 1:
+            first, size, slot = (0, cut)[which], cut, 0
+        place = slice(first, first + size)
+        value = own[place, :].astype(jnp.float32) + self.got[slot, place, :].astype(jnp.float32)
+        own[place, :] = value.astype(own.dtype)
+        self.hop(which, number).start()
+
+    def arrived(self):
+        self.hop(0, self.half - 1).wait_recv()
+        self.hop(1, self.half - 1).wait_recv()
+
+    def rest(self, spot):
+        half = self.half
+        if half == 1:
+            return self.got[0, spot, :].astype(jnp.float32)
+        value = self.got[half - 1, spot, :].astype(jnp.float32)
+        return value + self.got[2 * half - 2, spot, :].astype(jnp.float32)
+
+    def sent(self):
+        for number in range(self.half):
+            for which in range(2):
+                self.hop(which, number).wait_send()
+
+
+class TensorGather:
+    def __init__(self, peers, source, place, rows, sends, recvs):
+        self.peers, self.half = peers, peers // 2
+        self.here = lax.axis_index("tensor")
+        self.source, self.place, self.rows = source, place, rows
+        self.sends, self.recvs = sends, recvs
+
+    def hop(self, which, number):
+        peers, half = self.peers, self.half
+        cut = self.rows // 2
+        owner = (self.here + (peers - number, number)[which]) % peers
+        first, size = 0, self.rows
+        if number and number == half - 1:
+            first, size = (0, cut)[which], cut
+        target = self.place(owner, first, size)
+        source = self.source if number == 0 else target
+        device = (self.here + (1, peers - 1)[which]) % peers
+        return remote(
+            source, target, "tensor", device, self.sends, self.recvs, which * half + number
+        )
+
+    def begin(self):
+        self.hop(0, 0).start()
+        self.hop(1, 0).start()
+
+    def step(self, number):
+        for which in range(2):
+            self.hop(which, number - 1).wait_recv()
+            if number < self.half:
+                self.hop(which, number).start()
+
+    def sent(self):
+        for number in range(self.half):
+            for which in range(2):
+                self.hop(which, number).wait_send()
 
 
 def attend_back(heads, queries, keys, values, probs_ref, grad_context, cos_ref, sin_ref, grads):
@@ -1213,12 +1353,14 @@
     if not with_out:
         out_load = pltpu.make_async_copy(out_part_ref, out_sum, local_sem.at[2])
         out_load.start()
-    for number in range(half):
-        for k in order:
-            backs[k].step(number)
-    for offset in backs[0].order:
-        for k in outs:
-            outs[k].hand_over(offset)
+    for k in order:
+        backs[k].step(0)
+
+    def hand_outs():
+        for offset in backs[0].order:
+            for k in outs:
+                outs[k].hand_over(offset)
+
     vec_load.wait()
     for load in row_loads:
         load.wait()
@@ -1227,16 +1369,13 @@
     attn_gain = vectors[count + 1 : count + 2, :]
     ffn_gain = vectors[count + 2 : count + 3, :]
 
-    def z_copy(k):
-        slot = peers - k - 1
-        return remote(z_stage.at[k], z_got.at[slot], "tensor", away[k], z_sends, z_recvs, slot)
-
+    z_sum = TensorSum(peers, lambda k: z_stage.at[k], z_got, z_sends, z_recvs)
     def pass_z(k):
         def emit(spot, start, size, value):
             z_stage[k, spot, :] = value.astype(low)
 
         backs[k].total(emit)
-        z_copy(k).start()
+        z_sum.send(k)
 
     def results(step, wide):
         slot = step % 2
@@ -1262,8 +1401,7 @@
     gain_grad[...] = jnp.zeros_like(gain_grad)
 
     def norm_middle(spot, start, size, value):
-        for k in range(peers - 1):
-            value = value + z_got[k, spot, :].astype(jnp.float32)
+        value = value + z_sum.rest(spot)
         middle = middle_ref[spot, :]
         inverse = lax.rsqrt(jnp.mean(middle * middle, axis=-1, keepdims=True) + EPSILON)
         normed = middle * inverse
@@ -1276,23 +1414,34 @@
         gm_all[mine, :] = grad.astype(low)
         gain_grad[...] += jnp.sum(value * normed, axis=0, keepdims=True)
 
-    def spread():
-        mine = gm_all.at[pl.ds(first, rows)]
-        return to_peers(lambda k: low_ref, lambda slot: mine, m_sends, m_recvs)
+    def rows_in(target):
+        def place(device, start, size):
+            return target.at[pl.ds(device * rows + start, size)]
+
+        return place
+
+    def spread(source, target, sends, recvs):
+        return TensorGather(peers, source, rows_in(target), rows, sends, recvs)
+
+    gm_spread = spread(low_ref, gm_all, m_sends, m_recvs)
 
     def finish_norm():
-        for k in far_first:
-            z_copy(k).wait_recv()
+        z_sum.arrived()
         backs[0].total(norm_middle)
-        for copy in spread():
-            copy.start()
-
-    gap = 12 // (peers - 1)
-    events = [(3 + gap * index, functools.partial(pass_z, k)) for index, k in enumerate(far_first)]
+        gm_spread.begin()
+
+    events = []
+    for number in range(1, half):
+        for index, k in enumerate(order):
+            events.append((BACK_DUE[0] + number - 1 + index, functools.partial(backs[k].step, number)))
+    events.append((BACK_DUE[1], hand_outs))
+    gap = 6 // (peers - 2)
+    for index, k in enumerate(far_first):
+        events.append((BACK_DUE[2] + gap * index, functools.partial(pass_z, k)))
     for number in range(half):
-        for k in outs:
-            events.append((OUT_DUE + 3 * number, functools.partial(outs[k].step, number)))
-    events.append((NORM_DUE, finish_norm))
+        for index, k in enumerate(outs):
+            due = BACK_DUE[3 + number] + number * index
+            events.append((due, functools.partial(outs[k].step, number)))
 
     def grad_step(step, carry):
         wide, slot = step // blocks, step % 2
@@ -1360,119 +1509,10 @@
     for step in (steps - 2, steps - 1):
         for copy in results(step, 0):
             copy.wait()
+
+    finish_norm()
     small_own[count + 1 : count + 2, :] = jnp.zeros((1, width), jnp.float32)
     small_own[count + 2 : count + 3, :] = gain_grad[...]
-
-    if not with_out:
-        out_load.wait()
-    for k in outs:
-
-        def emit_out(spot, start, size, value, k=k):
-            there = pl.ds(pl.multiple_of(away[k] * rows + start, size), size)
-            out_sum[there, :] = value.astype(low)
-
-        outs[k].total(emit_out)
-    summed = to_peers(
-        lambda k: out_sum.at[pl.ds(away[k] * rows, rows)], lambda slot: o_got.at[slot], o_sends, o_recvs
-    )
-    for copy in summed:
-        copy.start()
-
-    for copy in spread():
-        copy.wait()
-    proj_load.wait()
-    out_weights = turned.at[pl.ds(head_width, head_width), pl.ds(0, width)]
-    grad_context[...] = matmul_last(gm_all[...], out_weights[...]).astype(low)
-    attend_back(heads, queries, keys, values, probs_ref, grad_context, cos_ref, sin_ref, grad_rows)
-    qkv_load.wait()
-
-    def through_qkv(spot):
-        attn_part[:, spot] = matmul_last(grad_rows[...], qkv_full[spot, :]).astype(low)
-
-    tiles(width, 256, through_qkv)
-    exchanged = to_peers(
-        lambda k: attn_part.at[pl.ds(away[k] * rows, rows)], lambda slot: a_got.at[slot], a_sends, a_recvs
-    )
-    for copy in exchanged:
-        copy.start()
-
-    def weight_tiles(spot):
-        qkv_full[spot, :] = matmul(attn_in[:, spot].T, grad_rows[...]).astype(low)
-
-    tiles(width, 256, weight_tiles)
-
-    def proj_tiles(spot):
-        turned[:head_width, spot] = matmul(context[...].T, gm_all[:, spot]).astype(low)
-
-    tiles(width, 256, proj_tiles)
-
-    for k in order:
-        backs[k].finish()
-    for partner in ring.partners():
-        pl.semaphore_signal(reuse_sem, inc=1, device_id=partner, device_id_type=MESH)
-    pl.semaphore_wait(reuse_sem, 3)
-    pieces = proj_buffers[0].shape[0]
-    lot, size = qkv_sum_ref.shape[0], qkv_sum_ref.shape[0] // pieces
-    proj_size = proj_buffers[0].shape[2]
-    narrow = [
-        buffer.at[pl.ds(0, pieces), :, pl.ds(0, size), pl.ds(0, 3 * head_width)] for buffer in buffers
-    ]
-    works = []
-    for piece in range(pieces):
-
-        def qkv_at(device, piece=piece):
-            return qkv_full.at[pl.ds(device * lot + piece * size, size)]
-
-        def proj_at(device, piece=piece):
-            return turned.at[pl.ds(piece * proj_size, proj_size), slice_of(device)]
-
-        works.append(RingReduce(ring, qkv_at, size, narrow, qkv_sems, piece))
-        works.append(RingReduce(ring, proj_at, proj_size, proj_buffers, proj_sems, piece))
-    for offset in works[0].order:
-        for work in works:
-            work.hand_over(offset)
-    for number in range(half):
-        for work in works:
-            work.step(number)
-
-    spot_row = count + 1
-
-    def norm_tokens(spot, start, size):
-        mine = pl.ds(pl.multiple_of(first + start, size), size)
-        value = attn_part[mine, :].astype(jnp.float32)
-        for k in range(peers - 1):
-            value = value + a_got[k, spot, :].astype(jnp.float32)
-        inputs = token_rows[spot, :].astype(jnp.float32)
-        inverse = lax.rsqrt(jnp.mean(inputs * inputs, axis=-1, keepdims=True) + EPSILON)
-        normed = inputs * inverse
-        scaled = value * attn_gain
-        back = inverse * (scaled - normed * jnp.mean(scaled * normed, axis=-1, keepdims=True))
-        low_ref[spot, :] = (grad_ref[spot, :] + back).astype(low)
-        small_own[spot_row : spot_row + 1, :] += jnp.sum(value * normed, axis=0, keepdims=True)
-
-    for copy in exchanged:
-        copy.wait_recv()
-    strips(rows, norm_tokens)
-    mine = input_ref.at[pl.ds(first, rows)]
-    inputs_out = to_peers(lambda k: low_ref, lambda slot: mine, x_sends, x_recvs)
-    for copy in inputs_out:
-        copy.start()
-    stores = [pltpu.make_async_copy(low_ref, mine, local_sem.at[5])]
-    stores[0].start()
-    handed = []
-    for k in range(1, ranks):
-        copy = remote(
-            small_own.at[:, slice_of(others[k])],
-            small_got.at[ranks - k - 1],
-            "dp",
-            others[k],
-            g_sends,
-            g_recvs,
-            ranks - k - 1,
-        )
-        copy.start()
-        handed.append(copy)
-
     shared = []
     for k in range(1, ranks):
         copy = remote(
@@ -1490,17 +1530,133 @@
         shared_grads_ref.at[:, :, slice_of(ring.me)], kept, local_sem.at[4]
     )
     keep.start()
+    half_peers = peers // 2
+    for number in range(1, half_peers):
+        gm_spread.step(number)
+
+    def chunk_of(source):
+        return lambda k: source.at[pl.ds(away[k] * rows, rows)]
+
+    if not with_out:
+        out_load.wait()
+    for k in outs:
+
+        def emit_out(spot, start, size, value, k=k):
+            there = pl.ds(pl.multiple_of(away[k] * rows + start, size), size)
+            out_sum[there, :] = value.astype(low)
+
+        outs[k].total(emit_out)
+    out_total = TensorSum(peers, chunk_of(out_sum), o_got, o_sends, o_recvs)
+    out_total.begin()
+
+    gm_spread.step(half_peers)
+    proj_load.wait()
+    out_weights = turned.at[pl.ds(head_width, head_width), pl.ds(0, width)]
+    grad_context[...] = matmul_last(gm_all[...], out_weights[...]).astype(low)
+    attend_back(heads, queries, keys, values, probs_ref, grad_context, cos_ref, sin_ref, grad_rows)
+    qkv_load.wait()
+
+    def through_qkv(spot):
+        attn_part[:, spot] = matmul_last(grad_rows[...], qkv_full[spot, :]).astype(low)
+
+    tiles(width, 256, through_qkv)
+    attn_total = TensorSum(peers, chunk_of(attn_part), a_got, a_sends, a_recvs)
+    attn_total.begin()
+    def weight_tiles(spot):
+        qkv_full[spot, :] = matmul(attn_in[:, spot].T, grad_rows[...]).astype(low)
+
+    tiles(width, 256, weight_tiles)
+    for k in far_first[1:]:
+        attn_total.send(k)
+    for k in far_first[1:]:
+        out_total.send(k)
+
+    def proj_tiles(spot):
+        turned[:head_width, spot] = matmul(context[...].T, gm_all[:, spot]).astype(low)
+
+    tiles(width, 256, proj_tiles)
+
+    for k in order:
+        backs[k].finish()
+    for partner in ring.partners():
+        pl.semaphore_signal(reuse_sem, inc=1, device_id=partner, device_id_type=MESH)
+    pl.semaphore_wait(reuse_sem, 3)
+    pieces = proj_buffers[0].shape[0]
+    lot, size = qkv_sum_ref.shape[0], qkv_sum_ref.shape[0] // pieces
+    proj_size = proj_buffers[0].shape[2]
+    narrow = [
+        buffer.at[pl.ds(0, pieces), :, pl.ds(0, size), pl.ds(0, 3 * head_width)] for buffer in buffers
+    ]
+    works = []
+    for piece in range(pieces):
+
+        def qkv_at(device, piece=piece):
+            return qkv_full.at[pl.ds(device * lot + piece * size, size)]
+
+        def proj_at(device, piece=piece):
+            return turned.at[pl.ds(piece * proj_size, proj_size), slice_of(device)]
+
+        works.append(RingReduce(ring, qkv_at, size, narrow, qkv_sems, piece))
+        works.append(RingReduce(ring, proj_at, proj_size, proj_buffers, proj_sems, piece))
+    for offset in works[0].order:
+        for work in works:
+            work.hand_over(offset)
+    for work in works:
+        work.step(0)
+
+    spot_row = count + 1
+
+    def norm_tokens(spot, start, size):
+        mine = pl.ds(pl.multiple_of(first + start, size), size)
+        value = attn_part[mine, :].astype(jnp.float32)
+        value = value + attn_total.rest(spot)
+        inputs = token_rows[spot, :].astype(jnp.float32)
+        inverse = lax.rsqrt(jnp.mean(inputs * inputs, axis=-1, keepdims=True) + EPSILON)
+        normed = inputs * inverse
+        scaled = value * attn_gain
+        back = inverse * (scaled - normed * jnp.mean(scaled * normed, axis=-1, keepdims=True))
+        low_ref[spot, :] = (grad_ref[spot, :] + back).astype(low)
+        small_own[spot_row : spot_row + 1, :] += jnp.sum(value * normed, axis=0, keepdims=True)
+
+    attn_total.arrived()
+    gm_spread.sent()
+    strips(rows, norm_tokens)
+    mine = input_ref.at[pl.ds(first, rows)]
+    input_spread = spread(low_ref, input_ref, x_sends, x_recvs)
+    input_spread.begin()
+    stores = [pltpu.make_async_copy(low_ref, mine, local_sem.at[5])]
+    stores[0].start()
+    handed = []
+    for k in range(1, ranks):
+        copy = remote(
+            small_own.at[:, slice_of(others[k])],
+            small_got.at[ranks - k - 1],
+            "dp",
+            others[k],
+            g_sends,
+            g_recvs,
+            ranks - k - 1,
+        )
+        copy.start()
+        handed.append(copy)
+
+    for number in range(1, half):
+        for work in works:
+            work.step(number)
 
     def finish_rows(spot, start, size):
         there = pl.ds(pl.multiple_of(first + start, size), size)
         value = out_sum[there, :].astype(jnp.float32)
-        for k in range(peers - 1):
-            value = value + o_got[k, spot, :].astype(jnp.float32)
+        value = value + out_total.rest(spot)
         out_low[spot, :] = (middle_ref[spot, :] + value).astype(low)
 
-    for copy in summed:
-        copy.wait_recv()
+    out_total.arrived()
     strips(rows, finish_rows)
+    out_mine = output_ref.at[pl.ds(first, rows)]
+    output_spread = spread(out_low, output_ref, y_sends, y_recvs)
+    output_spread.begin()
+    for number in range(1, half_peers):
+        input_spread.step(number)
     keep.wait()
     keep = pltpu.make_async_copy(kept, shared_got_ref.at[ring.me], local_sem.at[4])
     keep.start()
@@ -1513,10 +1669,6 @@
     last = to_peers(lambda k: small_part, lambda slot: small_z.at[slot], h_sends, h_recvs)
     for copy in last:
         copy.start()
-    out_mine = output_ref.at[pl.ds(first, rows)]
-    outputs_out = to_peers(lambda k: out_low, lambda slot: out_mine, y_sends, y_recvs)
-    for copy in outputs_out:
-        copy.start()
     stores.append(pltpu.make_async_copy(out_low, out_mine, local_sem.at[6]))
     stores[1].start()
     for piece in range(pieces):
@@ -1529,6 +1681,8 @@
 
         works[2 * piece].total(emit_qkv)
         works[2 * piece + 1].total(emit_proj)
+    for number in range(1, half_peers):
+        output_spread.step(number)
     for copy in last:
         copy.wait_recv()
     value = small_part[...]
@@ -1538,11 +1692,13 @@
     keep.wait()
     for copy in stores:
         copy.wait()
-    for k in far_first:
-        z_copy(k).wait_send()
-    for copy in exchanged + summed + handed + last:
+    input_spread.step(half_peers)
+    output_spread.step(half_peers)
+    for work in (z_sum, out_total, attn_total, input_spread, output_spread):
+        work.sent()
+    for copy in handed + last:
         copy.wait_send()
-    for copy in shared + inputs_out + outputs_out:
+    for copy in shared:
         copy.wait()
     for k in outs:
         outs[k].finish()
@@ -1634,7 +1790,7 @@
             pltpu.VMEM((block, width), low),
             pltpu.VMEM((3, own, columns), low),
         ]
-        + [dma((peers - 1,))] * 14
+        + [dma((peers,))] * 14
         + [dma((ranks - 1,))] * 4
         + [
             dma((7,)),

time: 404 us -> 379 us (0.938)
  Pallas kernels: 365 us -> 343 us
    pallas_call x1, Pallas kernels: 179 us -> 159 us  [rear(): pl.pallas_call(functools.partial(rear_kernel, layout, ranks, peers, with_...]
where the time goes in v5:
time: 379 us; the launch traced here: 378 us
  Pallas kernels  343 us (91%)
  local copies, waits for them, and re-layouts  18.3 us (5%)
  other arithmetic  16.5 us (4%)
    pallas_call x1, Pallas kernels, layer_forward_back(): pl.pallas_call(functools.partial(layer_kernel, layout, ranks, peers), out...  184 us
    pallas_call x1, Pallas kernels, rear(): pl.pallas_call(functools.partial(rear_kernel, layout, ranks, peers, with_...  159 us

profile of v5, /device:TPU:0, one launch (start us, length us, event | category | flops | bytes accessed | tf_op | source)
XLA Modules:
  0.0 378.0 jit_solution(14883413811158159580)
XLA Ops:
  0.7 0.7 stack.13
  1.3 0.7 stack.14
  2.0 0.7 stack.12
  2.6 0.6 pad_maximum_fusion.vectors_ref
  3.2 1.5 convert_reduce_fusion.chosen_own_ref
  4.8 1.6 fusion.1.allowed_ref
  6.3 2.2 copy.41
  8.6 2.2 copy.42
  10.8 183.6 %layer_forward_back.1 = (bf16[2048,1664]{1,0:T(8,128)(2,1)}, bf16[544,2048]{1,0:T(8,128)(2,1)}, bf16[256,2048]{1,0:T(8,128)(2,1)}, bf16[256,512]{1,0:T(8,128)(2,...) custom-call(bf16[256,512]{1,0:T(8,128)(2,1)} %query_ref.1, ...), custom_call_target="tpu_custom_call" | custom-call | tf_op jit(solution)/shard_map/layer_forward_back/pallas_call | solution.py:847
  194.4 158.9 %rear.1 = (bf16[256,2048]{1,0:T(8,128)(2,1)}, bf16[256,2048]{1,0:T(8,128)(2,1)}, f32[256,1536]{1,0:T(8,128)}, f32[512,256]{1,0:T(8,128)}, f32[32,256]{1,0:T(8,12...) custom-call(bf16[2048,2048]{1,0:T(8,128)(2,1)} %get-tuple-element.40, ...), custom_call_target="tpu_custom_call" | custom-call | tf_op jit(solution)/shard_map/rear/pallas_call | solution.py:1751
  353.4 0.0 copy-start.3
  353.4 1.4 fusion.4
  354.8 1.3 slice_bitcast_fusion
  356.1 0.0 copy-start
  356.1 2.7 fusion.3
  358.8 0.0 copy-done.3
  358.8 1.6 convert_element_type.23
  360.3 0.0 copy-done
  360.3 1.6 fusion.2
  361.9 1.5 copy.44
  363.5 1.5 copy.43
  365.0 0.0 copy-start.1
  365.0 0.0 copy-start.2
  365.0 5.3 %convert_element_type.25 = f32[2,352,2048]{2,1,0:T(8,128)} convert(bf16[2,352,2048]{2,1,0:T(8,128)(2,1)} %get-tuple-element.63) | non-fusion elementwise | flops 1441792 | bytes 8650752 | tf_op jit(solution)/shard_map/convert_element_type | solution.py:1964
  370.3 0.0 copy-done.1
  370.3 0.0 copy-done.2
  370.3 0.0 copy-start.4
  370.3 0.0 copy-start.5
  370.3 5.9 %convert_bitcast_fusion = (f32[2,2048,352]{1,2,0:T(8,128)}, f32[2,2048,352]{1,2,0:T(8,128)}) fusion(bf16[2,352,2048]{2,1,0:T(8,128)(2,1)S(1)} %copy-done.2, bf16[2,352,2048]{2,1,0:T(8,128)(2,1)S(1)} %copy-done.1), kind=kLoop, calls=%fused_computation | loop fusion | flops 2883584 | bytes 17301504 | tf_op jit(solution)/shard_map/transpose | solution.py:1981
  376.2 0.0 copy-done.4
  376.2 1.0 copy.47
  377.2 0.0 copy-done.5
  377.2 0.8 copy.48
  (1 shorter events, 0.0 us)
Async XLA Ops:
  353.4 5.4 %copy-start.3 = (bf16[256,2048]{1,0:T(8,128)(2,1)S(1)}, bf16[256,2048]{1,0:T(8,128)(2,1)}, u32[]{:S(2)}) copy-start(bf16[256,2048]{1,0:T(8,128)(2,1)} %get-tuple-element.56) | copy-start | bytes 3145732
  356.1 4.2 %copy-start = (bf16[8,3,176,256]{3,2,1,0:T(8,128)(2,1)S(1)}, bf16[8,3,176,256]{3,2,1,0:T(8,128)(2,1)}, u32[]{:S(2)}) copy-start(bf16[8,3,176,256]{3,2,1,0:T(8,128)(2,1)} %get-tuple-element.60) | copy-start | bytes 6488068
  365.0 5.3 %copy-start.1 = (bf16[2,352,2048]{2,1,0:T(8,128)(2,1)S(1)}, bf16[2,352,2048]{2,1,0:T(8,128)(2,1)}, u32[]{:S(2)}) copy-start(bf16[2,352,2048]{2,1,0:T(8,128)(2,1)} %get-tuple-element.61) | copy-start | bytes 8650756
  365.0 5.3 %copy-start.2 = (bf16[2,352,2048]{2,1,0:T(8,128)(2,1)S(1)}, bf16[2,352,2048]{2,1,0:T(8,128)(2,1)}, u32[]{:S(2)}) copy-start(bf16[2,352,2048]{2,1,0:T(8,128)(2,1)} %get-tuple-element.62) | copy-start | bytes 8650756
  370.3 6.0 %copy-start.4 = (bf16[256,2048]{1,0:T(8,128)(2,1)S(1)}, bf16[256,2048]{1,0:T(8,128)(2,1)}, u32[]{:S(2)}) copy-start(bf16[256,2048]{1,0:T(8,128)(2,1)} %get-tuple-element.91) | copy-start | bytes 3145732
  370.3 6.9 %copy-start.5 = (f32[512,256]{1,0:T(8,128)S(1)}, f32[512,256]{1,0:T(8,128)}, u32[]{:S(2)}) copy-start(f32[512,256]{1,0:T(8,128)} %get-tuple-element.96) | copy-start | bytes 1572868

commit v6 on v5

--- a/solution.py
+++ b/solution.py
@@ -295,9 +295,13 @@
     return values * cosine + pltpu.roll(values, HEAD_DIM // 2, 1) * (sine * sign)
 
 
-def attend(heads, qkv, allowed_ref, cos_ref, sin_ref, queries, keys, values, probs_ref, context):
+def attend(heads, qkv, segments_ref, cos_ref, sin_ref, queries, keys, values, probs_ref, context):
     cosine, sine = cos_ref[...], sin_ref[...]
-    allowed = allowed_ref[...] > 0.5
+    length = queries.shape[0]
+    segments = jnp.broadcast_to(segments_ref[...].astype(jnp.float32), (length, length))
+    row = lax.broadcasted_iota(jnp.int32, (length, length), 0)
+    column = lax.broadcasted_iota(jnp.int32, (length, length), 1)
+    allowed = (segments == segments.T) & (column <= row)
     low = queries.dtype
     for head in range(heads):
         columns = slice(head * HEAD_DIM, (head + 1) * HEAD_DIM)
@@ -319,13 +323,15 @@
     query_ref,
     key_ref,
     value_ref,
-    chosen_own_ref,
     proj_ref,
     router_ref,
-    vectors_ref,
+    routes_ref,
+    switch_ref,
+    attn_gain_ref,
+    ffn_gain_ref,
     tokens_ref,
     cot_ref,
-    allowed_ref,
+    segments_ref,
     cos_ref,
     sin_ref,
     expert_gate_ref,
@@ -359,6 +365,7 @@
     ups,
     downs,
     shared_got,
+    shared_rows,
     own,
     got,
     x_block,
@@ -412,7 +419,7 @@
     small_rows = height - head_width
     low = gates.dtype
     loads, start = [], 0
-    for index, source in enumerate((query_ref, key_ref, value_ref, chosen_own_ref)):
+    for index, source in enumerate((query_ref, key_ref, value_ref)):
         size = source.shape[1]
         loads.append(
             pltpu.make_async_copy(source, row_stage.at[:, pl.ds(start, size)], gather_sem.at[index])
@@ -428,12 +435,36 @@
     small = jnp.concatenate(
         [
             router_ref[...].astype(jnp.float32),
-            vectors_ref[...].astype(jnp.float32),
-            jnp.zeros((small_rows - count - vectors_ref.shape[0], depth), jnp.float32),
+            switch_ref[...].astype(jnp.float32).reshape(1, depth),
+            attn_gain_ref[...].astype(jnp.float32).reshape(1, depth),
+            ffn_gain_ref[...].astype(jnp.float32).reshape(1, depth),
+            jnp.zeros((small_rows - count - 3, depth), jnp.float32),
         ],
         axis=0,
     )
     column_stage[:small_rows, :] = small.astype(low)
+    top = routes_ref.shape[0]
+    routes = routes_ref[...].astype(jnp.float32)
+    routes = jnp.concatenate([routes, jnp.zeros((8 - top, block), jnp.float32)], axis=0).T
+    for fold in range(block // lot):
+        lane = lax.broadcasted_iota(jnp.int32, (lot, 128), 1).astype(jnp.float32) - lane0
+        mark = jnp.zeros((lot, 128), jnp.float32)
+        for k in range(top):
+            route = routes[fold * lot : (fold + 1) * lot, k : k + 1]
+            mark = jnp.where(lane == route, 1.0, mark)
+        row_stage[:, start + fold * 128 : start + (fold + 1) * 128] = mark.astype(low)
+    aligned = layout.shared_own % 16 == 0
+    shared_loads = []
+    if aligned:
+        shared_wide = ranks * layout.shared_own
+        for which, source in enumerate((shared_gate_ref, shared_up_ref)):
+            load = pltpu.make_async_copy(
+                source,
+                x_block.at[which, pl.ds(0, depth), pl.ds(0, shared_wide)],
+                gather_sem.at[10 + which],
+            )
+            load.start()
+            shared_loads.append(load)
     greet(
         [{"dp": others[k]} for k in range(1, ranks)] + [{"tensor": away[k]} for k in range(1, peers)]
     )
@@ -470,6 +501,13 @@
         )
         store.start()
         stores_own.append(store)
+    if aligned:
+        for which, load in enumerate(shared_loads):
+            load.wait()
+            for first in range(0, shared_wide, 128):
+                size = min(128, shared_wide - first)
+                part = x_block[which, :depth, first : first + size]
+                shared_rows[which, first : first + size, :] = part.T
     for number in range(1, half):
         for gather in gathers:
             gather.step(number)
@@ -497,12 +535,17 @@
     for gather in gathers:
         gather.step(half)
 
-    shared_refs = (shared_gate_ref, shared_up_ref, shared_down_ref)
+    def shared_source(which, device):
+        if which < 2 and aligned:
+            place = pl.ds(pl.multiple_of(device * layout.shared_own, 16), layout.shared_own)
+            return shared_rows.at[which, place]
+        return (shared_gate_ref, shared_up_ref, shared_down_ref)[which].at[device]
+
     handed, kept = [], []
     for k in range(1, ranks):
-        for which, source in enumerate(shared_refs):
+        for which in range(3):
             copy = remote(
-                source.at[others[k]],
+                shared_source(which, others[k]),
                 shared_got.at[which, ring.me],
                 "dp",
                 others[k],
@@ -512,9 +555,9 @@
             )
             copy.start()
             handed.append(copy)
-    for which, source in enumerate(shared_refs):
+    for which in range(3):
         copy = pltpu.make_async_copy(
-            source.at[ring.me], shared_got.at[which, ring.me], local_sem.at[which]
+            shared_source(which, ring.me), shared_got.at[which, ring.me], local_sem.at[which]
         )
         copy.start()
         kept.append(copy)
@@ -572,7 +615,7 @@
     def qkv(index):
         return qkv_raw[:, index * HEAD_DIM : (index + 1) * HEAD_DIM]
 
-    attend(heads, qkv, allowed_ref, cos_ref, sin_ref, queries, keys, values, probs_ref, context)
+    attend(heads, qkv, segments_ref, cos_ref, sin_ref, queries, keys, values, probs_ref, context)
 
     fetches[1].wait()
 
@@ -807,13 +850,15 @@
     query,
     key,
     value,
-    chosen,
     proj,
     router,
-    vectors,
+    routes,
+    switch,
+    attn_gain,
+    ffn_gain,
     tokens,
     cot,
-    allowed,
+    segments,
     cosine,
     sine,
     expert_gate,
@@ -835,7 +880,8 @@
     hidden = layout.hidden
     chip = 2 * block
     head_width = query.shape[1]
-    wide = 3 * head_width + chosen.shape[1]
+    wide = 3 * head_width + block // depth * 128
+    aligned = layout.shared_own % 16 == 0
     height = small_rows + head_width
     low = tokens.dtype
     vmem = pl.BlockSpec(memory_space=pltpu.VMEM)
@@ -860,7 +906,7 @@
             jax.ShapeDtypeStruct((total, width), low),
             jax.ShapeDtypeStruct((total, width), low),
         ),
-        in_specs=[hbm] * 5 + [vmem] * 7 + [hbm] * 6,
+        in_specs=[hbm] * 4 + [vmem] * 10 + [hbm] * 6,
         out_specs=(hbm, hbm, *[vmem] * 6, hbm, hbm, vmem, hbm, hbm, hbm, hbm),
         scratch_shapes=[
             pltpu.VMEM((depth, wide), low),
@@ -873,6 +919,7 @@
             pltpu.VMEM((hidden, width), low),
             pltpu.VMEM((hidden, width), low),
             pltpu.VMEM((3, ranks, layout.shared_own, depth), low),
+            pltpu.VMEM((2, ranks * layout.shared_own if aligned else 16, depth), low),
             pltpu.VMEM((rows, width), low),
             pltpu.VMEM((peers - 1, rows, width), low),
             pltpu.VMEM((2, chip, width), low),
@@ -886,7 +933,7 @@
             pltpu.VMEM((chip, width), low),
             pltpu.VMEM((chip, 128), low),
             dma((5 + 3 * layout.local_experts,)),
-            dma((10,)),
+            dma((12,)),
             dma((2 * gather_slots(half),)),
             dma((2 * gather_slots(half),)),
             dma((2 * side_slots(half),)),
@@ -917,13 +964,15 @@
         query,
         key,
         value,
-        chosen,
         proj,
         router,
-        vectors,
+        routes,
+        switch,
+        attn_gain,
+        ffn_gain,
         tokens,
         cot,
-        allowed,
+        segments,
         cosine,
         sine,
         expert_gate,
@@ -1832,6 +1881,129 @@
     )
 
 
+def widen_kernel(ranks, experts_in, with_shared, *refs):
+    ins, refs = refs[:8], refs[8:]
+    gate_in, up_in, down_in, input_in, output_in, qkv_in, proj_in, shared_in = ins
+    amount = 12 if with_shared else 9
+    outs, refs = refs[:amount], refs[amount:]
+    lows, wides, input_low, input_wide, output_low, qkv, proj, shared, rows, turned, sems, out_sems = refs
+    loads = []
+
+    def load(source, target):
+        copy = pltpu.make_async_copy(source, target, sems.at[len(loads)])
+        copy.start()
+        loads.append(copy)
+        return copy
+
+    stores = []
+
+    def store(source, target):
+        copy = pltpu.make_async_copy(source, target, out_sems.at[len(stores)])
+        copy.start()
+        stores.append(copy)
+
+    parts = []
+    for which, source in enumerate((gate_in, up_in, down_in)):
+        for j in range(experts_in):
+            parts.append((which, j, load(source.at[j], lows.at[which, j])))
+    rest = [
+        load(input_in, input_low),
+        load(output_in, output_low),
+        load(qkv_in, qkv),
+        load(proj_in, proj),
+    ]
+    if with_shared:
+        rest.append(load(shared_in, shared))
+
+    def convert(source, target):
+        size = 32 if source.shape[0] % 32 == 0 else 16
+
+        def step(index, carry):
+            spot = pl.ds(pl.multiple_of(index * size, size), size)
+            target[spot, :] = source[spot, :].astype(target.dtype)
+            return carry
+
+        lax.fori_loop(0, source.shape[0] // size, step, 0)
+
+    for which, j, copy in parts:
+        copy.wait()
+        convert(lows.at[which, j], wides.at[which, j])
+        store(wides.at[which, j], outs[which].at[j])
+    rest[0].wait()
+    convert(input_low, input_wide)
+    store(input_wide, outs[3])
+    rest[1].wait()
+    store(output_low, outs[4])
+    rest[2].wait()
+    head_width = qkv.shape[1] // 3
+    for which in range(3):
+        store(qkv.at[:, pl.ds(which * head_width, head_width)], outs[5 + which])
+    rest[3].wait()
+    store(proj, outs[8])
+    if with_shared:
+        rest[4].wait()
+        own = shared.shape[2]
+        for which in range(3):
+            for source in range(ranks):
+                rows[which, source * own : (source + 1) * own, :] = shared[source, which].astype(
+                    rows.dtype
+                )
+        for which in range(2):
+            for tile in range(rows.shape[1] // 128):
+                spot = slice(tile * 128, (tile + 1) * 128)
+                turned[which, :, spot] = rows[which, spot, :].T
+            store(turned.at[which], outs[9 + which])
+        store(rows.at[2], outs[11])
+    for copy in stores:
+        copy.wait()
+
+
+def widen(gate, up, down, grad_input, output, qkv, proj, shared):
+    experts, units, width = gate.shape
+    block = grad_input.shape[0]
+    lot, wide = qkv.shape
+    ranks, _, own, columns = shared.shape
+    with_shared = (ranks * own) % 128 == 0 and own % 16 == 0
+    hbm = pl.BlockSpec(memory_space=pl.ANY)
+    dma = pltpu.SemaphoreType.DMA
+    low, f32 = gate.dtype, jnp.float32
+    shape = jax.ShapeDtypeStruct
+    outs = [shape((experts, units, width), f32)] * 3
+    outs += [shape((block, width), f32), shape((block, width), low)]
+    outs += [shape((lot, wide // 3), f32)] * 3
+    outs.append(shape(proj.shape, f32))
+    if with_shared:
+        outs += [shape((columns, ranks * own), f32)] * 2
+        outs.append(shape((ranks * own, columns), f32))
+    results = pl.pallas_call(
+        functools.partial(widen_kernel, ranks, experts, with_shared),
+        out_shape=tuple(outs),
+        in_specs=[hbm] * 8,
+        out_specs=(hbm,) * len(outs),
+        scratch_shapes=[
+            pltpu.VMEM((3, experts, units, width), low),
+            pltpu.VMEM((3, experts, units, width), f32),
+            pltpu.VMEM((block, width), low),
+            pltpu.VMEM((block, width), f32),
+            pltpu.VMEM((block, width), low),
+            pltpu.VMEM((lot, wide), f32),
+            pltpu.VMEM(proj.shape, f32),
+            pltpu.VMEM(shared.shape, low),
+            pltpu.VMEM((3, ranks * own, columns), f32),
+            pltpu.VMEM((2, columns, ranks * own), f32),
+            dma((3 * experts + 5,)),
+            dma((3 * experts + 9,)),
+        ],
+        compiler_params=pltpu.CompilerParams(vmem_limit_bytes=60 << 20),
+        name="widen",
+    )(gate, up, down, grad_input, output, qkv, proj, shared)
+    if with_shared:
+        return results
+    shared = shared.astype(f32)
+    whole = [shared[:, which].reshape(ranks * own, columns) for which in range(3)]
+    return (*results, whole[0].T, whole[1].T, whole[2])
+
+
 def rope_tables():
     half_dim = HEAD_DIM // 2
     exponent = np.arange(half_dim, dtype=np.float32) * np.float32(2.0 / HEAD_DIM)
@@ -1876,21 +2048,16 @@
     expert_count = local_experts * ranks
     block = width // ranks
     head_width = w_query.shape[1]
-    shared_width = shared_gate.shape[1]
-    shared_own = shared_width // ranks
-    small_pad = 128
+    shared_own = shared_gate.shape[1] // ranks
     layout = Layout(local_experts, expert_hidden, shared_own, expert_count)
-    lane0 = layout.router_lane
 
     small_rows = -(-(expert_count + 3) // 16) * 16
-    spots = jnp.arange(small_pad, dtype=jnp.int32)[None, None, :] - lane0
-    chosen = jnp.sum((routes[:, :, None] == spots).astype(jnp.float32), axis=1).astype(low)
-    fold = token_count // block
-    chosen = chosen.reshape(fold, block, small_pad).transpose(1, 0, 2).reshape(block, fold * small_pad)
-    vectors = jnp.stack([shared_switch, gain_attn, gain_ffn])
     cosine, sine = rope_tables()
-    spots = jnp.arange(SEQ, dtype=jnp.int32)
-    allowed = (spots[None, :] <= spots[:, None]) & (segments[0][None, :] == segments[0][:, None])
+    gate_rows, up_rows = shared_gate, shared_up
+    if shared_own % 16:
+        gate_rows, up_rows = [
+            part.T.reshape(ranks, shared_own, block) for part in (shared_gate, shared_up)
+        ]
 
     (
         qkv_full,
@@ -1913,20 +2080,22 @@
         w_query,
         w_key,
         w_value,
-        chosen,
         w_out,
         w_router.T,
-        vectors,
+        routes.T,
+        shared_switch,
+        gain_attn,
+        gain_ffn,
         tokens,
         cotangent,
-        allowed.astype(jnp.float32),
+        segments,
         cosine,
         sine,
         expert_gate.swapaxes(1, 2),
         expert_up_weight.swapaxes(1, 2),
         expert_down,
-        shared_gate.T.reshape(ranks, shared_own, block),
-        shared_up.T.reshape(ranks, shared_own, block),
+        gate_rows,
+        up_rows,
         shared_down.reshape(ranks, shared_own, block),
         small_rows,
         ranks,
@@ -1961,25 +2130,37 @@
         peers,
         2,
     )
-    grad_experts = [grads.astype(jnp.float32) for grads in grad_experts]
-    grad_shared = grad_shared.astype(jnp.float32)
+    (
+        grad_gate,
+        grad_up,
+        grad_down,
+        grad_input,
+        output,
+        grad_query,
+        grad_key,
+        grad_value,
+        grad_proj,
+        grad_shared_gate,
+        grad_shared_up,
+        grad_shared_down,
+    ) = widen(*grad_experts, grad_input, output, grad_qkv, grad_proj, grad_shared)
     return (
         output,
-        grad_input.astype(jnp.float32),
-        grad_qkv[:, :head_width],
-        grad_qkv[:, head_width : 2 * head_width],
-        grad_qkv[:, 2 * head_width :],
+        grad_input,
+        grad_query,
+        grad_key,
+        grad_value,
         grad_proj,
         grad_small[expert_count + 1],
         grad_small[expert_count + 2],
         grad_small[:expert_count].T,
-        grad_shared[:, 0].reshape(shared_width, block).T,
-        grad_shared[:, 1].reshape(shared_width, block).T,
-        grad_shared[:, 2].reshape(shared_width, block),
+        grad_shared_gate,
+        grad_shared_up,
+        grad_shared_down,
         grad_small[expert_count],
-        grad_experts[0].swapaxes(1, 2),
-        grad_experts[1].swapaxes(1, 2),
-        grad_experts[2],
+        grad_gate.swapaxes(1, 2),
+        grad_up.swapaxes(1, 2),
+        grad_down,
     )
 
 

time: 379 us -> 361 us (0.953)
  other arithmetic: 16.5 us -> 0 us
  local copies, waits for them, and re-layouts: 18.3 us -> 2.7 us
  Pallas kernels: 343 us -> 357 us
    pallas_call x0 -> x1, Pallas kernels: none -> 14.6 us  [widen(): pl.pallas_call(functools.partial(widen_kernel, ranks, experts, with_share...]
    convert_element_type x3 -> x0, other arithmetic: 8.38 us -> none  [the longest x1 5.27 us: shards(): grad_experts = [grads.astype(jnp.float32) for grads in grad_experts]]
    transpose x1 -> x0, other arithmetic: 5.94 us -> none  [shards(): grad_experts[1].swapaxes(1, 2)]
    another operation x5 -> x0, local copies, waits for them, and re-layouts: 5.05 us -> none  [the longest x3 1.98 us: shards(): vectors = jnp.stack([shared_switch, gain_attn, gain_ffn])]
    transpose x2 -> x0, local copies, waits for them, and re-layouts: 4.48 us -> none  [the longest x1 2.24 us: shards(): shared_gate.T.reshape(ranks, shared_own, block)]
    slice x2 -> x0, local copies, waits for them, and re-layouts: 4.29 us -> none  [the longest x1 2.68 us: shards(): grad_qkv[:, 2 * head_width:]]
where the time goes in v6:
time: 361 us
  Pallas kernels  357 us (99%)
    pallas_call x1, Pallas kernels, layer_forward_back(): pl.pallas_call(functools.partial(layer_kernel, layout, ranks, peers), out...  184 us
    pallas_call x1, Pallas kernels, rear(): pl.pallas_call(functools.partial(rear_kernel, layout, ranks, peers, with_...  159 us
    pallas_call x1, Pallas kernels, widen(): pl.pallas_call(functools.partial(widen_kernel, ranks, experts, with_share...  14.6 us

profile of v6, /device:TPU:0, one launch (start us, length us, event | category | flops | bytes accessed | tf_op | source)
XLA Modules:
  0.0 360.9 jit_solution(9910695618400488476)
XLA Ops:
  0.7 183.8 %layer_forward_back.1 = (bf16[2048,1664]{1,0:T(8,128)(2,1)}, bf16[544,2048]{1,0:T(8,128)(2,1)}, bf16[256,2048]{1,0:T(8,128)(2,1)}, bf16[256,512]{1,0:T(8,128)(2,...) custom-call(bf16[256,512]{1,0:T(8,128)(2,1)} %query_ref.1, ...), custom_call_target="tpu_custom_call" | custom-call | tf_op jit(solution)/shard_map/layer_forward_back/pallas_call | solution.py:893
  184.5 158.9 %rear.1 = (bf16[256,2048]{1,0:T(8,128)(2,1)}, bf16[256,2048]{1,0:T(8,128)(2,1)}, f32[256,1536]{1,0:T(8,128)}, f32[512,256]{1,0:T(8,128)}, f32[32,256]{1,0:T(8,12...) custom-call(bf16[2048,2048]{1,0:T(8,128)(2,1)} %get-tuple-element.52, ...), custom_call_target="tpu_custom_call" | custom-call | tf_op jit(solution)/shard_map/rear/pallas_call | solution.py:1800
  343.4 1.4 fusion
  344.7 1.3 slice_bitcast_fusion
  346.1 14.6 %widen.1 = (f32[2,352,2048]{2,1,0:T(8,128)}, f32[2,352,2048]{2,1,0:T(8,128)}, f32[2,352,2048]{2,1,0:T(8,128)}, f32[256,2048]{1,0:T(8,128)}, bf16[256,2048]{1,0:T...) custom-call(bf16[2,352,2048]{2,1,0:T(8,128)(2,1)} %get-tuple-element, ...), custom_call_target="tpu_custom_call" | custom-call | tf_op jit(solution)/shard_map/widen/pallas_call | solution.py:1978

commit v7 on v6

--- a/solution.py
+++ b/solution.py
@@ -156,6 +156,7 @@
 
 STRIP = 64
 BACK_DUE = (0, 5, 11, 11, 17)
+NORM_DUE = 19
 
 
 def strips(rows, body):
@@ -1492,6 +1493,8 @@
             due = BACK_DUE[3 + number] + number * index
             events.append((due, functools.partial(outs[k].step, number)))
 
+    events.append((NORM_DUE, finish_norm))
+
     def grad_step(step, carry):
         wide, slot = step // blocks, step % 2
         for number in range(3):
@@ -1559,7 +1562,6 @@
         for copy in results(step, 0):
             copy.wait()
 
-    finish_norm()
     small_own[count + 1 : count + 2, :] = jnp.zeros((1, width), jnp.float32)
     small_own[count + 2 : count + 3, :] = gain_grad[...]
     shared = []

time: 361 us -> 361 us (level)
  no operation moved by 1% of the time
where the time goes in v7:
time: 361 us; the launch traced here: 360 us
  Pallas kernels  357 us (99%)
    pallas_call x1, Pallas kernels, layer_forward_back(): pl.pallas_call(functools.partial(layer_kernel, layout, ranks, peers), out...  184 us
    pallas_call x1, Pallas kernels, rear(): pl.pallas_call(functools.partial(rear_kernel, layout, ranks, peers, with_...  158 us
    pallas_call x1, Pallas kernels, widen(): pl.pallas_call(functools.partial(widen_kernel, ranks, experts, with_share...  14.6 us

profile of v7, /device:TPU:0, one launch (start us, length us, event | category | flops | bytes accessed | tf_op | source)
XLA Modules:
  0.0 360.1 jit_solution(1362398865268717632)
XLA Ops:
  0.7 183.8 %layer_forward_back.1 = (bf16[2048,1664]{1,0:T(8,128)(2,1)}, bf16[544,2048]{1,0:T(8,128)(2,1)}, bf16[256,2048]{1,0:T(8,128)(2,1)}, bf16[256,512]{1,0:T(8,128)(2,...) custom-call(bf16[256,512]{1,0:T(8,128)(2,1)} %query_ref.1, ...), custom_call_target="tpu_custom_call" | custom-call | tf_op jit(solution)/shard_map/layer_forward_back/pallas_call | solution.py:894
  184.5 158.1 %rear.1 = (bf16[256,2048]{1,0:T(8,128)(2,1)}, bf16[256,2048]{1,0:T(8,128)(2,1)}, f32[256,1536]{1,0:T(8,128)}, f32[512,256]{1,0:T(8,128)}, f32[32,256]{1,0:T(8,12...) custom-call(bf16[2048,2048]{1,0:T(8,128)(2,1)} %get-tuple-element.52, ...), custom_call_target="tpu_custom_call" | custom-call | tf_op jit(solution)/shard_map/rear/pallas_call | solution.py:1802
  342.6 1.4 fusion
  344.0 1.3 slice_bitcast_fusion
  345.3 14.6 %widen.1 = (f32[2,352,2048]{2,1,0:T(8,128)}, f32[2,352,2048]{2,1,0:T(8,128)}, f32[2,352,2048]{2,1,0:T(8,128)}, f32[256,2048]{1,0:T(8,128)}, bf16[256,2048]{1,0:T...) custom-call(bf16[2,352,2048]{2,1,0:T(8,128)(2,1)} %get-tuple-element, ...), custom_call_target="tpu_custom_call" | custom-call | tf_op jit(solution)/shard_map/widen/pallas_call | solution.py:1980
